TPU v7x, 32 devices: a whole 2x2x4 slice. The times are simulated.
32 devices in a mesh: blk: 16 (over z, y, core), grp: 2 (over x).
Axes of the slice: x: 2, y: 2, z: 4, core: 2. Of those that a mesh axis runs over, the one named last changes fastest.
Arguments:
- points: float32 [4096, 4096], P(('blk', 'grp')), may hold values from -40 to 40
- cand_index: int32 [32, 128], P(('blk', 'grp')), may hold values from 0 to 127, as said below
- cand_count: int32 [32], P(('blk', 'grp')), may hold values from 32 to 128
- neighbor_ids: int32 [4096, 16], P(('blk', 'grp')), may hold values from 0 to 4095
- old_dist: float32 [4096, 16], P(('blk', 'grp')), may hold values from 0.3 to 10
Outputs:
- scaled_dist: float32 [4096, 16], P(('blk', 'grp'))
Inputs may be any that keep to these rules, and one draw needn't show every extreme that they name: `cand_index`: within each row, distinct indices of rows of the block.
All inputs are finite; a program needn't handle non-finite values.
Results may differ from a plain program's by a relative error of at most 0.0003.
Values sent between devices are 32-bit elements; how exact they have to be, the bound alone decides.
No kernel may reach another device: no remote copies, remote signals or barrier semaphores. Data moves between devices by JAX's collectives and lax.ppermute only.
A program may use at most 128 MiB of HBM per device.

v0:
```python
import functools

import jax
import jax.numpy as jnp
from jax import lax
from jax.experimental import pallas as pl
from jax.experimental.pallas import tpu as pltpu
from jax.sharding import PartitionSpec as P


AXES = ("blk", "grp")
LANES = 128
SUBLANES = 8
NT = (((1,), (1,)), ((), ()))
FAR = 1e30
NEVER = -3e38


def exchange(tiles, i, j):
    low, high = jnp.minimum(tiles[i], tiles[j]), jnp.maximum(tiles[i], tiles[j])
    tiles[i], tiles[j] = low, high


def sort_tiles(tiles):
    tiles = list(tiles)
    n = len(tiles)
    p = 1
    while p < n:
        k = p
        while k >= 1:
            for j in range(k % p, n - k, 2 * k):
                for i in range(min(k, n - j - k)):
                    if (i + j) // (2 * p) == (i + j + k) // (2 * p):
                        exchange(tiles, i + j, i + j + k)
            k //= 2
        p *= 2
    return tiles


def bitonic(tiles):
    tiles = list(tiles)
    step = len(tiles) // 2
    while step >= 1:
        for i in range(len(tiles)):
            if not i & step:
                exchange(tiles, i, i + step)
        step //= 2
    return tiles


def merge_lowest(a, b, keep):
    if len(a) + len(b) <= keep:
        return bitonic(a + b[::-1])
    return bitonic([jnp.minimum(x, y) for x, y in zip(a, b[::-1])])


def lowest(tiles, keep):
    group = 1
    while group * 2 <= min(keep, len(tiles)):
        group *= 2
    while len(tiles) % group:
        tiles = tiles + [jnp.full((SUBLANES, LANES), FAR, jnp.float32)]
    lists = [sort_tiles(tiles[i : i + group]) for i in range(0, len(tiles), group)]
    while len(lists) > 1:
        paired = [
            merge_lowest(lists[i], lists[i + 1], keep)
            for i in range(0, len(lists) - 1, 2)
        ]
        if len(lists) % 2:
            rest = lists[-1]
            while len(rest) < len(paired[0]):
                rest = rest + [jnp.full((SUBLANES, LANES), FAR, jnp.float32)]
            paired.append(rest)
        lists = paired
    found = lists[0]
    shift = SUBLANES // 2
    while shift:
        found = merge_lowest(found, [pltpu.roll(t, shift, 0) for t in found], keep)
        shift //= 2
    return found


def tiles_of(array):
    return [array[i : i + SUBLANES] for i in range(0, array.shape[0], SUBLANES)]


def describe_kernel(count_ref, index_ref, lists_ref, meta_ref):
    listed, pts = lists_ref.shape
    slots = index_ref.shape[1]
    meta_ref[0:listed] = lists_ref[...]
    spread = jnp.broadcast_to(index_ref[...].astype(jnp.float32), (pts, slots)).T
    slot = lax.broadcasted_iota(jnp.int32, (slots, pts), 0)
    row = lax.broadcasted_iota(jnp.int32, (slots, pts), 1)
    hit = (spread.astype(jnp.int32) == row) & (slot < count_ref[0])
    live = jnp.max(jnp.where(hit, 1.0, 0.0), axis=0, keepdims=True)
    meta_ref[listed : listed + SUBLANES] = jnp.broadcast_to(
        live.astype(jnp.int32), (SUBLANES, pts)
    )


def mask_kernel(listed, base_ref, o, t, o2, t2, u, v, own_ref, far_ref):
    metas = (o, t, o2, t2, u, v)
    pts = o.shape[1]
    alive = [
        jnp.broadcast_to(m[listed : listed + 1].astype(jnp.float32), (pts, pts)).T > 0.5
        for m in metas
    ]
    row = lax.broadcasted_iota(jnp.int32, (pts, pts), 0)
    lane = lax.broadcasted_iota(jnp.int32, (pts, pts), 1)

    def floor(target, cand):
        ids = row + base_ref[cand] * pts
        lists = metas[target]
        bad = jnp.logical_not(alive[cand])
        for k in range(listed):
            bad = bad | (ids == lists[k : k + 1])
        if target == cand:
            bad = bad | (row == lane)
        return jnp.where(bad, FAR, NEVER)

    for i in range(6):
        own_ref[i * pts : (i + 1) * pts] = floor(0, i)
    for i, (target, cand) in enumerate(((2, 4), (2, 5), (4, 0), (4, 2))):
        far_ref[i * pts : (i + 1) * pts] = floor(target, cand)


def split(x):
    high = x.astype(jnp.bfloat16)
    return high, (x - high.astype(jnp.float32)).astype(jnp.bfloat16)


def squared(x):
    total = x[:, :LANES] * x[:, :LANES]
    for j in range(LANES, x.shape[1], LANES):
        total = total + x[:, j : j + LANES] * x[:, j : j + LANES]
    return total


def product(rows, columns):
    def dot(a, b):
        return lax.dot_general(a, b, NT, preferred_element_type=jnp.float32)

    return (
        dot(rows[0], columns[1]) + dot(rows[1], columns[0]) + dot(rows[0], columns[0])
    )


def early_kernel(o, t, o2, u, hi_ref, lo_ref, near_ref, far_ref, squares_ref):
    pts = o.shape[0]
    for i, ref in enumerate((o, t, o2, u)):
        at = slice(i * pts, (i + 1) * pts)
        hi_ref[at], lo_ref[at] = split(ref[...])
        squares_ref[at] = squared(ref[...])

    def part(first, last):
        at = slice(first * pts, last * pts)
        return hi_ref[at], lo_ref[at]

    near_ref[...] = product(part(0, 4), part(0, 2))
    far_ref[...] = product(part(3, 4), part(2, 3))


def late_kernel(t2, v, hi, lo, near, far, squares, mine_ref, sib_ref):
    pts = t2.shape[0]

    def part(first, last):
        at = slice(first * pts, last * pts)
        return hi[at], lo[at]

    crossed, beyond = split(t2[...]), split(v[...])
    both = tuple(jnp.concatenate(pair, axis=0) for pair in zip(crossed, beyond))
    here = product(both, part(0, 2))
    over = product(beyond, part(2, 3)), product(both, crossed)
    ahead = product(part(3, 4), crossed)
    sums = [squares[i * pts : (i + 1) * pts] for i in range(4)]
    sums = sums[:3] + [squared(t2[...]), sums[3], squared(v[...])]
    down = [jnp.sum(x, axis=1, keepdims=True) for x in sums]
    across = [jnp.sum(x.T, axis=0, keepdims=True) for x in sums[:4]]

    def near_block(cand, target):
        lanes = slice(target * pts, (target + 1) * pts)
        if cand in (3, 5):
            at = 0 if cand == 3 else pts
            return here[at : at + pts, lanes]
        at = (0, 1, 2, None, 3)[cand] * pts
        return near[at : at + pts, lanes]

    far_block = {
        (4, 2): far[...],
        (5, 2): over[0],
        (5, 3): over[1][pts : 2 * pts],
        (4, 3): ahead,
    }

    def put(ref, at, block, cand, target):
        ref[at * pts : (at + 1) * pts] = down[cand] + across[target] - 2.0 * block

    for i in range(6):
        put(mine_ref, i, near_block(i, 0), i, 0)
        put(sib_ref, i, near_block(i ^ 1, 1), i ^ 1, 1)
    for i in range(2):
        put(mine_ref, 6 + i, far_block[4 + i, 2], 4 + i, 2)
        put(sib_ref, 6 + i, far_block[5 - i, 3], 5 - i, 3)


def exchange_kernel(scale, keep, mine, theirs, floors, across_ref, along_ref):
    pts = mine.shape[1]

    def whole(i):
        at = slice(i * pts, (i + 1) * pts)
        return (mine[at] + theirs[at]) * scale

    def store(ref, blocks):
        tiles = []
        for i, block in blocks:
            tiles += tiles_of(jnp.maximum(block, floors[i * pts : (i + 1) * pts]))
        for i, tile in enumerate(lowest(tiles, keep)):
            ref[i : i + 1] = tile[0:1]

    store(across_ref, ((0, whole(6)), (1, whole(7))))
    store(along_ref, ((2, whole(4).T), (3, whole(6).T)))


def own_kernel(scale, keep, mine, theirs, floors, old, found_ref):
    pts = mine.shape[1]
    tiles = []
    for i in range(6):
        at = slice(i * pts, (i + 1) * pts)
        tiles += tiles_of(jnp.maximum((mine[at] + theirs[at]) * scale, floors[at]))
    for i, tile in enumerate(lowest(tiles, keep)):
        found_ref[i : i + 1] = tile[0:1]
    found_ref[keep : 2 * keep] = old[...]


def finish_kernel(keep, found, across, along, best_ref, total_ref):
    tiles = tiles_of(found[...]) + tiles_of(across[...]) + tiles_of(along[...])
    ranked = lowest(tiles, keep)
    total_ref[...] = jnp.broadcast_to(
        jnp.sum(ranked[keep - 1], axis=1, keepdims=True), total_ref.shape
    )
    for i, tile in enumerate(ranked):
        best_ref[i : i + 1] = tile[0:1]


def body(points, cand_index, cand_count, neighbor_ids, old_dist):
    pts, width = points.shape
    keep = old_dist.shape[1]
    cycle = lax.axis_size("blk")
    members = lax.axis_size("grp")
    half = width // 2
    blk = lax.axis_index("blk")
    grp = lax.axis_index("grp")
    core = blk % 2
    f32 = jnp.float32

    def links(move):
        return [
            (b * members + g, (move(b, g)[0] % cycle) * members + move(b, g)[1])
            for b in range(cycle)
            for g in range(members)
        ]

    sibling = links(lambda b, g: (b ^ 1, g))
    over_same = links(lambda b, g: (b, 1 - g))
    over_cross = links(lambda b, g: (b ^ 1, 1 - g))
    along_same = links(lambda b, g: (b + (2 if b % 2 else -2), g))
    along_cross = links(lambda b, g: (b + (1 if b % 2 else -1), g))
    along_back = [(b, a) for a, b in along_same]

    def send(array, pairs):
        return lax.ppermute(array, AXES, pairs)

    whole_array = pl.BlockSpec(memory_space=pltpu.VMEM)
    scalars = pl.BlockSpec(memory_space=pltpu.SMEM)

    def call(kernel, out_shape, args, flops=0, first=whole_array, limit=4):
        return pl.pallas_call(
            kernel,
            out_shape=out_shape,
            in_specs=[first] + [whole_array] * (len(args) - 1),
            out_specs=jax.tree.map(lambda _: whole_array, out_shape),
            cost_estimate=pl.CostEstimate(
                flops=flops, bytes_accessed=0, transcendentals=0
            ),
            compiler_params=pltpu.CompilerParams(vmem_limit_bytes=limit << 20),
        )(*args)

    def array(rows, lanes=pts, dtype=f32):
        return jax.ShapeDtypeStruct((rows, lanes), dtype)

    meta = call(
        describe_kernel,
        array(keep + SUBLANES, dtype=jnp.int32),
        (cand_count, cand_index, neighbor_ids.T),
        first=scalars,
    )
    o = lax.dynamic_slice(points, (0, core * half), (pts, half))
    later, described = lax.optimization_barrier((points, meta))
    other = lax.dynamic_slice(later, (0, (1 - core) * half), (pts, half))

    o2 = send(o, over_same)
    u = send(o, along_same)
    metas = (
        meta,
        send(described, sibling),
        send(described, over_same),
        send(described, over_cross),
        send(described, along_same),
        send(described, along_cross),
    )
    t2 = send(other, over_cross)
    v = send(other, along_cross)
    t = send(other, sibling)

    ahead = jnp.where(core == 0, 2, -2)
    beside = jnp.where(core == 0, -1, 1)
    steps = (0, 1 - 2 * core, 0, 1 - 2 * core, ahead, beside)
    sides = (grp, grp, 1 - grp, 1 - grp, grp, grp)
    bases = jnp.stack(
        [
            ((blk + step + cycle) % cycle) * members + side
            for step, side in zip(steps, sides)
        ]
    ).astype(jnp.int32)
    own_floor, far_floor = call(
        functools.partial(mask_kernel, keep),
        (array(6 * pts), array(4 * pts)),
        (bases,) + metas,
        flops=1 << 29,
        first=scalars,
    )

    block_flops = 6 * pts * pts * half
    hi, lo, near, far, squares = call(
        early_kernel,
        (
            array(4 * pts, half, jnp.bfloat16),
            array(4 * pts, half, jnp.bfloat16),
            array(4 * pts, 2 * pts),
            array(pts),
            array(4 * pts, LANES),
        ),
        (o, t, o2, u),
        flops=9 * block_flops,
        limit=24,
    )
    t2, v, own_floor, far_floor = lax.optimization_barrier(
        (t2, v, own_floor, far_floor)
    )
    mine, for_sibling = call(
        late_kernel,
        (array(8 * pts),) * 2,
        (t2, v, hi, lo, near, far, squares),
        flops=7 * block_flops,
        limit=24,
    )
    theirs = send(for_sibling, sibling)

    scale = 1.0 / width
    across, along = call(
        functools.partial(exchange_kernel, scale, keep),
        (array(keep),) * 2,
        (mine, theirs, far_floor),
        flops=1 << 28,
    )
    across = send(across, over_same)
    along = send(along, along_back)
    found = call(
        functools.partial(own_kernel, scale, keep),
        array(2 * keep),
        (mine, theirs, own_floor, old_dist.T),
        flops=1 << 29,
    )
    best, total = call(
        functools.partial(finish_kernel, keep),
        (array(keep), array(SUBLANES, LANES)),
        (found, across, along),
        flops=1 << 26,
    )

    devices = cycle * members
    copies = jnp.broadcast_to(total[:1].reshape(1, 1, LANES), (devices, 1, LANES))
    totals = lax.all_to_all(copies, AXES, 0, 0)
    mean_last = jnp.sum(totals[:, 0, 0]) / (pts * devices)
    return (best / mean_last).T


def solution(mesh):
    return jax.shard_map(
        body,
        mesh=mesh,
        in_specs=(
            P(AXES, None),
            P(AXES, None),
            P(AXES),
            P(AXES, None),
            P(AXES, None),
        ),
        out_specs=P(AXES, None),
        check_vma=False,
    )
```

profile of v0, /device:TPU:0, one launch (start us, length us, event | category | flops | bytes accessed | tf_op | source)
XLA Modules:
  0.0 91.6 jit_solution(17623539796595092650)
XLA Ops:
  0.8 0.7 copy-done.1
  1.5 0.7 copy-done.2
  2.2 0.1 shard_map.55.o
  2.3 0.6 collective-permute-start.2
  2.8 2.6 %collective-permute-start.3 = (s32[24,128]{1,0:T(8,128)S(1)}, s32[24,128]{1,0:T(8,128)S(1)}, u32[]{:S(2)}, u32[]{:S(2)}) collective-permute-start(s32[24,128]{1,0:T(8,128)S(1)} %shard_map.55.o), channel_id=1, source_target_pairs={{0,1},{1,0},{2,3},{3,2},{4,5},{5,4},{6,7},{7,6},{8,9},{9,8},{10,11... | collective-permute-start | bytes 36872 | tf_op jit(solution)/shard_map/ppermute | solution.py:271
  5.4 0.0 collective-permute-start.4
  5.4 4.8 %collective-permute-start.5 = (s32[24,128]{1,0:T(8,128)S(1)}, s32[24,128]{1,0:T(8,128)S(1)}, u32[]{:S(2)}, u32[]{:S(2)}) collective-permute-start(s32[24,128]{1,0:T(8,128)S(1)} %shard_map.55.o), channel_id=1, source_target_pairs={{0,28},{1,29},{2,6},{3,7},{4,0},{5,1},{6,10},{7,11},{8,4},{9,5},{1... | collective-permute-start | bytes 36872 | tf_op jit(solution)/shard_map/ppermute | solution.py:271
  10.2 0.0 collective-permute-start.6
  10.2 1.1 %constant_dynamic-slice_fusion.1 = f32[128,2048]{1,0:T(8,128)} fusion(f32[128,4096]{1,0:T(8,128)S(1)} %copy-done, s32[]{:T(128)S(6)} %select_n.41), kind=kLoop, calls=%fused_computation.4 | loop fusion | bytes 2097156 | tf_op jit(solution)/shard_map/dynamic_slice | solution.py:299
  11.3 4.5 %collective-permute-start.1 = (f32[128,2048]{1,0:T(8,128)}, f32[128,2048]{1,0:T(8,128)}, u32[]{:S(2)}, u32[]{:S(2)}) collective-permute-start(f32[128,2048]{1,0:T(8,128)} %constant_dynamic-slice_fusion.1), channel_id=1, source_target_pairs={{0,30},{1,31},{2,4},{3,5},{4,2},{5,3},{6,8},{7,9},{8,6},{9,7},{10,... | collective-permute-start | bytes 3145736 | tf_op jit(solution)/shard_map/ppermute | solution.py:271
  15.8 1.0 %constant_dynamic-slice_fusion.o = f32[128,2048]{1,0:T(8,128)} fusion(f32[128,4096]{1,0:T(8,128)S(1)} %copy-done, s32[]{:T(128)S(6)} %select_n.48), kind=kLoop, calls=%fused_computation.3 | loop fusion | bytes 2097156 | tf_op jit(solution)/shard_map/dynamic_slice | solution.py:297
  16.9 1.5 %collective-permute-start.8 = (f32[128,2048]{1,0:T(8,128)}, f32[128,2048]{1,0:T(8,128)}, u32[]{:S(2)}, u32[]{:S(2)}) collective-permute-start(f32[128,2048]{1,0:T(8,128)} %constant_dynamic-slice_fusion.o), channel_id=1, source_target_pairs={{0,1},{1,0},{2,3},{3,2},{4,5},{5,4},{6,7},{7,6},{8,9},{9,8},{10,11... | collective-permute-start | bytes 3145736 | tf_op jit(solution)/shard_map/ppermute | solution.py:271
  18.4 0.5 collective-permute-start.9
  18.8 0.1 stack.27.base_ref
  18.9 2.0 %shard_map.56 = (f32[768,128]{1,0:T(8,128)S(1)}, f32[512,128]{1,0:T(8,128)S(1)}) custom-call(s32[6]{0:T(128)S(1)} %stack.27.base_ref, s32[24,128]{1,0:T(8,128)S(1)} %shard_map.55.o, s32[24,128]{1,0:T(8,128)S(1)} %collective-permute-done.2.t, s32[24,128]{1,0:T(8,128)S(1)} %collective-permute-done.3.o2, s32[24,128]{1,0:T(8,128)S(1)} %collective-permute-done.4.t2, ...), custom_call_target="tpu_custom_call" | custom-call | flops 536870912 | tf_op jit(solution)/shard_map/pallas_call | solution.py:277
  20.9 16.0 %collective-permute-done.t2 = f32[128,2048]{1,0:T(8,128)S(1)} collective-permute-done((f32[128,2048]{1,0:T(8,128)}, f32[128,2048]{1,0:T(8,128)S(1)}, u32[]{:S(2)}, u32[]{:S(2)}) %collective-permute-start) | collective-permute-done | bytes 1048608 | tf_op jit(solution)/shard_map/ppermute | solution.py:271
  36.9 22.6 %collective-permute-done.8.o2 = f32[128,2048]{1,0:T(8,128)} collective-permute-done((f32[128,2048]{1,0:T(8,128)}, f32[128,2048]{1,0:T(8,128)}, u32[]{:S(2)}, u32[]{:S(2)}) %collective-permute-start.8) | collective-permute-done | bytes 1048608 | tf_op jit(solution)/shard_map/ppermute | solution.py:271
  59.5 1.8 %collective-permute-done.9.u = f32[128,2048]{1,0:T(8,128)} collective-permute-done((f32[128,2048]{1,0:T(8,128)}, f32[128,2048]{1,0:T(8,128)}, u32[]{:S(2)}, u32[]{:S(2)}) %collective-permute-start.9) | collective-permute-done | bytes 1048608 | tf_op jit(solution)/shard_map/ppermute | solution.py:271
  61.3 4.7 %shard_map.57 = (bf16[512,2048]{1,0:T(8,128)(2,1)S(1)}, bf16[512,2048]{1,0:T(8,128)(2,1)S(1)}, f32[512,256]{1,0:T(8,128)S(1)}, f32[128,128]{1,0:T(8,128)S(1)}, f32[512,128]{1,0:T(8,128)S(1)}) custom-call(f32[128,2048]{1,0:T(8,128)} %constant_dynamic-slice_fusion.o, f32[128,2048]{1,0:T(8,128)} %collective-permute-done.7.t, ...), custom_call_target="tpu_custom_call" | custom-call | flops 1811939328 | tf_op jit(solution)/shard_map/pallas_call | solution.py:277
  66.0 0.0 copy-start.3
  66.0 3.9 %shard_map.58 = (f32[1024,128]{1,0:T(8,128)S(1)}, f32[1024,128]{1,0:T(8,128)S(1)}) custom-call(f32[128,2048]{1,0:T(8,128)S(1)} %collective-permute-done.t2, f32[128,2048]{1,0:T(8,128)} %collective-permute-done.1.v, bf16[512,2048]{1,0:T(8,128)(2,1)S(1)} %get-tuple-element.30.hi, bf16[512,2048]{1,0:T(8,128)(2,1)S(1)} %get-tuple-element.31.lo, ...), custom_call_target="tpu_custom_call" | custom-call | flops 1409286144 | tf_op jit(solution)/shard_map/pallas_call | solution.py:277
  69.9 0.1 collective-permute-start.10
  70.0 1.9 %collective-permute-done.10.theirs = f32[1024,128]{1,0:T(8,128)S(1)} collective-permute-done((f32[1024,128]{1,0:T(8,128)S(1)}, f32[1024,128]{1,0:T(8,128)S(1)}, u32[]{:S(2)}, u32[]{:S(2)}) %collective-permute-start.10) | collective-permute-done | bytes 524320 | tf_op jit(solution)/shard_map/ppermute | solution.py:271
  71.9 0.3 shard_map.60
  72.2 0.7 collective-permute-start.11
  72.9 0.2 shard_map.59.found
  73.2 2.7 %collective-permute-done.11.across = f32[16,128]{1,0:T(8,128)S(1)} collective-permute-done((f32[16,128]{1,0:T(8,128)S(1)}, f32[16,128]{1,0:T(8,128)S(1)}, u32[]{:S(2)}, u32[]{:S(2)}) %collective-permute-start.11) | collective-permute-done | bytes 8224 | tf_op jit(solution)/shard_map/ppermute | solution.py:271
  75.9 3.4 %collective-permute-done.12.along = f32[16,128]{1,0:T(8,128)S(1)} collective-permute-done((f32[16,128]{1,0:T(8,128)S(1)}, f32[16,128]{1,0:T(8,128)S(1)}, u32[]{:S(2)}, u32[]{:S(2)}) %collective-permute-start.12) | collective-permute-done | bytes 8224 | tf_op jit(solution)/shard_map/ppermute | solution.py:271
  79.3 0.1 shard_map.61
  79.4 10.3 %all_to_all.5 = f32[32,1,128]{2,1,0:T(1,128)S(1)} all-to-all(f32[32,1,128]{2,1,0:T(1,128)S(1)} %broadcast_in_dim.8), channel_id=1, replica_groups=mesh['blk'=16,'grp'=2] {'blk','grp'}, dimensions={0} | all-to-all | bytes 32768 | tf_op jit(solution)/shard_map/all_to_all | solution.py:383
  89.7 0.6 slice_reduce_fusion
  91.0 0.6 divide_bitcast_fusion
  (17 shorter events, 0.1 us)
Async XLA Ops:
  0.0 10.2 %copy-start = (f32[128,4096]{1,0:T(8,128)S(1)}, f32[128,4096]{1,0:T(8,128)}, u32[]{:S(2)}) copy-start(f32[128,4096]{1,0:T(8,128)} %param.5) | copy-start | bytes 6291460
  0.8 0.7 copy-start.1
  1.5 0.7 copy-start.2
  2.3 9.0 %collective-permute-start.2 = (s32[24,128]{1,0:T(8,128)S(1)}, s32[24,128]{1,0:T(8,128)S(1)}, u32[]{:S(2)}, u32[]{:S(2)}) collective-permute-start(s32[24,128]{1,0:T(8,128)S(1)} %shard_map.55.o), channel_id=1, source_target_pairs={{0,2},{1,3},{2,0},{3,1},{4,6},{5,7},{6,4},{7,5},{8,10},{9,11},{10,... | collective-permute-start | bytes 36872 | tf_op jit(solution)/shard_map/ppermute | solution.py:271
  2.8 8.5 %collective-permute-start.3 = (s32[24,128]{1,0:T(8,128)S(1)}, s32[24,128]{1,0:T(8,128)S(1)}, u32[]{:S(2)}, u32[]{:S(2)}) collective-permute-start(s32[24,128]{1,0:T(8,128)S(1)} %shard_map.55.o), channel_id=1, source_target_pairs={{0,1},{1,0},{2,3},{3,2},{4,5},{5,4},{6,7},{7,6},{8,9},{9,8},{10,11... | collective-permute-start | bytes 36872 | tf_op jit(solution)/shard_map/ppermute | solution.py:271
  5.4 11.5 %collective-permute-start.4 = (s32[24,128]{1,0:T(8,128)S(1)}, s32[24,128]{1,0:T(8,128)S(1)}, u32[]{:S(2)}, u32[]{:S(2)}) collective-permute-start(s32[24,128]{1,0:T(8,128)S(1)} %shard_map.55.o), channel_id=1, source_target_pairs={{0,3},{1,2},{2,1},{3,0},{4,7},{5,6},{6,5},{7,4},{8,11},{9,10},{10,... | collective-permute-start | bytes 36872 | tf_op jit(solution)/shard_map/ppermute | solution.py:271
  5.4 12.9 %collective-permute-start.5 = (s32[24,128]{1,0:T(8,128)S(1)}, s32[24,128]{1,0:T(8,128)S(1)}, u32[]{:S(2)}, u32[]{:S(2)}) collective-permute-start(s32[24,128]{1,0:T(8,128)S(1)} %shard_map.55.o), channel_id=1, source_target_pairs={{0,28},{1,29},{2,6},{3,7},{4,0},{5,1},{6,10},{7,11},{8,4},{9,5},{1... | collective-permute-start | bytes 36872 | tf_op jit(solution)/shard_map/ppermute | solution.py:271
  10.2 8.6 %collective-permute-start.6 = (s32[24,128]{1,0:T(8,128)S(1)}, s32[24,128]{1,0:T(8,128)S(1)}, u32[]{:S(2)}, u32[]{:S(2)}) collective-permute-start(s32[24,128]{1,0:T(8,128)S(1)} %shard_map.55.o), channel_id=1, source_target_pairs={{0,30},{1,31},{2,4},{3,5},{4,2},{5,3},{6,8},{7,9},{8,6},{9,7},{10,... | collective-permute-start | bytes 36872 | tf_op jit(solution)/shard_map/ppermute | solution.py:271
  11.3 25.6 %collective-permute-start = (f32[128,2048]{1,0:T(8,128)}, f32[128,2048]{1,0:T(8,128)S(1)}, u32[]{:S(2)}, u32[]{:S(2)}) collective-permute-start(f32[128,2048]{1,0:T(8,128)} %constant_dynamic-slice_fusion.1), channel_id=1, source_target_pairs={{0,3},{1,2},{2,1},{3,0},{4,7},{5,6},{6,5},{7,4},{8,11},{9,10},{10,... | collective-permute-start | bytes 3145736 | tf_op jit(solution)/shard_map/ppermute | solution.py:271
  11.3 25.6 %collective-permute-start.1 = (f32[128,2048]{1,0:T(8,128)}, f32[128,2048]{1,0:T(8,128)}, u32[]{:S(2)}, u32[]{:S(2)}) collective-permute-start(f32[128,2048]{1,0:T(8,128)} %constant_dynamic-slice_fusion.1), channel_id=1, source_target_pairs={{0,30},{1,31},{2,4},{3,5},{4,2},{5,3},{6,8},{7,9},{8,6},{9,7},{10,... | collective-permute-start | bytes 3145736 | tf_op jit(solution)/shard_map/ppermute | solution.py:271
  16.9 42.7 %collective-permute-start.8 = (f32[128,2048]{1,0:T(8,128)}, f32[128,2048]{1,0:T(8,128)}, u32[]{:S(2)}, u32[]{:S(2)}) collective-permute-start(f32[128,2048]{1,0:T(8,128)} %constant_dynamic-slice_fusion.o), channel_id=1, source_target_pairs={{0,1},{1,0},{2,3},{3,2},{4,5},{5,4},{6,7},{7,6},{8,9},{9,8},{10,11... | collective-permute-start | bytes 3145736 | tf_op jit(solution)/shard_map/ppermute | solution.py:271
  18.4 43.0 %collective-permute-start.9 = (f32[128,2048]{1,0:T(8,128)}, f32[128,2048]{1,0:T(8,128)}, u32[]{:S(2)}, u32[]{:S(2)}) collective-permute-start(f32[128,2048]{1,0:T(8,128)} %constant_dynamic-slice_fusion.o), channel_id=1, source_target_pairs={{0,28},{1,29},{2,6},{3,7},{4,0},{5,1},{6,10},{7,11},{8,4},{9,5},{1... | collective-permute-start | bytes 3145736 | tf_op jit(solution)/shard_map/ppermute | solution.py:271
  18.8 42.5 %collective-permute-start.7 = (f32[128,2048]{1,0:T(8,128)}, f32[128,2048]{1,0:T(8,128)}, u32[]{:S(2)}, u32[]{:S(2)}) collective-permute-start(f32[128,2048]{1,0:T(8,128)} %constant_dynamic-slice_fusion.1), channel_id=1, source_target_pairs={{0,2},{1,3},{2,0},{3,1},{4,6},{5,7},{6,4},{7,5},{8,10},{9,11},{10,... | collective-permute-start | bytes 3145736 | tf_op jit(solution)/shard_map/ppermute | solution.py:271
  66.0 6.9 %copy-start.3 = (f32[128,16]{0,1:T(8,128)S(1)}, f32[128,16]{0,1:T(8,128)}, u32[]{:S(2)}) copy-start(f32[128,16]{0,1:T(8,128)} %param.9) | copy-start | bytes 24580
  69.9 2.0 %collective-permute-start.10 = (f32[1024,128]{1,0:T(8,128)S(1)}, f32[1024,128]{1,0:T(8,128)S(1)}, u32[]{:S(2)}, u32[]{:S(2)}) collective-permute-start(f32[1024,128]{1,0:T(8,128)S(1)} %get-tuple-element.36), channel_id=1, source_target_pairs={{0,2},{1,3},{2,0},{3,1},{4,6},{5,7},{6,4},{7,5},{8,10},{9,11},{10,... | collective-permute-start | bytes 1572872 | tf_op jit(solution)/shard_map/ppermute | solution.py:271
  72.2 3.7 %collective-permute-start.11 = (f32[16,128]{1,0:T(8,128)S(1)}, f32[16,128]{1,0:T(8,128)S(1)}, u32[]{:S(2)}, u32[]{:S(2)}) collective-permute-start(f32[16,128]{1,0:T(8,128)S(1)} %get-tuple-element.39), channel_id=1, source_target_pairs={{0,1},{1,0},{2,3},{3,2},{4,5},{5,4},{6,7},{7,6},{8,9},{9,8},{10,11... | collective-permute-start | bytes 24584 | tf_op jit(solution)/shard_map/ppermute | solution.py:271
  72.9 6.3 %collective-permute-start.12 = (f32[16,128]{1,0:T(8,128)S(1)}, f32[16,128]{1,0:T(8,128)S(1)}, u32[]{:S(2)}, u32[]{:S(2)}) collective-permute-start(f32[16,128]{1,0:T(8,128)S(1)} %get-tuple-element.40), channel_id=1, source_target_pairs={{28,0},{29,1},{6,2},{7,3},{0,4},{1,5},{10,6},{11,7},{4,8},{5,9},{1... | collective-permute-start | bytes 24584 | tf_op jit(solution)/shard_map/ppermute | solution.py:271
where the time goes:
time: 91.9 us; the launch traced here: 91.6 us
  waiting for transfers between devices  48.4 us (53%)
  starting transfers between devices  15.2 us (17%)
  Pallas kernels  11.3 us (12%)
  blocking collectives  10.3 us (11%)
  local copies, waits for them, and re-layouts  3.55 us (4%)
  between operations  1.54 us (2%)
  other arithmetic  1.24 us (1%)
    ppermute x13, waiting for transfers between devices, send(): return lax.ppermute(array, AXES, pairs)  48.4 us
    ppermute x13, starting transfers between devices, send(): return lax.ppermute(array, AXES, pairs)  15.2 us
    pallas_call x7, Pallas kernels, call(): pl.pallas_call(kernel, out_shape=out_shape, in_specs=[first] + [whole_arr...  11.3 us
    all_to_all x1, blocking collectives, body(): totals = lax.all_to_all(copies, AXES, 0, 0)  10.3 us
  transfers between devices with their start and end apart: 13, of which 6 were waited for; matrix products, arithmetic and copies ran while one was open for 2% of the time, Pallas kernels for 2%

commit v1 on v0

--- a/solution.py
+++ b/solution.py
@@ -160,37 +160,62 @@
     far_ref[...] = product(part(3, 4), part(2, 3))
 
 
-def late_kernel(t2, v, hi, lo, near, far, squares, mine_ref, sib_ref):
-    pts = t2.shape[0]
+def middle_kernel(t2, v, hi, lo, here_ref, over_ref, squares_ref):
+    pts, width = t2.shape
 
     def part(first, last):
         at = slice(first * pts, last * pts)
-        return hi[at], lo[at]
-
-    crossed, beyond = split(t2[...]), split(v[...])
+        return hi[at, :width], lo[at, :width]
+
+    blocks = split(t2[...]), split(v[...])
+    late_products(blocks, part, pts, here_ref, over_ref)
+    squares_ref[0:pts] = squared(t2[...])
+    squares_ref[pts : 2 * pts] = squared(v[...])
+
+
+def late_products(blocks, part, pts, here_ref, over_ref):
+    crossed, beyond = blocks
     both = tuple(jnp.concatenate(pair, axis=0) for pair in zip(crossed, beyond))
-    here = product(both, part(0, 2))
-    over = product(beyond, part(2, 3)), product(both, crossed)
-    ahead = product(part(3, 4), crossed)
+    here_ref[...] = product(both, part(0, 2))
+    over_ref[0:pts] = product(beyond, part(2, 3))
+    over_ref[pts : 2 * pts] = product(beyond, crossed)
+    over_ref[2 * pts : 3 * pts] = product(part(3, 4), crossed)
+
+
+def late_kernel(
+    t2, v, hi, lo, near, far, squares, here, over, more, mine_ref, sib_ref, rest, last
+):
+    pts, width = t2.shape
+    start = hi.shape[1] - width
+
+    def part(first, last):
+        at = slice(first * pts, last * pts)
+        return hi[at, start:], lo[at, start:]
+
+    late_products((split(t2[...]), split(v[...])), part, pts, rest, last)
     sums = [squares[i * pts : (i + 1) * pts] for i in range(4)]
-    sums = sums[:3] + [squared(t2[...]), sums[3], squared(v[...])]
+    sums = sums[:3] + [
+        more[0:pts] + squared(t2[...]),
+        sums[3],
+        more[pts : 2 * pts] + squared(v[...]),
+    ]
     down = [jnp.sum(x, axis=1, keepdims=True) for x in sums]
     across = [jnp.sum(x.T, axis=0, keepdims=True) for x in sums[:4]]
 
     def near_block(cand, target):
         lanes = slice(target * pts, (target + 1) * pts)
         if cand in (3, 5):
-            at = 0 if cand == 3 else pts
-            return here[at : at + pts, lanes]
+            at = slice(0, pts) if cand == 3 else slice(pts, 2 * pts)
+            return here[at, lanes] + rest[at, lanes]
         at = (0, 1, 2, None, 3)[cand] * pts
         return near[at : at + pts, lanes]
 
-    far_block = {
-        (4, 2): far[...],
-        (5, 2): over[0],
-        (5, 3): over[1][pts : 2 * pts],
-        (4, 3): ahead,
-    }
+    def far_block(cand, target):
+        if (cand, target) == (4, 2):
+            return far[...]
+        i = ((5, 2), (5, 3), (4, 3)).index((cand, target))
+        at = slice(i * pts, (i + 1) * pts)
+        return over[at] + last[at]
 
     def put(ref, at, block, cand, target):
         ref[at * pts : (at + 1) * pts] = down[cand] + across[target] - 2.0 * block
@@ -199,8 +224,8 @@
         put(mine_ref, i, near_block(i, 0), i, 0)
         put(sib_ref, i, near_block(i ^ 1, 1), i ^ 1, 1)
     for i in range(2):
-        put(mine_ref, 6 + i, far_block[4 + i, 2], 4 + i, 2)
-        put(sib_ref, 6 + i, far_block[5 - i, 3], 5 - i, 3)
+        put(mine_ref, 6 + i, far_block(4 + i, 2), 4 + i, 2)
+        put(sib_ref, 6 + i, far_block(5 - i, 3), 5 - i, 3)
 
 
 def exchange_kernel(scale, keep, mine, theirs, floors, across_ref, along_ref):
@@ -240,6 +265,20 @@
     )
     for i, tile in enumerate(ranked):
         best_ref[i : i + 1] = tile[0:1]
+
+
+def scale_kernel(points_in_all, best, totals, out_ref):
+    total = jnp.sum(totals[:, 0, :], axis=0, keepdims=True)
+    out_ref[...] = best[...] / (total * (1.0 / points_in_all))
+
+
+def cut_kernel(start_ref, points, out_ref, done):
+    start = pl.multiple_of(start_ref[0], LANES)
+    copy = pltpu.make_async_copy(
+        points.at[:, pl.ds(start, out_ref.shape[1])], out_ref, done
+    )
+    copy.start()
+    copy.wait()
 
 
 def body(points, cand_index, cand_count, neighbor_ids, old_dist):
@@ -273,11 +312,22 @@
     whole_array = pl.BlockSpec(memory_space=pltpu.VMEM)
     scalars = pl.BlockSpec(memory_space=pltpu.SMEM)
 
-    def call(kernel, out_shape, args, flops=0, first=whole_array, limit=4):
+    def call(
+        kernel,
+        out_shape,
+        args,
+        flops=0,
+        first=whole_array,
+        second=whole_array,
+        scratch=(),
+        limit=4,
+    ):
+        specs = [first, second] + [whole_array] * len(args)
         return pl.pallas_call(
             kernel,
             out_shape=out_shape,
-            in_specs=[first] + [whole_array] * (len(args) - 1),
+            in_specs=specs[: len(args)],
+            scratch_shapes=scratch,
             out_specs=jax.tree.map(lambda _: whole_array, out_shape),
             cost_estimate=pl.CostEstimate(
                 flops=flops, bytes_accessed=0, transcendentals=0
@@ -294,9 +344,23 @@
         (cand_count, cand_index, neighbor_ids.T),
         first=scalars,
     )
-    o = lax.dynamic_slice(points, (0, core * half), (pts, half))
-    later, described = lax.optimization_barrier((points, meta))
-    other = lax.dynamic_slice(later, (0, (1 - core) * half), (pts, half))
+
+    def cut(source, start):
+        return call(
+            cut_kernel,
+            pltpu.VMEM((pts, half), f32),
+            (
+                start.astype(jnp.int32).reshape(1),
+                pltpu.with_memory_space_constraint(source, pltpu.HBM),
+            ),
+            first=scalars,
+            second=pl.BlockSpec(memory_space=pltpu.HBM),
+            scratch=[pltpu.SemaphoreType.DMA],
+        )
+
+    o = cut(points, core * half)
+    turn, described = lax.optimization_barrier(((1 - core) * half, meta))
+    other = cut(points, turn)
 
     o2 = send(o, over_same)
     u = send(o, along_same)
@@ -308,8 +372,11 @@
         send(described, along_same),
         send(described, along_cross),
     )
-    t2 = send(other, over_cross)
-    v = send(other, along_cross)
+    most = half * 3 // 4
+    t2 = send(other[:, :most], over_cross)
+    v = send(other[:, :most], along_cross)
+    t2_rest = send(other[:, most:], over_cross)
+    v_rest = send(other[:, most:], along_cross)
     t = send(other, sibling)
 
     ahead = jnp.where(core == 0, 2, -2)
@@ -344,14 +411,22 @@
         flops=9 * block_flops,
         limit=24,
     )
-    t2, v, own_floor, far_floor = lax.optimization_barrier(
-        (t2, v, own_floor, far_floor)
+    here, over, more = call(
+        middle_kernel,
+        (array(2 * pts, 2 * pts), array(3 * pts), array(2 * pts, LANES)),
+        (t2, v, hi, lo),
+        flops=6 * block_flops,
+        limit=24,
+    )
+    t2_rest, v_rest, own_floor, far_floor = lax.optimization_barrier(
+        (t2_rest, v_rest, own_floor, far_floor)
     )
     mine, for_sibling = call(
         late_kernel,
         (array(8 * pts),) * 2,
-        (t2, v, hi, lo, near, far, squares),
-        flops=7 * block_flops,
+        (t2_rest, v_rest, hi, lo, near, far, squares, here, over, more),
+        flops=2 * block_flops,
+        scratch=[pltpu.VMEM((2 * pts, 2 * pts), f32), pltpu.VMEM((3 * pts, pts), f32)],
         limit=24,
     )
     theirs = send(for_sibling, sibling)
@@ -381,8 +456,10 @@
     devices = cycle * members
     copies = jnp.broadcast_to(total[:1].reshape(1, 1, LANES), (devices, 1, LANES))
     totals = lax.all_to_all(copies, AXES, 0, 0)
-    mean_last = jnp.sum(totals[:, 0, 0]) / (pts * devices)
-    return (best / mean_last).T
+    scaled = call(
+        functools.partial(scale_kernel, pts * devices), array(keep), (best, totals)
+    )
+    return scaled.T
 
 
 def solution(mesh):

time: 91.9 us -> 92.8 us (level)
  starting transfers between devices: 15.2 us -> 20.6 us
  waiting for transfers between devices: 48.4 us -> 44.5 us
  Pallas kernels: 11.3 us -> 13.9 us
  other arithmetic: 1.24 us -> 0 us
  local copies, waits for them, and re-layouts: 3.55 us -> 2.42 us
    ppermute x13 -> x15, starting transfers between devices: 15.2 us -> 20.6 us  [send(): return lax.ppermute(array, AXES, pairs)]
    ppermute x13 -> x15, waiting for transfers between devices: 48.4 us -> 44.5 us  [send(): return lax.ppermute(array, AXES, pairs)]
    pallas_call x7 -> x11, Pallas kernels: 11.3 us -> 13.9 us  [call(): pl.pallas_call(kernel, out_shape=out_shape, in_specs=specs[:len(args)], s...]
    dynamic_slice x2 -> x0, local copies, waits for them, and re-layouts: 2.1 us -> none  [the longest x1 1.06 us: body(): other = lax.dynamic_slice(later, (0, (1 - core) * half), (pts, half))]
    slice x0 -> x2, local copies, waits for them, and re-layouts: none -> 0.97 us  [the longest x1 0.95 us: body(): t2 = send(other[:, :most], over_cross)]
  transfers between devices with their start and end apart: 13 -> 15, of which waited for: 6 -> 10; matrix products, arithmetic and copies ran while one was open for 2% -> 1% of each run, Pallas kernels for 2% -> 9%
where the time goes in v1:
time: 92.8 us; the launch traced here: 92.4 us
  waiting for transfers between devices  44.5 us (48%)
  starting transfers between devices  20.6 us (22%)
  Pallas kernels  13.9 us (15%)
  blocking collectives  10.3 us (11%)
  local copies, waits for them, and re-layouts  2.42 us (3%)
    ppermute x15, waiting for transfers between devices, send(): return lax.ppermute(array, AXES, pairs)  44.5 us
    ppermute x15, starting transfers between devices, send(): return lax.ppermute(array, AXES, pairs)  20.6 us
    pallas_call x11, Pallas kernels, call(): pl.pallas_call(kernel, out_shape=out_shape, in_specs=specs[:len(args)], s...  13.9 us
    all_to_all x1, blocking collectives, body(): totals = lax.all_to_all(copies, AXES, 0, 0)  10.3 us
  transfers between devices with their start and end apart: 15, of which 10 were waited for; matrix products, arithmetic and copies ran while one was open for 1% of the time, Pallas kernels for 9%

profile of v1, /device:TPU:0, one launch (start us, length us, event | category | flops | bytes accessed | tf_op | source)
XLA Modules:
  0.0 92.4 jit_solution(9548376693859867667)
XLA Ops:
  0.7 0.7 copy-done
  1.4 0.7 copy-done.1
  2.1 1.2 %shard_map.56 = f32[128,2048]{1,0:T(8,128)S(1)} custom-call(s32[1]{0:T(128)} %bitcast.1.start_ref, f32[128,4096]{1,0:T(8,128)} %points.3), custom_call_target="tpu_custom_call" | custom-call | tf_op jit(solution)/shard_map/pallas_call | solution.py:326
  3.4 0.6 collective-permute-start.7
  3.9 1.2 %shard_map.58.o = f32[128,2048]{1,0:T(8,128)S(1)} custom-call(s32[1]{0:T(128)} %bitcast.8.start_ref, f32[128,4096]{1,0:T(8,128)} %points.3), custom_call_target="tpu_custom_call" | custom-call | tf_op jit(solution)/shard_map/pallas_call | solution.py:326
  5.2 2.6 %collective-permute-start.8 = (f32[128,2048]{1,0:T(8,128)S(1)}, f32[128,2048]{1,0:T(8,128)}, u32[]{:S(2)}, u32[]{:S(2)}) collective-permute-start(f32[128,2048]{1,0:T(8,128)S(1)} %shard_map.58.o), channel_id=1, source_target_pairs={{0,1},{1,0},{2,3},{3,2},{4,5},{5,4},{6,7},{7,6},{8,9},{9,8},{10,11... | collective-permute-start | bytes 3145736 | tf_op jit(solution)/shard_map/ppermute | solution.py:310
  7.7 4.6 %collective-permute-start.9 = (f32[128,2048]{1,0:T(8,128)S(1)}, f32[128,2048]{1,0:T(8,128)}, u32[]{:S(2)}, u32[]{:S(2)}) collective-permute-start(f32[128,2048]{1,0:T(8,128)S(1)} %shard_map.58.o), channel_id=1, source_target_pairs={{0,28},{1,29},{2,6},{3,7},{4,0},{5,1},{6,10},{7,11},{8,4},{9,5},{1... | collective-permute-start | bytes 3145736 | tf_op jit(solution)/shard_map/ppermute | solution.py:310
  12.3 0.5 collective-permute-start.3
  12.8 0.6 collective-permute-done.2.t
  13.5 0.7 collective-permute-start.4
  14.2 17.8 %collective-permute-done.3.o2 = s32[24,128]{1,0:T(8,128)S(1)} collective-permute-done((s32[24,128]{1,0:T(8,128)S(1)}, s32[24,128]{1,0:T(8,128)S(1)}, u32[]{:S(2)}, u32[]{:S(2)}) %collective-permute-start.3) | collective-permute-done | bytes 12320 | tf_op jit(solution)/shard_map/ppermute | solution.py:310
  31.9 4.8 %collective-permute-start.5 = (s32[24,128]{1,0:T(8,128)S(1)}, s32[24,128]{1,0:T(8,128)S(1)}, u32[]{:S(2)}, u32[]{:S(2)}) collective-permute-start(s32[24,128]{1,0:T(8,128)S(1)} %shard_map.55.o), channel_id=1, source_target_pairs={{0,28},{1,29},{2,6},{3,7},{4,0},{5,1},{6,10},{7,11},{8,4},{9,5},{1... | collective-permute-start | bytes 36872 | tf_op jit(solution)/shard_map/ppermute | solution.py:310
  36.8 1.4 %collective-permute-done.5.u = s32[24,128]{1,0:T(8,128)S(1)} collective-permute-done((s32[24,128]{1,0:T(8,128)S(1)}, s32[24,128]{1,0:T(8,128)S(1)}, u32[]{:S(2)}, u32[]{:S(2)}) %collective-permute-start.5) | collective-permute-done | bytes 12320 | tf_op jit(solution)/shard_map/ppermute | solution.py:310
  38.2 4.3 %collective-permute-done.6.v = s32[24,128]{1,0:T(8,128)S(1)} collective-permute-done((s32[24,128]{1,0:T(8,128)S(1)}, s32[24,128]{1,0:T(8,128)S(1)}, u32[]{:S(2)}, u32[]{:S(2)}) %collective-permute-start.6) | collective-permute-done | bytes 12320 | tf_op jit(solution)/shard_map/ppermute | solution.py:310
  42.6 1.8 %collective-permute-start.1 = (f32[128,512]{1,0:T(8,128)S(1)}, f32[128,512]{1,0:T(8,128)S(1)}, u32[]{:S(2)}, u32[]{:S(2)}) collective-permute-start(f32[128,512]{1,0:T(8,128)S(1)} %slice.14), channel_id=1, source_target_pairs={{0,30},{1,31},{2,4},{3,5},{4,2},{5,3},{6,8},{7,9},{8,6},{9,7},{10,... | collective-permute-start | bytes 786440 | tf_op jit(solution)/shard_map/ppermute | solution.py:310
  44.3 0.9 %slice.15 = f32[128,1536]{1,0:T(8,128)} slice(f32[128,2048]{1,0:T(8,128)S(1)} %shard_map.56), slice={[0:128], [0:1536]} | slice | bytes 1572864 | tf_op jit(solution)/shard_map/slice | solution.py:376
  45.3 1.4 %collective-permute-done.t2 = f32[128,512]{1,0:T(8,128)S(1)} collective-permute-done((f32[128,512]{1,0:T(8,128)S(1)}, f32[128,512]{1,0:T(8,128)S(1)}, u32[]{:S(2)}, u32[]{:S(2)}) %collective-permute-start) | collective-permute-done | bytes 262176 | tf_op jit(solution)/shard_map/ppermute | solution.py:310
  46.7 4.4 %collective-permute-done.1.v = f32[128,512]{1,0:T(8,128)S(1)} collective-permute-done((f32[128,512]{1,0:T(8,128)S(1)}, f32[128,512]{1,0:T(8,128)S(1)}, u32[]{:S(2)}, u32[]{:S(2)}) %collective-permute-start.1) | collective-permute-done | bytes 262176 | tf_op jit(solution)/shard_map/ppermute | solution.py:310
  51.1 1.8 %collective-permute-start.11 = (f32[128,1536]{1,0:T(8,128)}, f32[128,1536]{1,0:T(8,128)}, u32[]{:S(2)}, u32[]{:S(2)}) collective-permute-start(f32[128,1536]{1,0:T(8,128)} %slice.15), channel_id=1, source_target_pairs={{0,30},{1,31},{2,4},{3,5},{4,2},{5,3},{6,8},{7,9},{8,6},{9,7},{10,... | collective-permute-start | bytes 2359304 | tf_op jit(solution)/shard_map/ppermute | solution.py:310
  52.9 2.0 %shard_map.57 = (f32[768,128]{1,0:T(8,128)S(1)}, f32[512,128]{1,0:T(8,128)S(1)}) custom-call(s32[6]{0:T(128)S(1)} %stack.27.base_ref, s32[24,128]{1,0:T(8,128)S(1)} %shard_map.55.o, s32[24,128]{1,0:T(8,128)S(1)} %collective-permute-done.2.t, s32[24,128]{1,0:T(8,128)S(1)} %collective-permute-done.3.o2, s32[24,128]{1,0:T(8,128)S(1)} %collective-permute-done.4.t2, ...), custom_call_target="tpu_custom_call" | custom-call | flops 536870912 | tf_op jit(solution)/shard_map/pallas_call | solution.py:326
  55.0 4.4 %shard_map.59 = (bf16[512,2048]{1,0:T(8,128)(2,1)S(1)}, bf16[512,2048]{1,0:T(8,128)(2,1)S(1)}, f32[512,256]{1,0:T(8,128)S(1)}, f32[128,128]{1,0:T(8,128)S(1)}, f32[512,128]{1,0:T(8,128)S(1)}) custom-call(f32[128,2048]{1,0:T(8,128)S(1)} %shard_map.58.o, f32[128,2048]{1,0:T(8,128)} %collective-permute-done.7.t, f32[128,2048]{1,0:T(8,128)} %collective-permute-done.8.o2, ...), custom_call_target="tpu_custom_call" | custom-call | flops 1811939328 | tf_op jit(solution)/shard_map/pallas_call | solution.py:326
  59.4 7.1 %collective-permute-done.10.t2 = f32[128,1536]{1,0:T(8,128)S(1)} collective-permute-done((f32[128,1536]{1,0:T(8,128)}, f32[128,1536]{1,0:T(8,128)S(1)}, u32[]{:S(2)}, u32[]{:S(2)}) %collective-permute-start.10) | collective-permute-done | bytes 786464 | tf_op jit(solution)/shard_map/ppermute | solution.py:310
  66.5 2.9 %shard_map.60 = (f32[256,256]{1,0:T(8,128)S(1)}, f32[384,128]{1,0:T(8,128)S(1)}, f32[256,128]{1,0:T(8,128)S(1)}) custom-call(f32[128,1536]{1,0:T(8,128)S(1)} %collective-permute-done.10.t2, f32[128,1536]{1,0:T(8,128)} %collective-permute-done.11.v, bf16[512,2048]{1,0:T(8,128)(2,1)S(1)} %get-tuple-element.33.hi, bf16[512,2048]{1,0:T(8,128)(2,1)S(1)} %get-tuple-element.34.lo), custom_call_target="tpu_custom_call" | custom-call | flops 1207959552 | tf_op jit(solution)/shard_map/pallas_call | solution.py:326
  69.4 0.7 shard_map.61
  70.2 1.4 %collective-permute-start.12 = (f32[1024,128]{1,0:T(8,128)S(1)}, f32[1024,128]{1,0:T(8,128)S(1)}, u32[]{:S(2)}, u32[]{:S(2)}) collective-permute-start(f32[1024,128]{1,0:T(8,128)S(1)} %get-tuple-element.42), channel_id=1, source_target_pairs={{0,2},{1,3},{2,0},{3,1},{4,6},{5,7},{6,4},{7,5},{8,10},{9,11},{10,... | collective-permute-start | bytes 1572872 | tf_op jit(solution)/shard_map/ppermute | solution.py:310
  71.6 1.5 %collective-permute-done.12.theirs = f32[1024,128]{1,0:T(8,128)S(1)} collective-permute-done((f32[1024,128]{1,0:T(8,128)S(1)}, f32[1024,128]{1,0:T(8,128)S(1)}, u32[]{:S(2)}, u32[]{:S(2)}) %collective-permute-start.12) | collective-permute-done | bytes 524320 | tf_op jit(solution)/shard_map/ppermute | solution.py:310
  73.1 0.3 shard_map.63
  73.4 1.7 %collective-permute-start.13 = (f32[16,128]{1,0:T(8,128)S(1)}, f32[16,128]{1,0:T(8,128)S(1)}, u32[]{:S(2)}, u32[]{:S(2)}) collective-permute-start(f32[16,128]{1,0:T(8,128)S(1)} %get-tuple-element.45), channel_id=1, source_target_pairs={{0,1},{1,0},{2,3},{3,2},{4,5},{5,4},{6,7},{7,6},{8,9},{9,8},{10,11... | collective-permute-start | bytes 24584 | tf_op jit(solution)/shard_map/ppermute | solution.py:310
  75.4 1.7 %collective-permute-done.13.across = f32[16,128]{1,0:T(8,128)S(1)} collective-permute-done((f32[16,128]{1,0:T(8,128)S(1)}, f32[16,128]{1,0:T(8,128)S(1)}, u32[]{:S(2)}, u32[]{:S(2)}) %collective-permute-start.13) | collective-permute-done | bytes 8224 | tf_op jit(solution)/shard_map/ppermute | solution.py:310
  77.1 4.3 %collective-permute-done.14.along = f32[16,128]{1,0:T(8,128)S(1)} collective-permute-done((f32[16,128]{1,0:T(8,128)S(1)}, f32[16,128]{1,0:T(8,128)S(1)}, u32[]{:S(2)}, u32[]{:S(2)}) %collective-permute-start.14) | collective-permute-done | bytes 8224 | tf_op jit(solution)/shard_map/ppermute | solution.py:310
  81.5 10.3 %all_to_all.5.totals = f32[32,1,128]{2,1,0:T(1,128)S(1)} all-to-all(f32[32,1,128]{2,1,0:T(1,128)S(1)} %broadcast_in_dim.8), channel_id=1, replica_groups=mesh['blk'=16,'grp'=2] {'blk','grp'}, dimensions={0} | all-to-all | bytes 32768 | tf_op jit(solution)/shard_map/all_to_all | solution.py:458
  91.8 0.6 shard_map.65
  (21 shorter events, 0.8 us)
Async XLA Ops:
  0.7 0.7 copy-start
  1.4 0.7 copy-start.1
  3.4 51.6 %collective-permute-start.7 = (f32[128,2048]{1,0:T(8,128)S(1)}, f32[128,2048]{1,0:T(8,128)}, u32[]{:S(2)}, u32[]{:S(2)}) collective-permute-start(f32[128,2048]{1,0:T(8,128)S(1)} %shard_map.56), channel_id=1, source_target_pairs={{0,2},{1,3},{2,0},{3,1},{4,6},{5,7},{6,4},{7,5},{8,10},{9,11},{10,... | collective-permute-start | bytes 3145736 | tf_op jit(solution)/shard_map/ppermute | solution.py:310
  5.2 49.8 %collective-permute-start.8 = (f32[128,2048]{1,0:T(8,128)S(1)}, f32[128,2048]{1,0:T(8,128)}, u32[]{:S(2)}, u32[]{:S(2)}) collective-permute-start(f32[128,2048]{1,0:T(8,128)S(1)} %shard_map.58.o), channel_id=1, source_target_pairs={{0,1},{1,0},{2,3},{3,2},{4,5},{5,4},{6,7},{7,6},{8,9},{9,8},{10,11... | collective-permute-start | bytes 3145736 | tf_op jit(solution)/shard_map/ppermute | solution.py:310
  7.7 47.2 %collective-permute-start.9 = (f32[128,2048]{1,0:T(8,128)S(1)}, f32[128,2048]{1,0:T(8,128)}, u32[]{:S(2)}, u32[]{:S(2)}) collective-permute-start(f32[128,2048]{1,0:T(8,128)S(1)} %shard_map.58.o), channel_id=1, source_target_pairs={{0,28},{1,29},{2,6},{3,7},{4,0},{5,1},{6,10},{7,11},{8,4},{9,5},{1... | collective-permute-start | bytes 3145736 | tf_op jit(solution)/shard_map/ppermute | solution.py:310
  12.3 1.2 %collective-permute-start.2 = (s32[24,128]{1,0:T(8,128)S(1)}, s32[24,128]{1,0:T(8,128)S(1)}, u32[]{:S(2)}, u32[]{:S(2)}) collective-permute-start(s32[24,128]{1,0:T(8,128)S(1)} %shard_map.55.o), channel_id=1, source_target_pairs={{0,2},{1,3},{2,0},{3,1},{4,6},{5,7},{6,4},{7,5},{8,10},{9,11},{10,... | collective-permute-start | bytes 36872 | tf_op jit(solution)/shard_map/ppermute | solution.py:310
  12.3 19.6 %collective-permute-start.3 = (s32[24,128]{1,0:T(8,128)S(1)}, s32[24,128]{1,0:T(8,128)S(1)}, u32[]{:S(2)}, u32[]{:S(2)}) collective-permute-start(s32[24,128]{1,0:T(8,128)S(1)} %shard_map.55.o), channel_id=1, source_target_pairs={{0,1},{1,0},{2,3},{3,2},{4,5},{5,4},{6,7},{7,6},{8,9},{9,8},{10,11... | collective-permute-start | bytes 36872 | tf_op jit(solution)/shard_map/ppermute | solution.py:310
  13.5 23.3 %collective-permute-start.4 = (s32[24,128]{1,0:T(8,128)S(1)}, s32[24,128]{1,0:T(8,128)S(1)}, u32[]{:S(2)}, u32[]{:S(2)}) collective-permute-start(s32[24,128]{1,0:T(8,128)S(1)} %shard_map.55.o), channel_id=1, source_target_pairs={{0,3},{1,2},{2,1},{3,0},{4,7},{5,6},{6,5},{7,4},{8,11},{9,10},{10,... | collective-permute-start | bytes 36872 | tf_op jit(solution)/shard_map/ppermute | solution.py:310
  31.9 6.2 %collective-permute-start.5 = (s32[24,128]{1,0:T(8,128)S(1)}, s32[24,128]{1,0:T(8,128)S(1)}, u32[]{:S(2)}, u32[]{:S(2)}) collective-permute-start(s32[24,128]{1,0:T(8,128)S(1)} %shard_map.55.o), channel_id=1, source_target_pairs={{0,28},{1,29},{2,6},{3,7},{4,0},{5,1},{6,10},{7,11},{8,4},{9,5},{1... | collective-permute-start | bytes 36872 | tf_op jit(solution)/shard_map/ppermute | solution.py:310
  36.7 5.8 %collective-permute-start.6 = (s32[24,128]{1,0:T(8,128)S(1)}, s32[24,128]{1,0:T(8,128)S(1)}, u32[]{:S(2)}, u32[]{:S(2)}) collective-permute-start(s32[24,128]{1,0:T(8,128)S(1)} %shard_map.55.o), channel_id=1, source_target_pairs={{0,30},{1,31},{2,4},{3,5},{4,2},{5,3},{6,8},{7,9},{8,6},{9,7},{10,... | collective-permute-start | bytes 36872 | tf_op jit(solution)/shard_map/ppermute | solution.py:310
  38.1 8.6 %collective-permute-start = (f32[128,512]{1,0:T(8,128)S(1)}, f32[128,512]{1,0:T(8,128)S(1)}, u32[]{:S(2)}, u32[]{:S(2)}) collective-permute-start(f32[128,512]{1,0:T(8,128)S(1)} %slice.14), channel_id=1, source_target_pairs={{0,3},{1,2},{2,1},{3,0},{4,7},{5,6},{6,5},{7,4},{8,11},{9,10},{10,... | collective-permute-start | bytes 786440 | tf_op jit(solution)/shard_map/ppermute | solution.py:310
  42.6 8.5 %collective-permute-start.1 = (f32[128,512]{1,0:T(8,128)S(1)}, f32[128,512]{1,0:T(8,128)S(1)}, u32[]{:S(2)}, u32[]{:S(2)}) collective-permute-start(f32[128,512]{1,0:T(8,128)S(1)} %slice.14), channel_id=1, source_target_pairs={{0,30},{1,31},{2,4},{3,5},{4,2},{5,3},{6,8},{7,9},{8,6},{9,7},{10,... | collective-permute-start | bytes 786440 | tf_op jit(solution)/shard_map/ppermute | solution.py:310
  46.7 19.8 %collective-permute-start.10 = (f32[128,1536]{1,0:T(8,128)}, f32[128,1536]{1,0:T(8,128)S(1)}, u32[]{:S(2)}, u32[]{:S(2)}) collective-permute-start(f32[128,1536]{1,0:T(8,128)} %slice.15), channel_id=1, source_target_pairs={{0,3},{1,2},{2,1},{3,0},{4,7},{5,6},{6,5},{7,4},{8,11},{9,10},{10,... | collective-permute-start | bytes 2359304 | tf_op jit(solution)/shard_map/ppermute | solution.py:310
  51.1 15.4 %collective-permute-start.11 = (f32[128,1536]{1,0:T(8,128)}, f32[128,1536]{1,0:T(8,128)}, u32[]{:S(2)}, u32[]{:S(2)}) collective-permute-start(f32[128,1536]{1,0:T(8,128)} %slice.15), channel_id=1, source_target_pairs={{0,30},{1,31},{2,4},{3,5},{4,2},{5,3},{6,8},{7,9},{8,6},{9,7},{10,... | collective-permute-start | bytes 2359304 | tf_op jit(solution)/shard_map/ppermute | solution.py:310
  69.4 5.8 %copy-start.2 = (f32[128,16]{0,1:T(8,128)S(1)}, f32[128,16]{0,1:T(8,128)}, u32[]{:S(2)}) copy-start(f32[128,16]{0,1:T(8,128)} %param.9) | copy-start | bytes 24580
  70.2 3.0 %collective-permute-start.12 = (f32[1024,128]{1,0:T(8,128)S(1)}, f32[1024,128]{1,0:T(8,128)S(1)}, u32[]{:S(2)}, u32[]{:S(2)}) collective-permute-start(f32[1024,128]{1,0:T(8,128)S(1)} %get-tuple-element.42), channel_id=1, source_target_pairs={{0,2},{1,3},{2,0},{3,1},{4,6},{5,7},{6,4},{7,5},{8,10},{9,11},{10,... | collective-permute-start | bytes 1572872 | tf_op jit(solution)/shard_map/ppermute | solution.py:310
  73.4 3.7 %collective-permute-start.13 = (f32[16,128]{1,0:T(8,128)S(1)}, f32[16,128]{1,0:T(8,128)S(1)}, u32[]{:S(2)}, u32[]{:S(2)}) collective-permute-start(f32[16,128]{1,0:T(8,128)S(1)} %get-tuple-element.45), channel_id=1, source_target_pairs={{0,1},{1,0},{2,3},{3,2},{4,5},{5,4},{6,7},{7,6},{8,9},{9,8},{10,11... | collective-permute-start | bytes 24584 | tf_op jit(solution)/shard_map/ppermute | solution.py:310
  75.1 6.3 %collective-permute-start.14 = (f32[16,128]{1,0:T(8,128)S(1)}, f32[16,128]{1,0:T(8,128)S(1)}, u32[]{:S(2)}, u32[]{:S(2)}) collective-permute-start(f32[16,128]{1,0:T(8,128)S(1)} %get-tuple-element.46), channel_id=1, source_target_pairs={{28,0},{29,1},{6,2},{7,3},{0,4},{1,5},{10,6},{11,7},{4,8},{5,9},{1... | collective-permute-start | bytes 24584 | tf_op jit(solution)/shard_map/ppermute | solution.py:310

commit v2 on v1

v2 whole, which is shorter than its diff:
```python
import functools

import jax
import jax.numpy as jnp
from jax import lax
from jax.experimental import pallas as pl
from jax.experimental.pallas import tpu as pltpu
from jax.sharding import PartitionSpec as P


AXES = ("blk", "grp")
LANES = 128
SUBLANES = 8
NT = (((1,), (1,)), ((), ()))
FAR = 1e30
NEVER = -3e38


def exchange(tiles, i, j):
    low, high = jnp.minimum(tiles[i], tiles[j]), jnp.maximum(tiles[i], tiles[j])
    tiles[i], tiles[j] = low, high


def sort_tiles(tiles):
    tiles = list(tiles)
    n = len(tiles)
    p = 1
    while p < n:
        k = p
        while k >= 1:
            for j in range(k % p, n - k, 2 * k):
                for i in range(min(k, n - j - k)):
                    if (i + j) // (2 * p) == (i + j + k) // (2 * p):
                        exchange(tiles, i + j, i + j + k)
            k //= 2
        p *= 2
    return tiles


def bitonic(tiles):
    tiles = list(tiles)
    step = len(tiles) // 2
    while step >= 1:
        for i in range(len(tiles)):
            if not i & step:
                exchange(tiles, i, i + step)
        step //= 2
    return tiles


def merge_lowest(a, b, keep):
    if len(a) + len(b) <= keep:
        return bitonic(a + b[::-1])
    return bitonic([jnp.minimum(x, y) for x, y in zip(a, b[::-1])])


def lowest(tiles, keep):
    group = 1
    while group * 2 <= min(keep, len(tiles)):
        group *= 2
    while len(tiles) % group:
        tiles = tiles + [jnp.full((SUBLANES, LANES), FAR, jnp.float32)]
    lists = [sort_tiles(tiles[i : i + group]) for i in range(0, len(tiles), group)]
    while len(lists) > 1:
        paired = [
            merge_lowest(lists[i], lists[i + 1], keep)
            for i in range(0, len(lists) - 1, 2)
        ]
        if len(lists) % 2:
            rest = lists[-1]
            while len(rest) < len(paired[0]):
                rest = rest + [jnp.full((SUBLANES, LANES), FAR, jnp.float32)]
            paired.append(rest)
        lists = paired
    found = lists[0]
    shift = SUBLANES // 2
    while shift:
        found = merge_lowest(found, [pltpu.roll(t, shift, 0) for t in found], keep)
        shift //= 2
    return found


def tiles_of(array):
    return [array[i : i + SUBLANES] for i in range(0, array.shape[0], SUBLANES)]


def describe_kernel(count_ref, index_ref, lists_ref, meta_ref):
    listed, pts = lists_ref.shape
    slots = index_ref.shape[1]
    meta_ref[0:listed] = lists_ref[...]
    spread = jnp.broadcast_to(index_ref[...].astype(jnp.float32), (pts, slots)).T
    slot = lax.broadcasted_iota(jnp.int32, (slots, pts), 0)
    row = lax.broadcasted_iota(jnp.int32, (slots, pts), 1)
    hit = (spread.astype(jnp.int32) == row) & (slot < count_ref[0])
    live = jnp.max(jnp.where(hit, 1.0, 0.0), axis=0, keepdims=True)
    meta_ref[listed : listed + SUBLANES] = jnp.broadcast_to(
        live.astype(jnp.int32), (SUBLANES, pts)
    )


def mask_kernel(
    listed, cycle, members, o, t, o2, t2, u, v, own_ref, far_ref
):
    blk, grp = lax.axis_index("blk"), lax.axis_index("grp")
    turned = lax.rem(blk, 2)
    steps = (0, 1 - 2 * turned, 0, 1 - 2 * turned, 2 - 4 * turned, 2 * turned - 1)
    sides = (grp, grp, 1 - grp, 1 - grp, grp, grp)
    base = [
        lax.rem(blk + step + cycle, cycle) * members + side
        for step, side in zip(steps, sides)
    ]
    metas = (o, t, o2, t2, u, v)
    pts = o.shape[1]
    alive = [
        jnp.broadcast_to(m[listed : listed + 1].astype(jnp.float32), (pts, pts)).T > 0.5
        for m in metas
    ]
    row = lax.broadcasted_iota(jnp.int32, (pts, pts), 0)
    lane = lax.broadcasted_iota(jnp.int32, (pts, pts), 1)

    def floor(target, cand):
        ids = row + base[cand] * pts
        lists = metas[target]
        bad = jnp.logical_not(alive[cand])
        for k in range(listed):
            bad = bad | (ids == lists[k : k + 1])
        if target == cand:
            bad = bad | (row == lane)
        return jnp.where(bad, FAR, NEVER)

    for i in range(6):
        own_ref[i * pts : (i + 1) * pts] = floor(0, i)
    for i, (target, cand) in enumerate(((2, 4), (2, 5), (4, 0), (4, 2))):
        far_ref[i * pts : (i + 1) * pts] = floor(target, cand)


def split(x):
    high = x.astype(jnp.bfloat16)
    return high, (x - high.astype(jnp.float32)).astype(jnp.bfloat16)


def squared(x):
    total = x[:, :LANES] * x[:, :LANES]
    for j in range(LANES, x.shape[1], LANES):
        total = total + x[:, j : j + LANES] * x[:, j : j + LANES]
    return total


def product(rows, columns):
    def dot(a, b):
        return lax.dot_general(a, b, NT, preferred_element_type=jnp.float32)

    return (
        dot(rows[0], columns[1]) + dot(rows[1], columns[0]) + dot(rows[0], columns[0])
    )


def lengths(total):
    return (
        jnp.sum(total, axis=1, keepdims=True),
        jnp.sum(total.T, axis=0, keepdims=True),
    )


def early_kernel(o, t, o2, u, hi_ref, lo_ref, squares_ref, mine_ref, sib_ref):
    pts = o.shape[0]
    norms = []
    for i, ref in enumerate((o, t, o2, u)):
        at = slice(i * pts, (i + 1) * pts)
        hi_ref[at], lo_ref[at] = split(ref[...])
        squares_ref[at] = squared(ref[...])
        norms.append(lengths(squares_ref[at]))

    def part(first, last):
        at = slice(first * pts, last * pts)
        return hi_ref[at], lo_ref[at]

    near = product(part(0, 4), part(0, 2))

    def put(ref, at, block, cand, target):
        ref[at * pts : (at + 1) * pts] = (
            norms[cand][0] + norms[target][1] - 2.0 * block
        )

    for i in range(4):
        at = slice(i * pts, (i + 1) * pts)
        put(mine_ref, i, near[at, :pts], i, 0)
        put(sib_ref, (1, 0, 2, 3)[i], near[at, pts:], i, 1)
    put(mine_ref, 4, product(part(3, 4), part(2, 3)), 3, 2)


def late_products(blocks, hi, lo):
    crossed, beyond = blocks
    lanes = tuple(jnp.concatenate(pair, axis=0) for pair in zip(crossed, beyond))
    rows = tuple(jnp.concatenate(pair, axis=0) for pair in zip((hi, lo), beyond))
    return product(rows, lanes)


def middle_kernel(t2, v, hi, lo, partial_ref, squares_ref):
    pts, width = t2.shape
    blocks = split(t2[...]), split(v[...])
    partial_ref[...] = late_products(blocks, hi[:, :width], lo[:, :width])
    squares_ref[0:pts] = squared(t2[...])
    squares_ref[pts : 2 * pts] = squared(v[...])


def late_kernel(t2, v, hi, lo, squares, partial, more, mine_ref, sib_ref):
    pts, width = t2.shape
    start = hi.shape[1] - width
    blocks = split(t2[...]), split(v[...])
    total = partial[...] + late_products(blocks, hi[:, start:], lo[:, start:])
    of_o, of_t, of_o2, of_u = [
        lengths(squares[i * pts : (i + 1) * pts]) for i in range(4)
    ]
    of_t2 = lengths(more[0:pts] + squared(t2[...]))
    of_v = lengths(more[pts : 2 * pts] + squared(v[...]))

    def block(row, lane):
        return total[
            row * pts : (row + 1) * pts, lane * pts : (lane + 1) * pts
        ]

    def put(ref, at, product, cand, target):
        ref[at * pts : (at + 1) * pts] = cand[0] + target[1] - 2.0 * product

    put(mine_ref, 0, block(0, 0).T, of_t2, of_o)
    put(mine_ref, 1, block(0, 1).T, of_v, of_o)
    put(mine_ref, 2, block(2, 1).T, of_v, of_o2)
    put(sib_ref, 0, block(1, 0).T, of_t2, of_t)
    put(sib_ref, 1, block(1, 1).T, of_v, of_t)
    put(sib_ref, 2, block(4, 0), of_v, of_t2)
    put(sib_ref, 3, block(3, 0), of_u, of_t2)


def exchange_kernel(
    scale, keep, mine_early, mine_late, their_late, floors, across_ref, along_ref
):
    pts = floors.shape[1]

    def rows(ref, i):
        return ref[i * pts : (i + 1) * pts]

    def store(ref, blocks):
        tiles = []
        for i, block in blocks:
            tiles += tiles_of(jnp.maximum(block * scale, rows(floors, i)))
        for i, tile in enumerate(lowest(tiles, keep)):
            ref[i : i + 1] = tile[0:1]

    near_u = rows(mine_early, 3) + rows(their_late, 1)
    far_u = rows(mine_early, 4) + rows(their_late, 2)
    far_v = rows(mine_late, 2) + rows(their_late, 3)
    store(across_ref, ((0, far_u), (1, far_v)))
    store(along_ref, ((2, near_u.T), (3, far_u.T)))


def own_kernel(
    scale, keep, mine_early, their_early, mine_late, their_late, floors, old, found_ref
):
    pts = floors.shape[1]

    def rows(ref, i):
        return ref[i * pts : (i + 1) * pts]

    blocks = (
        rows(mine_early, 0) + rows(their_early, 0),
        rows(mine_early, 1) + rows(their_early, 1),
        rows(mine_early, 2) + rows(their_late, 0),
        rows(mine_late, 0) + rows(their_early, 2),
        rows(mine_early, 3) + rows(their_late, 1),
        rows(mine_late, 1) + rows(their_early, 3),
    )
    tiles = []
    for i, block in enumerate(blocks):
        tiles += tiles_of(jnp.maximum(block * scale, rows(floors, i)))
    for i, tile in enumerate(lowest(tiles, keep)):
        found_ref[i : i + 1] = tile[0:1]
    found_ref[keep : 2 * keep] = old[...]


def finish_kernel(keep, found, across, along, best_ref, total_ref):
    tiles = tiles_of(found[...]) + tiles_of(across[...]) + tiles_of(along[...])
    ranked = lowest(tiles, keep)
    total = jnp.sum(ranked[keep - 1][0:1], axis=1, keepdims=True)
    total_ref[...] = jnp.broadcast_to(total[None], total_ref.shape)
    for i, tile in enumerate(ranked):
        best_ref[i : i + 1] = tile[0:1]


def scale_kernel(points_in_all, best, totals, out_ref):
    total = jnp.sum(totals[:, 0, :], axis=0, keepdims=True)
    out_ref[...] = best[...] / (total * (1.0 / points_in_all))


def cut_kernel(turned, pieces, points, *refs):
    *outs, done = refs[-1 - len(pieces) :]
    core = lax.rem(lax.axis_index("blk"), 2)
    side = 1 - core if turned else core
    half = points.shape[1] // 2
    copies = []
    for (offset, count), out in zip(pieces, outs):
        rows, width = out.shape
        tall = rows // count
        start = pl.multiple_of(side * half + offset, LANES)
        for i in range(count):
            at = pl.ds(i * tall, tall)
            copies.append(
                pltpu.make_async_copy(
                    points.at[at, pl.ds(start, width)],
                    out.at[at],
                    done.at[len(copies)],
                )
            )
    for copy in copies:
        copy.start()
    for copy in copies:
        copy.wait()


def body(points, cand_index, cand_count, neighbor_ids, old_dist):
    pts, width = points.shape
    keep = old_dist.shape[1]
    cycle = lax.axis_size("blk")
    members = lax.axis_size("grp")
    half = width // 2
    f32 = jnp.float32

    def links(move):
        return [
            (b * members + g, (move(b, g)[0] % cycle) * members + move(b, g)[1])
            for b in range(cycle)
            for g in range(members)
        ]

    sibling = links(lambda b, g: (b ^ 1, g))
    over_same = links(lambda b, g: (b, 1 - g))
    over_cross = links(lambda b, g: (b ^ 1, 1 - g))
    along_same = links(lambda b, g: (b + (2 if b % 2 else -2), g))
    along_cross = links(lambda b, g: (b + (1 if b % 2 else -1), g))
    along_back = [(b, a) for a, b in along_same]

    def send(array, pairs):
        return lax.ppermute(array, AXES, pairs)

    whole_array = pl.BlockSpec(memory_space=pltpu.VMEM)
    scalars = pl.BlockSpec(memory_space=pltpu.SMEM)

    def call(
        kernel,
        out_shape,
        args,
        flops=0,
        first=whole_array,
        second=whole_array,
        scratch=(),
        limit=4,
    ):
        specs = [first, second] + [whole_array] * len(args)
        return pl.pallas_call(
            kernel,
            out_shape=out_shape,
            in_specs=specs[: len(args)],
            scratch_shapes=scratch,
            out_specs=jax.tree.map(lambda _: whole_array, out_shape),
            cost_estimate=pl.CostEstimate(
                flops=flops, bytes_accessed=0, transcendentals=0
            ),
            compiler_params=pltpu.CompilerParams(vmem_limit_bytes=limit << 20),
        )(*args)

    def array(rows, lanes=pts, dtype=f32):
        return jax.ShapeDtypeStruct((rows, lanes), dtype)

    meta = call(
        describe_kernel,
        array(keep + SUBLANES, dtype=jnp.int32),
        (cand_count, cand_index, neighbor_ids.T),
        first=scalars,
    )

    def cut(turned, pieces, after=()):
        held = pl.BlockSpec(memory_space=pltpu.HBM)
        return call(
            functools.partial(
                cut_kernel, turned, [(at, count) for at, _, count in pieces]
            ),
            [pltpu.VMEM((pts, wide), f32) for _, wide, _ in pieces],
            (pltpu.with_memory_space_constraint(points, pltpu.HBM),) + after,
            first=held,
            scratch=[
                pltpu.SemaphoreType.DMA((sum(count for _, _, count in pieces),))
            ],
        )

    most = half * 3 // 4
    (o,) = cut(False, [(0, half, 8)])
    other, other_most, other_rest = cut(
        True, [(0, half, 4), (0, most, 4), (most, half - most, 2)], (meta,)
    )

    o2 = send(o, over_same)
    u = send(o, along_same)
    metas = (
        meta,
        send(meta, sibling),
        send(meta, over_same),
        send(meta, over_cross),
        send(meta, along_same),
        send(meta, along_cross),
    )
    t2 = send(other_most, over_cross)
    v = send(other_most, along_cross)
    t2_rest = send(other_rest, over_cross)
    v_rest = send(other_rest, along_cross)
    t = send(other, sibling)

    own_floor, far_floor = call(
        functools.partial(mask_kernel, keep, cycle, members),
        (array(6 * pts), array(4 * pts)),
        metas,
        flops=1 << 29,
    )

    block_flops = 6 * pts * pts * half
    hi, lo, squares, mine_early, for_sibling = call(
        early_kernel,
        (
            array(4 * pts, half, jnp.bfloat16),
            array(4 * pts, half, jnp.bfloat16),
            array(4 * pts, LANES),
            array(5 * pts),
            array(4 * pts),
        ),
        (o, t, o2, u),
        flops=9 * block_flops,
        limit=24,
    )
    their_early = send(for_sibling, sibling)
    partial, more = call(
        middle_kernel,
        (array(5 * pts, 2 * pts), array(2 * pts, LANES)),
        (t2, v, hi, lo),
        flops=8 * block_flops,
        limit=24,
    )
    t2_rest, v_rest, their_early, own_floor, far_floor = lax.optimization_barrier(
        (t2_rest, v_rest, their_early, own_floor, far_floor)
    )
    mine_late, for_sibling = call(
        late_kernel,
        (array(3 * pts), array(4 * pts)),
        (t2_rest, v_rest, hi, lo, squares, partial, more),
        flops=2 * block_flops,
        limit=24,
    )
    their_late = send(for_sibling, sibling)

    scale = 1.0 / width
    across, along = call(
        functools.partial(exchange_kernel, scale, keep),
        (array(keep),) * 2,
        (mine_early, mine_late, their_late, far_floor),
        flops=1 << 28,
    )
    across = send(across, over_same)
    along = send(along, along_back)
    found = call(
        functools.partial(own_kernel, scale, keep),
        array(2 * keep),
        (mine_early, their_early, mine_late, their_late, own_floor, old_dist.T),
        flops=1 << 29,
    )
    devices = cycle * members
    best, total = call(
        functools.partial(finish_kernel, keep),
        (array(keep), jax.ShapeDtypeStruct((devices, 1, LANES), f32)),
        (found, across, along),
        flops=1 << 26,
    )
    totals = lax.all_to_all(total, AXES, 0, 0)
    scaled = call(
        functools.partial(scale_kernel, pts * devices), array(keep), (best, totals)
    )
    return scaled.T


def solution(mesh):
    return jax.shard_map(
        body,
        mesh=mesh,
        in_specs=(
            P(AXES, None),
            P(AXES, None),
            P(AXES),
            P(AXES, None),
            P(AXES, None),
        ),
        out_specs=P(AXES, None),
        check_vma=False,
    )
```

time: 92.8 us -> 83.6 us (0.901)
  waiting for transfers between devices: 44.5 us -> 34.6 us
  starting transfers between devices: 20.6 us -> 25.6 us
  Pallas kernels: 13.9 us -> 10.8 us
  local copies, waits for them, and re-layouts: 2.42 us -> 1.35 us
    ppermute x15 -> x16, waiting for transfers between devices: 44.5 us -> 34.6 us  [send(): return lax.ppermute(array, AXES, pairs)]
    ppermute x15 -> x16, starting transfers between devices: 20.6 us -> 25.6 us  [send(): return lax.ppermute(array, AXES, pairs)]
    pallas_call x11, Pallas kernels: 13.9 us -> 10.8 us  [call(): pl.pallas_call(kernel, out_shape=out_shape, in_specs=specs[:len(args)], s...]
    slice x2 -> x0, local copies, waits for them, and re-layouts: 0.97 us -> none  [the longest x1 0.95 us: body(): t2 = send(other[:, :most], over_cross)]
  transfers between devices with their start and end apart: 15 -> 16, of which waited for: 10 -> 8; matrix products, arithmetic and copies ran while one was open for 1% -> 0% of each run, Pallas kernels for 9% -> 9%
where the time goes in v2:
time: 83.6 us; the launch traced here: 83.3 us
  waiting for transfers between devices  34.6 us (41%)
  starting transfers between devices  25.6 us (31%)
  Pallas kernels  10.8 us (13%)
  blocking collectives  10.2 us (12%)
  local copies, waits for them, and re-layouts  1.35 us (2%)
    ppermute x16, waiting for transfers between devices, send(): return lax.ppermute(array, AXES, pairs)  34.6 us
    ppermute x16, starting transfers between devices, send(): return lax.ppermute(array, AXES, pairs)  25.6 us
    pallas_call x11, Pallas kernels, call(): pl.pallas_call(kernel, out_shape=out_shape, in_specs=specs[:len(args)], s...  10.8 us
    all_to_all x1, blocking collectives, body(): totals = lax.all_to_all(total, AXES, 0, 0)  10.2 us
  transfers between devices with their start and end apart: 16, of which 8 were waited for; matrix products, arithmetic and copies ran while one was open for 0% of the time, Pallas kernels for 9%

profile of v2, /device:TPU:0, one launch (start us, length us, event | category | flops | bytes accessed | tf_op | source)
XLA Modules:
  0.0 83.3 jit_solution(13486385016270839756)
XLA Ops:
  0.7 0.7 copy-done
  1.4 0.7 copy-done.1
  2.1 1.7 %shard_map.57 = (f32[128,2048]{1,0:T(8,128)S(1)}, f32[128,1536]{1,0:T(8,128)S(1)}, f32[128,512]{1,0:T(8,128)S(1)}) custom-call(f32[128,4096]{1,0:T(8,128)} %points.3, s32[24,128]{1,0:T(8,128)S(1)} %shard_map.56.refs_0_.o), custom_call_target="tpu_custom_call" | custom-call | tf_op jit(solution)/shard_map/pallas_call | solution.py:359
  3.8 0.6 collective-permute-start
  4.4 1.3 %shard_map.55.o = f32[128,2048]{1,0:T(8,128)S(1)} custom-call(f32[128,4096]{1,0:T(8,128)} %points.3), custom_call_target="tpu_custom_call" | custom-call | tf_op jit(solution)/shard_map/pallas_call | solution.py:359
  5.7 2.5 %collective-permute-start.1 = (f32[128,2048]{1,0:T(8,128)S(1)}, f32[128,2048]{1,0:T(8,128)S(1)}, u32[]{:S(2)}, u32[]{:S(2)}) collective-permute-start(f32[128,2048]{1,0:T(8,128)S(1)} %shard_map.55.o), channel_id=1, source_target_pairs={{0,1},{1,0},{2,3},{3,2},{4,5},{5,4},{6,7},{7,6},{8,9},{9,8},{10,11... | collective-permute-start | bytes 3145736 | tf_op jit(solution)/shard_map/ppermute | solution.py:343
  8.3 4.6 %collective-permute-start.2 = (f32[128,2048]{1,0:T(8,128)S(1)}, f32[128,2048]{1,0:T(8,128)S(1)}, u32[]{:S(2)}, u32[]{:S(2)}) collective-permute-start(f32[128,2048]{1,0:T(8,128)S(1)} %shard_map.55.o), channel_id=1, source_target_pairs={{0,28},{1,29},{2,6},{3,7},{4,0},{5,1},{6,10},{7,11},{8,4},{9,5},{1... | collective-permute-start | bytes 3145736 | tf_op jit(solution)/shard_map/ppermute | solution.py:343
  12.8 0.5 collective-permute-start.7
  13.4 0.6 collective-permute-done.6.t
  14.0 0.7 collective-permute-start.11
  14.7 17.8 %collective-permute-done.7.o2 = s32[24,128]{1,0:T(8,128)S(1)} collective-permute-done((s32[24,128]{1,0:T(8,128)S(1)}, s32[24,128]{1,0:T(8,128)S(1)}, u32[]{:S(2)}, u32[]{:S(2)}) %collective-permute-start.7) | collective-permute-done | bytes 12320 | tf_op jit(solution)/shard_map/ppermute | solution.py:343
  32.5 3.8 %collective-permute-start.12 = (f32[128,1536]{1,0:T(8,128)S(1)}, f32[128,1536]{1,0:T(8,128)S(1)}, u32[]{:S(2)}, u32[]{:S(2)}) collective-permute-start(f32[128,1536]{1,0:T(8,128)S(1)} %get-tuple-element.40), channel_id=1, source_target_pairs={{0,30},{1,31},{2,4},{3,5},{4,2},{5,3},{6,8},{7,9},{8,6},{9,7},{10,... | collective-permute-start | bytes 2359304 | tf_op jit(solution)/shard_map/ppermute | solution.py:343
  36.4 2.6 %collective-permute-start.9 = (s32[24,128]{1,0:T(8,128)S(1)}, s32[24,128]{1,0:T(8,128)S(1)}, u32[]{:S(2)}, u32[]{:S(2)}) collective-permute-start(s32[24,128]{1,0:T(8,128)S(1)} %shard_map.56.refs_0_.o), channel_id=1, source_target_pairs={{0,28},{1,29},{2,6},{3,7},{4,0},{5,1},{6,10},{7,11},{8,4},{9,5},{1... | collective-permute-start | bytes 36872 | tf_op jit(solution)/shard_map/ppermute | solution.py:343
  39.0 3.0 %collective-permute-start.10 = (s32[24,128]{1,0:T(8,128)S(1)}, s32[24,128]{1,0:T(8,128)S(1)}, u32[]{:S(2)}, u32[]{:S(2)}) collective-permute-start(s32[24,128]{1,0:T(8,128)S(1)} %shard_map.56.refs_0_.o), channel_id=1, source_target_pairs={{0,30},{1,31},{2,4},{3,5},{4,2},{5,3},{6,8},{7,9},{8,6},{9,7},{10,... | collective-permute-start | bytes 36872 | tf_op jit(solution)/shard_map/ppermute | solution.py:343
  42.0 2.4 %shard_map.58 = (bf16[512,2048]{1,0:T(8,128)(2,1)S(1)}, bf16[512,2048]{1,0:T(8,128)(2,1)S(1)}, f32[512,128]{1,0:T(8,128)S(1)}, f32[640,128]{1,0:T(8,128)S(1)}, f32[512,128]{1,0:T(8,128)S(1)}) custom-call(f32[128,2048]{1,0:T(8,128)S(1)} %shard_map.55.o, f32[128,2048]{1,0:T(8,128)S(1)} %collective-permute-done.t, f32[128,2048]{1,0:T(8,128)S(1)} %collective-permute-done.1.o2, ...), custom_call_target="tpu_custom_call" | custom-call | flops 1811939328 | tf_op jit(solution)/shard_map/pallas_call | solution.py:359
  44.5 4.8 %collective-permute-done.8.t2 = s32[24,128]{1,0:T(8,128)S(1)} collective-permute-done((s32[24,128]{1,0:T(8,128)S(1)}, s32[24,128]{1,0:T(8,128)S(1)}, u32[]{:S(2)}, u32[]{:S(2)}) %collective-permute-start.8) | collective-permute-done | bytes 12320 | tf_op jit(solution)/shard_map/ppermute | solution.py:343
  49.2 1.4 %collective-permute-start.3 = (f32[128,512]{1,0:T(8,128)S(1)}, f32[128,512]{1,0:T(8,128)S(1)}, u32[]{:S(2)}, u32[]{:S(2)}) collective-permute-start(f32[128,512]{1,0:T(8,128)S(1)} %get-tuple-element.30), channel_id=1, source_target_pairs={{0,3},{1,2},{2,1},{3,0},{4,7},{5,6},{6,5},{7,4},{8,11},{9,10},{10,... | collective-permute-start | bytes 786440 | tf_op jit(solution)/shard_map/ppermute | solution.py:343
  50.6 2.8 %collective-permute-done.9.u = s32[24,128]{1,0:T(8,128)S(1)} collective-permute-done((s32[24,128]{1,0:T(8,128)S(1)}, s32[24,128]{1,0:T(8,128)S(1)}, u32[]{:S(2)}, u32[]{:S(2)}) %collective-permute-start.9) | collective-permute-done | bytes 12320 | tf_op jit(solution)/shard_map/ppermute | solution.py:343
  53.4 4.2 %collective-permute-start.4 = (f32[128,512]{1,0:T(8,128)S(1)}, f32[128,512]{1,0:T(8,128)S(1)}, u32[]{:S(2)}, u32[]{:S(2)}) collective-permute-start(f32[128,512]{1,0:T(8,128)S(1)} %get-tuple-element.30), channel_id=1, source_target_pairs={{0,30},{1,31},{2,4},{3,5},{4,2},{5,3},{6,8},{7,9},{8,6},{9,7},{10,... | collective-permute-start | bytes 786440 | tf_op jit(solution)/shard_map/ppermute | solution.py:343
  57.6 1.5 %shard_map.59 = (f32[768,128]{1,0:T(8,128)S(1)}, f32[512,128]{1,0:T(8,128)S(1)}) custom-call(s32[24,128]{1,0:T(8,128)S(1)} %shard_map.56.refs_0_.o, s32[24,128]{1,0:T(8,128)S(1)} %collective-permute-done.6.t, s32[24,128]{1,0:T(8,128)S(1)} %collective-permute-done.7.o2, s32[24,128]{1,0:T(8,128)S(1)} %collective-permute-done.8.t2, ...), custom_call_target="tpu_custom_call" | custom-call | flops 536870912 | tf_op jit(solution)/shard_map/pallas_call | solution.py:359
  59.1 1.8 %shard_map.60 = (f32[640,256]{1,0:T(8,128)S(1)}, f32[256,128]{1,0:T(8,128)S(1)}) custom-call(f32[128,1536]{1,0:T(8,128)S(1)} %collective-permute-done.11.t2, f32[128,1536]{1,0:T(8,128)S(1)} %collective-permute-done.12.v, bf16[512,2048]{1,0:T(8,128)(2,1)S(1)} %get-tuple-element.37.hi, bf16[512,2048]{1,0:T(8,128)(2,1)S(1)} %get-tuple-element.38.lo), custom_call_target="tpu_custom_call" | custom-call | flops 1610612736 | tf_op jit(solution)/shard_map/pallas_call | solution.py:359
  60.9 1.0 %collective-permute-done.4.v = f32[128,512]{1,0:T(8,128)S(1)} collective-permute-done((f32[128,512]{1,0:T(8,128)S(1)}, f32[128,512]{1,0:T(8,128)S(1)}, u32[]{:S(2)}, u32[]{:S(2)}) %collective-permute-start.4) | collective-permute-done | bytes 262176 | tf_op jit(solution)/shard_map/ppermute | solution.py:343
  61.9 0.8 shard_map.61
  62.7 1.5 %collective-permute-done.13.their_late = f32[512,128]{1,0:T(8,128)S(1)} collective-permute-done((f32[512,128]{1,0:T(8,128)S(1)}, f32[512,128]{1,0:T(8,128)S(1)}, u32[]{:S(2)}, u32[]{:S(2)}) %collective-permute-start.13) | collective-permute-done | bytes 262176 | tf_op jit(solution)/shard_map/ppermute | solution.py:343
  64.2 0.2 shard_map.63
  64.5 1.6 %collective-permute-start.14 = (f32[16,128]{1,0:T(8,128)S(1)}, f32[16,128]{1,0:T(8,128)S(1)}, u32[]{:S(2)}, u32[]{:S(2)}) collective-permute-start(f32[16,128]{1,0:T(8,128)S(1)} %get-tuple-element.47), channel_id=1, source_target_pairs={{0,1},{1,0},{2,3},{3,2},{4,5},{5,4},{6,7},{7,6},{8,9},{9,8},{10,11... | collective-permute-start | bytes 24584 | tf_op jit(solution)/shard_map/ppermute | solution.py:343
  66.0 0.3 shard_map.62.found
  66.3 1.9 %collective-permute-done.14.across = f32[16,128]{1,0:T(8,128)S(1)} collective-permute-done((f32[16,128]{1,0:T(8,128)S(1)}, f32[16,128]{1,0:T(8,128)S(1)}, u32[]{:S(2)}, u32[]{:S(2)}) %collective-permute-start.14) | collective-permute-done | bytes 8224 | tf_op jit(solution)/shard_map/ppermute | solution.py:343
  68.2 4.2 %collective-permute-done.15.along = f32[16,128]{1,0:T(8,128)S(1)} collective-permute-done((f32[16,128]{1,0:T(8,128)S(1)}, f32[16,128]{1,0:T(8,128)S(1)}, u32[]{:S(2)}, u32[]{:S(2)}) %collective-permute-start.15) | collective-permute-done | bytes 8224 | tf_op jit(solution)/shard_map/ppermute | solution.py:343
  72.4 0.1 shard_map.64
  72.5 10.2 %all_to_all.5.totals = f32[32,1,128]{2,1,0:T(1,128)S(1)} all-to-all(f32[32,1,128]{2,1,0:T(1,128)S(1)} %get-tuple-element.50), channel_id=1, replica_groups=mesh['blk'=16,'grp'=2] {'blk','grp'}, dimensions={0} | all-to-all | bytes 32768 | tf_op jit(solution)/shard_map/all_to_all | solution.py:480
  82.7 0.6 shard_map.65
  (18 shorter events, 0.2 us)
Async XLA Ops:
  0.7 0.7 copy-start
  1.4 0.7 copy-start.1
  3.8 32.6 %collective-permute-start = (f32[128,2048]{1,0:T(8,128)S(1)}, f32[128,2048]{1,0:T(8,128)S(1)}, u32[]{:S(2)}, u32[]{:S(2)}) collective-permute-start(f32[128,2048]{1,0:T(8,128)S(1)} %get-tuple-element.28), channel_id=1, source_target_pairs={{0,2},{1,3},{2,0},{3,1},{4,6},{5,7},{6,4},{7,5},{8,10},{9,11},{10,... | collective-permute-start | bytes 3145736 | tf_op jit(solution)/shard_map/ppermute | solution.py:343
  5.7 30.7 %collective-permute-start.1 = (f32[128,2048]{1,0:T(8,128)S(1)}, f32[128,2048]{1,0:T(8,128)S(1)}, u32[]{:S(2)}, u32[]{:S(2)}) collective-permute-start(f32[128,2048]{1,0:T(8,128)S(1)} %shard_map.55.o), channel_id=1, source_target_pairs={{0,1},{1,0},{2,3},{3,2},{4,5},{5,4},{6,7},{7,6},{8,9},{9,8},{10,11... | collective-permute-start | bytes 3145736 | tf_op jit(solution)/shard_map/ppermute | solution.py:343
  8.3 30.7 %collective-permute-start.2 = (f32[128,2048]{1,0:T(8,128)S(1)}, f32[128,2048]{1,0:T(8,128)S(1)}, u32[]{:S(2)}, u32[]{:S(2)}) collective-permute-start(f32[128,2048]{1,0:T(8,128)S(1)} %shard_map.55.o), channel_id=1, source_target_pairs={{0,28},{1,29},{2,6},{3,7},{4,0},{5,1},{6,10},{7,11},{8,4},{9,5},{1... | collective-permute-start | bytes 3145736 | tf_op jit(solution)/shard_map/ppermute | solution.py:343
  12.8 1.2 %collective-permute-start.6 = (s32[24,128]{1,0:T(8,128)S(1)}, s32[24,128]{1,0:T(8,128)S(1)}, u32[]{:S(2)}, u32[]{:S(2)}) collective-permute-start(s32[24,128]{1,0:T(8,128)S(1)} %shard_map.56.refs_0_.o), channel_id=1, source_target_pairs={{0,2},{1,3},{2,0},{3,1},{4,6},{5,7},{6,4},{7,5},{8,10},{9,11},{10,... | collective-permute-start | bytes 36872 | tf_op jit(solution)/shard_map/ppermute | solution.py:343
  12.8 19.7 %collective-permute-start.7 = (s32[24,128]{1,0:T(8,128)S(1)}, s32[24,128]{1,0:T(8,128)S(1)}, u32[]{:S(2)}, u32[]{:S(2)}) collective-permute-start(s32[24,128]{1,0:T(8,128)S(1)} %shard_map.56.refs_0_.o), channel_id=1, source_target_pairs={{0,1},{1,0},{2,3},{3,2},{4,5},{5,4},{6,7},{7,6},{8,9},{9,8},{10,11... | collective-permute-start | bytes 36872 | tf_op jit(solution)/shard_map/ppermute | solution.py:343
  14.0 45.1 %collective-permute-start.11 = (f32[128,1536]{1,0:T(8,128)S(1)}, f32[128,1536]{1,0:T(8,128)S(1)}, u32[]{:S(2)}, u32[]{:S(2)}) collective-permute-start(f32[128,1536]{1,0:T(8,128)S(1)} %get-tuple-element.40), channel_id=1, source_target_pairs={{0,3},{1,2},{2,1},{3,0},{4,7},{5,6},{6,5},{7,4},{8,11},{9,10},{10,... | collective-permute-start | bytes 2359304 | tf_op jit(solution)/shard_map/ppermute | solution.py:343
  32.5 26.5 %collective-permute-start.12 = (f32[128,1536]{1,0:T(8,128)S(1)}, f32[128,1536]{1,0:T(8,128)S(1)}, u32[]{:S(2)}, u32[]{:S(2)}) collective-permute-start(f32[128,1536]{1,0:T(8,128)S(1)} %get-tuple-element.40), channel_id=1, source_target_pairs={{0,30},{1,31},{2,4},{3,5},{4,2},{5,3},{6,8},{7,9},{8,6},{9,7},{10,... | collective-permute-start | bytes 2359304 | tf_op jit(solution)/shard_map/ppermute | solution.py:343
  36.4 12.9 %collective-permute-start.8 = (s32[24,128]{1,0:T(8,128)S(1)}, s32[24,128]{1,0:T(8,128)S(1)}, u32[]{:S(2)}, u32[]{:S(2)}) collective-permute-start(s32[24,128]{1,0:T(8,128)S(1)} %shard_map.56.refs_0_.o), channel_id=1, source_target_pairs={{0,3},{1,2},{2,1},{3,0},{4,7},{5,6},{6,5},{7,4},{8,11},{9,10},{10,... | collective-permute-start | bytes 36872 | tf_op jit(solution)/shard_map/ppermute | solution.py:343
  36.4 17.0 %collective-permute-start.9 = (s32[24,128]{1,0:T(8,128)S(1)}, s32[24,128]{1,0:T(8,128)S(1)}, u32[]{:S(2)}, u32[]{:S(2)}) collective-permute-start(s32[24,128]{1,0:T(8,128)S(1)} %shard_map.56.refs_0_.o), channel_id=1, source_target_pairs={{0,28},{1,29},{2,6},{3,7},{4,0},{5,1},{6,10},{7,11},{8,4},{9,5},{1... | collective-permute-start | bytes 36872 | tf_op jit(solution)/shard_map/ppermute | solution.py:343
  39.0 18.6 %collective-permute-start.10 = (s32[24,128]{1,0:T(8,128)S(1)}, s32[24,128]{1,0:T(8,128)S(1)}, u32[]{:S(2)}, u32[]{:S(2)}) collective-permute-start(s32[24,128]{1,0:T(8,128)S(1)} %shard_map.56.refs_0_.o), channel_id=1, source_target_pairs={{0,30},{1,31},{2,4},{3,5},{4,2},{5,3},{6,8},{7,9},{8,6},{9,7},{10,... | collective-permute-start | bytes 36872 | tf_op jit(solution)/shard_map/ppermute | solution.py:343
  49.2 11.6 %collective-permute-start.3 = (f32[128,512]{1,0:T(8,128)S(1)}, f32[128,512]{1,0:T(8,128)S(1)}, u32[]{:S(2)}, u32[]{:S(2)}) collective-permute-start(f32[128,512]{1,0:T(8,128)S(1)} %get-tuple-element.30), channel_id=1, source_target_pairs={{0,3},{1,2},{2,1},{3,0},{4,7},{5,6},{6,5},{7,4},{8,11},{9,10},{10,... | collective-permute-start | bytes 786440 | tf_op jit(solution)/shard_map/ppermute | solution.py:343
  53.4 8.5 %collective-permute-start.4 = (f32[128,512]{1,0:T(8,128)S(1)}, f32[128,512]{1,0:T(8,128)S(1)}, u32[]{:S(2)}, u32[]{:S(2)}) collective-permute-start(f32[128,512]{1,0:T(8,128)S(1)} %get-tuple-element.30), channel_id=1, source_target_pairs={{0,30},{1,31},{2,4},{3,5},{4,2},{5,3},{6,8},{7,9},{8,6},{9,7},{10,... | collective-permute-start | bytes 786440 | tf_op jit(solution)/shard_map/ppermute | solution.py:343
  57.6 4.3 %collective-permute-start.5 = (f32[512,128]{1,0:T(8,128)S(1)}, f32[512,128]{1,0:T(8,128)S(1)}, u32[]{:S(2)}, u32[]{:S(2)}) collective-permute-start(f32[512,128]{1,0:T(8,128)S(1)} %get-tuple-element.31), channel_id=1, source_target_pairs={{0,2},{1,3},{2,0},{3,1},{4,6},{5,7},{6,4},{7,5},{8,10},{9,11},{10,... | collective-permute-start | bytes 786440 | tf_op jit(solution)/shard_map/ppermute | solution.py:343
  61.9 4.2 %copy-start.2 = (f32[128,16]{0,1:T(8,128)S(1)}, f32[128,16]{0,1:T(8,128)}, u32[]{:S(2)}) copy-start(f32[128,16]{0,1:T(8,128)} %param.9) | copy-start | bytes 24580
  62.6 1.6 %collective-permute-start.13 = (f32[512,128]{1,0:T(8,128)S(1)}, f32[512,128]{1,0:T(8,128)S(1)}, u32[]{:S(2)}, u32[]{:S(2)}) collective-permute-start(f32[512,128]{1,0:T(8,128)S(1)} %get-tuple-element.44), channel_id=1, source_target_pairs={{0,2},{1,3},{2,0},{3,1},{4,6},{5,7},{6,4},{7,5},{8,10},{9,11},{10,... | collective-permute-start | bytes 786440 | tf_op jit(solution)/shard_map/ppermute | solution.py:343
  64.5 3.7 %collective-permute-start.14 = (f32[16,128]{1,0:T(8,128)S(1)}, f32[16,128]{1,0:T(8,128)S(1)}, u32[]{:S(2)}, u32[]{:S(2)}) collective-permute-start(f32[16,128]{1,0:T(8,128)S(1)} %get-tuple-element.47), channel_id=1, source_target_pairs={{0,1},{1,0},{2,3},{3,2},{4,5},{5,4},{6,7},{7,6},{8,9},{9,8},{10,11... | collective-permute-start | bytes 24584 | tf_op jit(solution)/shard_map/ppermute | solution.py:343
  66.0 6.3 %collective-permute-start.15 = (f32[16,128]{1,0:T(8,128)S(1)}, f32[16,128]{1,0:T(8,128)S(1)}, u32[]{:S(2)}, u32[]{:S(2)}) collective-permute-start(f32[16,128]{1,0:T(8,128)S(1)} %get-tuple-element.48), channel_id=1, source_target_pairs={{28,0},{29,1},{6,2},{7,3},{0,4},{1,5},{10,6},{11,7},{4,8},{5,9},{1... | collective-permute-start | bytes 24584 | tf_op jit(solution)/shard_map/ppermute | solution.py:343

commit v3 on v2

--- a/solution.py
+++ b/solution.py
@@ -162,14 +162,21 @@
     )
 
 
-def early_kernel(o, t, o2, u, hi_ref, lo_ref, squares_ref, mine_ref, sib_ref):
-    pts = o.shape[0]
+def early_kernel(*refs):
+    *pieces, hi_ref, lo_ref, squares_ref, mine_ref, sib_ref = refs
+    pts = pieces[0].shape[0]
     norms = []
-    for i, ref in enumerate((o, t, o2, u)):
+    for i, parts in enumerate((pieces[0:2], pieces[2:3], pieces[3:5], pieces[5:7])):
         at = slice(i * pts, (i + 1) * pts)
-        hi_ref[at], lo_ref[at] = split(ref[...])
-        squares_ref[at] = squared(ref[...])
-        norms.append(lengths(squares_ref[at]))
+        start = 0
+        total = None
+        for ref in parts:
+            lanes = slice(start, start + ref.shape[1])
+            hi_ref[at, lanes], lo_ref[at, lanes] = split(ref[...])
+            total = squared(ref[...]) if total is None else total + squared(ref[...])
+            start += ref.shape[1]
+        squares_ref[at] = total
+        norms.append(lengths(total))
 
     def part(first, last):
         at = slice(first * pts, last * pts)
@@ -392,14 +399,18 @@
             ],
         )
 
-    most = half * 3 // 4
-    (o,) = cut(False, [(0, half, 8)])
+    lead = half // 4
+    most = half * 7 // 8
+    (o_lead,) = cut(False, [(0, lead, 1)])
+    (o_rest,) = cut(False, [(lead, half - lead, 4)])
     other, other_most, other_rest = cut(
-        True, [(0, half, 4), (0, most, 4), (most, half - most, 2)], (meta,)
-    )
-
-    o2 = send(o, over_same)
-    u = send(o, along_same)
+        True, [(0, half, 4), (0, most, 4), (most, half - most, 1)], (meta,)
+    )
+
+    o2_lead = send(o_lead, over_same)
+    u_lead = send(o_lead, along_same)
+    o2_rest = send(o_rest, over_same)
+    u_rest = send(o_rest, along_same)
     metas = (
         meta,
         send(meta, sibling),
@@ -431,7 +442,7 @@
             array(5 * pts),
             array(4 * pts),
         ),
-        (o, t, o2, u),
+        (o_lead, o_rest, t, o2_lead, o2_rest, u_lead, u_rest),
         flops=9 * block_flops,
         limit=24,
     )

time: 83.6 us -> 89.8 us (1.074)
  waiting for transfers between devices: 34.6 us -> 47.5 us
  starting transfers between devices: 25.6 us -> 19.5 us
  blocking collectives: 10.2 us -> 8.9 us
    ppermute x16 -> x18, waiting for transfers between devices: 34.6 us -> 47.5 us  [send(): return lax.ppermute(array, AXES, pairs)]
    ppermute x16 -> x18, starting transfers between devices: 25.6 us -> 19.5 us  [send(): return lax.ppermute(array, AXES, pairs)]
    all_to_all x1, blocking collectives: 10.2 us -> 8.9 us  [body(): totals = lax.all_to_all(total, AXES, 0, 0)]
    pallas_call x11 -> x12, Pallas kernels: 10.8 us -> 11.5 us  [call(): pl.pallas_call(kernel, out_shape=out_shape, in_specs=specs[:len(args)], s...]
  transfers between devices with their start and end apart: 16 -> 18, of which waited for: 8 -> 12; matrix products, arithmetic and copies ran while one was open for 0% -> 0% of each run, Pallas kernels for 9% -> 9%
where the time goes in v3:
time: 89.8 us; the launch traced here: 89.5 us
  waiting for transfers between devices  47.5 us (53%)
  starting transfers between devices  19.5 us (22%)
  Pallas kernels  11.5 us (13%)
  blocking collectives  8.9 us (10%)
  local copies, waits for them, and re-layouts  1.35 us (2%)
    ppermute x18, waiting for transfers between devices, send(): return lax.ppermute(array, AXES, pairs)  47.5 us
    ppermute x18, starting transfers between devices, send(): return lax.ppermute(array, AXES, pairs)  19.5 us
    pallas_call x12, Pallas kernels, call(): pl.pallas_call(kernel, out_shape=out_shape, in_specs=specs[:len(args)], s...  11.5 us
    all_to_all x1, blocking collectives, body(): totals = lax.all_to_all(total, AXES, 0, 0)  8.9 us
  transfers between devices with their start and end apart: 18, of which 12 were waited for; matrix products, arithmetic and copies ran while one was open for 0% of the time, Pallas kernels for 9%

profile of v3, /device:TPU:0, one launch (start us, length us, event | category | flops | bytes accessed | tf_op | source)
XLA Modules:
  0.0 89.5 jit_solution(9220228456403331428)
XLA Ops:
  0.7 0.7 copy-done
  1.4 0.7 copy-done.1
  2.1 1.6 %shard_map.58 = (f32[128,2048]{1,0:T(8,128)S(1)}, f32[128,1792]{1,0:T(8,128)S(1)}, f32[128,256]{1,0:T(8,128)S(1)}) custom-call(f32[128,4096]{1,0:T(8,128)} %points.5, s32[24,128]{1,0:T(8,128)S(1)} %shard_map.57.refs_0_.o), custom_call_target="tpu_custom_call" | custom-call | tf_op jit(solution)/shard_map/pallas_call | solution.py:366
  3.8 0.6 collective-permute-start
  4.4 1.0 %shard_map.55.refs_0_ = f32[128,512]{1,0:T(8,128)S(1)} custom-call(f32[128,4096]{1,0:T(8,128)} %points.5), custom_call_target="tpu_custom_call" | custom-call | tf_op jit(solution)/shard_map/pallas_call | solution.py:366
  5.3 2.5 %collective-permute-start.1 = (f32[128,512]{1,0:T(8,128)S(1)}, f32[128,512]{1,0:T(8,128)S(1)}, u32[]{:S(2)}, u32[]{:S(2)}) collective-permute-start(f32[128,512]{1,0:T(8,128)S(1)} %shard_map.55.refs_0_), channel_id=1, source_target_pairs={{0,1},{1,0},{2,3},{3,2},{4,5},{5,4},{6,7},{7,6},{8,9},{9,8},{10,11... | collective-permute-start | bytes 786440 | tf_op jit(solution)/shard_map/ppermute | solution.py:350
  7.9 4.6 %collective-permute-start.3 = (f32[128,512]{1,0:T(8,128)S(1)}, f32[128,512]{1,0:T(8,128)S(1)}, u32[]{:S(2)}, u32[]{:S(2)}) collective-permute-start(f32[128,512]{1,0:T(8,128)S(1)} %shard_map.55.refs_0_), channel_id=1, source_target_pairs={{0,28},{1,29},{2,6},{3,7},{4,0},{5,1},{6,10},{7,11},{8,4},{9,5},{1... | collective-permute-start | bytes 786440 | tf_op jit(solution)/shard_map/ppermute | solution.py:350
  12.4 1.3 %shard_map.56.refs_1_ = f32[128,1536]{1,0:T(8,128)S(1)} custom-call(f32[128,4096]{1,0:T(8,128)} %points.5), custom_call_target="tpu_custom_call" | custom-call | tf_op jit(solution)/shard_map/pallas_call | solution.py:366
  13.7 0.6 collective-permute-start.2
  14.3 0.5 collective-permute-start.4
  15.0 0.8 collective-permute-start.13
  15.8 9.7 %collective-permute-done.3.refs_5_ = f32[128,512]{1,0:T(8,128)S(1)} collective-permute-done((f32[128,512]{1,0:T(8,128)S(1)}, f32[128,512]{1,0:T(8,128)S(1)}, u32[]{:S(2)}, u32[]{:S(2)}) %collective-permute-start.3) | collective-permute-done | bytes 262176 | tf_op jit(solution)/shard_map/ppermute | solution.py:350
  25.5 8.7 %collective-permute-done.2.refs_4_ = f32[128,1536]{1,0:T(8,128)S(1)} collective-permute-done((f32[128,1536]{1,0:T(8,128)S(1)}, f32[128,1536]{1,0:T(8,128)S(1)}, u32[]{:S(2)}, u32[]{:S(2)}) %collective-permute-start.2) | collective-permute-done | bytes 786464 | tf_op jit(solution)/shard_map/ppermute | solution.py:350
  34.2 9.6 %collective-permute-done.4.refs_6_ = f32[128,1536]{1,0:T(8,128)S(1)} collective-permute-done((f32[128,1536]{1,0:T(8,128)S(1)}, f32[128,1536]{1,0:T(8,128)S(1)}, u32[]{:S(2)}, u32[]{:S(2)}) %collective-permute-start.4) | collective-permute-done | bytes 786464 | tf_op jit(solution)/shard_map/ppermute | solution.py:350
  43.7 2.3 %shard_map.59 = (bf16[512,2048]{1,0:T(8,128)(2,1)S(1)}, bf16[512,2048]{1,0:T(8,128)(2,1)S(1)}, f32[512,128]{1,0:T(8,128)S(1)}, f32[640,128]{1,0:T(8,128)S(1)}, f32[512,128]{1,0:T(8,128)S(1)}) custom-call(f32[128,512]{1,0:T(8,128)S(1)} %shard_map.55.refs_0_, f32[128,1536]{1,0:T(8,128)S(1)} %shard_map.56.refs_1_, ...), custom_call_target="tpu_custom_call" | custom-call | flops 1811939328 | tf_op jit(solution)/shard_map/pallas_call | solution.py:366
  46.1 0.5 collective-permute-start.8
  46.6 0.6 collective-permute-start.9
  48.0 3.7 %collective-permute-done.9.o2 = s32[24,128]{1,0:T(8,128)S(1)} collective-permute-done((s32[24,128]{1,0:T(8,128)S(1)}, s32[24,128]{1,0:T(8,128)S(1)}, u32[]{:S(2)}, u32[]{:S(2)}) %collective-permute-start.9) | collective-permute-done | bytes 12320 | tf_op jit(solution)/shard_map/ppermute | solution.py:350
  51.7 4.8 %collective-permute-start.11 = (s32[24,128]{1,0:T(8,128)S(1)}, s32[24,128]{1,0:T(8,128)S(1)}, u32[]{:S(2)}, u32[]{:S(2)}) collective-permute-start(s32[24,128]{1,0:T(8,128)S(1)} %shard_map.57.refs_0_.o), channel_id=1, source_target_pairs={{0,28},{1,29},{2,6},{3,7},{4,0},{5,1},{6,10},{7,11},{8,4},{9,5},{1... | collective-permute-start | bytes 36872 | tf_op jit(solution)/shard_map/ppermute | solution.py:350
  56.5 1.4 %collective-permute-done.11.u = s32[24,128]{1,0:T(8,128)S(1)} collective-permute-done((s32[24,128]{1,0:T(8,128)S(1)}, s32[24,128]{1,0:T(8,128)S(1)}, u32[]{:S(2)}, u32[]{:S(2)}) %collective-permute-start.11) | collective-permute-done | bytes 12320 | tf_op jit(solution)/shard_map/ppermute | solution.py:350
  57.9 4.4 %collective-permute-done.12.v = s32[24,128]{1,0:T(8,128)S(1)} collective-permute-done((s32[24,128]{1,0:T(8,128)S(1)}, s32[24,128]{1,0:T(8,128)S(1)}, u32[]{:S(2)}, u32[]{:S(2)}) %collective-permute-start.12) | collective-permute-done | bytes 12320 | tf_op jit(solution)/shard_map/ppermute | solution.py:350
  62.4 1.8 %collective-permute-start.6 = (f32[128,256]{1,0:T(8,128)S(1)}, f32[128,256]{1,0:T(8,128)S(1)}, u32[]{:S(2)}, u32[]{:S(2)}) collective-permute-start(f32[128,256]{1,0:T(8,128)S(1)} %get-tuple-element.30), channel_id=1, source_target_pairs={{0,30},{1,31},{2,4},{3,5},{4,2},{5,3},{6,8},{7,9},{8,6},{9,7},{10,... | collective-permute-start | bytes 393224 | tf_op jit(solution)/shard_map/ppermute | solution.py:350
  64.1 1.5 %shard_map.60 = (f32[768,128]{1,0:T(8,128)S(1)}, f32[512,128]{1,0:T(8,128)S(1)}) custom-call(s32[24,128]{1,0:T(8,128)S(1)} %shard_map.57.refs_0_.o, s32[24,128]{1,0:T(8,128)S(1)} %collective-permute-done.8.t, s32[24,128]{1,0:T(8,128)S(1)} %collective-permute-done.9.o2, s32[24,128]{1,0:T(8,128)S(1)} %collective-permute-done.10.t2, ...), custom_call_target="tpu_custom_call" | custom-call | flops 536870912 | tf_op jit(solution)/shard_map/pallas_call | solution.py:366
  65.6 2.0 %shard_map.61 = (f32[640,256]{1,0:T(8,128)S(1)}, f32[256,128]{1,0:T(8,128)S(1)}) custom-call(f32[128,1792]{1,0:T(8,128)S(1)} %collective-permute-done.13.t2, f32[128,1792]{1,0:T(8,128)S(1)} %collective-permute-done.14.v, bf16[512,2048]{1,0:T(8,128)(2,1)S(1)} %get-tuple-element.37.hi, bf16[512,2048]{1,0:T(8,128)(2,1)S(1)} %get-tuple-element.38.lo), custom_call_target="tpu_custom_call" | custom-call | flops 1610612736 | tf_op jit(solution)/shard_map/pallas_call | solution.py:366
  67.7 1.8 %collective-permute-done.6.v = f32[128,256]{1,0:T(8,128)S(1)} collective-permute-done((f32[128,256]{1,0:T(8,128)S(1)}, f32[128,256]{1,0:T(8,128)S(1)}, u32[]{:S(2)}, u32[]{:S(2)}) %collective-permute-start.6) | collective-permute-done | bytes 131104 | tf_op jit(solution)/shard_map/ppermute | solution.py:350
  69.5 0.5 shard_map.62
  70.0 1.5 %collective-permute-done.15.their_late = f32[512,128]{1,0:T(8,128)S(1)} collective-permute-done((f32[512,128]{1,0:T(8,128)S(1)}, f32[512,128]{1,0:T(8,128)S(1)}, u32[]{:S(2)}, u32[]{:S(2)}) %collective-permute-start.15) | collective-permute-done | bytes 262176 | tf_op jit(solution)/shard_map/ppermute | solution.py:350
  71.8 1.7 %collective-permute-start.16 = (f32[16,128]{1,0:T(8,128)S(1)}, f32[16,128]{1,0:T(8,128)S(1)}, u32[]{:S(2)}, u32[]{:S(2)}) collective-permute-start(f32[16,128]{1,0:T(8,128)S(1)} %get-tuple-element.47), channel_id=1, source_target_pairs={{0,1},{1,0},{2,3},{3,2},{4,5},{5,4},{6,7},{7,6},{8,9},{9,8},{10,11... | collective-permute-start | bytes 24584 | tf_op jit(solution)/shard_map/ppermute | solution.py:350
  73.8 1.8 %collective-permute-done.16.across = f32[16,128]{1,0:T(8,128)S(1)} collective-permute-done((f32[16,128]{1,0:T(8,128)S(1)}, f32[16,128]{1,0:T(8,128)S(1)}, u32[]{:S(2)}, u32[]{:S(2)}) %collective-permute-start.16) | collective-permute-done | bytes 8224 | tf_op jit(solution)/shard_map/ppermute | solution.py:350
  75.5 4.3 %collective-permute-done.17.along = f32[16,128]{1,0:T(8,128)S(1)} collective-permute-done((f32[16,128]{1,0:T(8,128)S(1)}, f32[16,128]{1,0:T(8,128)S(1)}, u32[]{:S(2)}, u32[]{:S(2)}) %collective-permute-start.17) | collective-permute-done | bytes 8224 | tf_op jit(solution)/shard_map/ppermute | solution.py:350
  79.9 8.9 %all_to_all.5.totals = f32[32,1,128]{2,1,0:T(1,128)S(1)} all-to-all(f32[32,1,128]{2,1,0:T(1,128)S(1)} %get-tuple-element.50), channel_id=1, replica_groups=mesh['blk'=16,'grp'=2] {'blk','grp'}, dimensions={0} | all-to-all | bytes 32768 | tf_op jit(solution)/shard_map/all_to_all | solution.py:491
  88.8 0.6 shard_map.66
  (23 shorter events, 2.0 us)
Async XLA Ops:
  0.7 0.7 copy-start
  1.4 0.7 copy-start.1
  3.8 40.0 %collective-permute-start = (f32[128,2048]{1,0:T(8,128)S(1)}, f32[128,2048]{1,0:T(8,128)S(1)}, u32[]{:S(2)}, u32[]{:S(2)}) collective-permute-start(f32[128,2048]{1,0:T(8,128)S(1)} %get-tuple-element.28), channel_id=1, source_target_pairs={{0,2},{1,3},{2,0},{3,1},{4,6},{5,7},{6,4},{7,5},{8,10},{9,11},{10,... | collective-permute-start | bytes 3145736 | tf_op jit(solution)/shard_map/ppermute | solution.py:350
  5.3 9.7 %collective-permute-start.1 = (f32[128,512]{1,0:T(8,128)S(1)}, f32[128,512]{1,0:T(8,128)S(1)}, u32[]{:S(2)}, u32[]{:S(2)}) collective-permute-start(f32[128,512]{1,0:T(8,128)S(1)} %shard_map.55.refs_0_), channel_id=1, source_target_pairs={{0,1},{1,0},{2,3},{3,2},{4,5},{5,4},{6,7},{7,6},{8,9},{9,8},{10,11... | collective-permute-start | bytes 786440 | tf_op jit(solution)/shard_map/ppermute | solution.py:350
  7.9 17.6 %collective-permute-start.3 = (f32[128,512]{1,0:T(8,128)S(1)}, f32[128,512]{1,0:T(8,128)S(1)}, u32[]{:S(2)}, u32[]{:S(2)}) collective-permute-start(f32[128,512]{1,0:T(8,128)S(1)} %shard_map.55.refs_0_), channel_id=1, source_target_pairs={{0,28},{1,29},{2,6},{3,7},{4,0},{5,1},{6,10},{7,11},{8,4},{9,5},{1... | collective-permute-start | bytes 786440 | tf_op jit(solution)/shard_map/ppermute | solution.py:350
  13.7 20.5 %collective-permute-start.2 = (f32[128,1536]{1,0:T(8,128)S(1)}, f32[128,1536]{1,0:T(8,128)S(1)}, u32[]{:S(2)}, u32[]{:S(2)}) collective-permute-start(f32[128,1536]{1,0:T(8,128)S(1)} %shard_map.56.refs_1_), channel_id=1, source_target_pairs={{0,1},{1,0},{2,3},{3,2},{4,5},{5,4},{6,7},{7,6},{8,9},{9,8},{10,11... | collective-permute-start | bytes 2359304 | tf_op jit(solution)/shard_map/ppermute | solution.py:350
  14.3 29.4 %collective-permute-start.4 = (f32[128,1536]{1,0:T(8,128)S(1)}, f32[128,1536]{1,0:T(8,128)S(1)}, u32[]{:S(2)}, u32[]{:S(2)}) collective-permute-start(f32[128,1536]{1,0:T(8,128)S(1)} %shard_map.56.refs_1_), channel_id=1, source_target_pairs={{0,28},{1,29},{2,6},{3,7},{4,0},{5,1},{6,10},{7,11},{8,4},{9,5},{1... | collective-permute-start | bytes 2359304 | tf_op jit(solution)/shard_map/ppermute | solution.py:350
  15.0 50.6 %collective-permute-start.13 = (f32[128,1792]{1,0:T(8,128)S(1)}, f32[128,1792]{1,0:T(8,128)S(1)}, u32[]{:S(2)}, u32[]{:S(2)}) collective-permute-start(f32[128,1792]{1,0:T(8,128)S(1)} %get-tuple-element.40), channel_id=1, source_target_pairs={{0,3},{1,2},{2,1},{3,0},{4,7},{5,6},{6,5},{7,4},{8,11},{9,10},{10,... | collective-permute-start | bytes 2752520 | tf_op jit(solution)/shard_map/ppermute | solution.py:350
  25.5 40.2 %collective-permute-start.14 = (f32[128,1792]{1,0:T(8,128)S(1)}, f32[128,1792]{1,0:T(8,128)S(1)}, u32[]{:S(2)}, u32[]{:S(2)}) collective-permute-start(f32[128,1792]{1,0:T(8,128)S(1)} %get-tuple-element.40), channel_id=1, source_target_pairs={{0,30},{1,31},{2,4},{3,5},{4,2},{5,3},{6,8},{7,9},{8,6},{9,7},{10,... | collective-permute-start | bytes 2752520 | tf_op jit(solution)/shard_map/ppermute | solution.py:350
  46.0 23.4 %collective-permute-start.7 = (f32[512,128]{1,0:T(8,128)S(1)}, f32[512,128]{1,0:T(8,128)S(1)}, u32[]{:S(2)}, u32[]{:S(2)}) collective-permute-start(f32[512,128]{1,0:T(8,128)S(1)} %get-tuple-element.31), channel_id=1, source_target_pairs={{0,2},{1,3},{2,0},{3,1},{4,6},{5,7},{6,4},{7,5},{8,10},{9,11},{10,... | collective-permute-start | bytes 786440 | tf_op jit(solution)/shard_map/ppermute | solution.py:350
  46.1 1.5 %collective-permute-start.8 = (s32[24,128]{1,0:T(8,128)S(1)}, s32[24,128]{1,0:T(8,128)S(1)}, u32[]{:S(2)}, u32[]{:S(2)}) collective-permute-start(s32[24,128]{1,0:T(8,128)S(1)} %shard_map.57.refs_0_.o), channel_id=1, source_target_pairs={{0,2},{1,3},{2,0},{3,1},{4,6},{5,7},{6,4},{7,5},{8,10},{9,11},{10,... | collective-permute-start | bytes 36872 | tf_op jit(solution)/shard_map/ppermute | solution.py:350
  46.6 5.1 %collective-permute-start.9 = (s32[24,128]{1,0:T(8,128)S(1)}, s32[24,128]{1,0:T(8,128)S(1)}, u32[]{:S(2)}, u32[]{:S(2)}) collective-permute-start(s32[24,128]{1,0:T(8,128)S(1)} %shard_map.57.refs_0_.o), channel_id=1, source_target_pairs={{0,1},{1,0},{2,3},{3,2},{4,5},{5,4},{6,7},{7,6},{8,9},{9,8},{10,11... | collective-permute-start | bytes 36872 | tf_op jit(solution)/shard_map/ppermute | solution.py:350
  47.6 8.9 %collective-permute-start.10 = (s32[24,128]{1,0:T(8,128)S(1)}, s32[24,128]{1,0:T(8,128)S(1)}, u32[]{:S(2)}, u32[]{:S(2)}) collective-permute-start(s32[24,128]{1,0:T(8,128)S(1)} %shard_map.57.refs_0_.o), channel_id=1, source_target_pairs={{0,3},{1,2},{2,1},{3,0},{4,7},{5,6},{6,5},{7,4},{8,11},{9,10},{10,... | collective-permute-start | bytes 36872 | tf_op jit(solution)/shard_map/ppermute | solution.py:350
  51.7 6.2 %collective-permute-start.11 = (s32[24,128]{1,0:T(8,128)S(1)}, s32[24,128]{1,0:T(8,128)S(1)}, u32[]{:S(2)}, u32[]{:S(2)}) collective-permute-start(s32[24,128]{1,0:T(8,128)S(1)} %shard_map.57.refs_0_.o), channel_id=1, source_target_pairs={{0,28},{1,29},{2,6},{3,7},{4,0},{5,1},{6,10},{7,11},{8,4},{9,5},{1... | collective-permute-start | bytes 36872 | tf_op jit(solution)/shard_map/ppermute | solution.py:350
  56.5 5.8 %collective-permute-start.12 = (s32[24,128]{1,0:T(8,128)S(1)}, s32[24,128]{1,0:T(8,128)S(1)}, u32[]{:S(2)}, u32[]{:S(2)}) collective-permute-start(s32[24,128]{1,0:T(8,128)S(1)} %shard_map.57.refs_0_.o), channel_id=1, source_target_pairs={{0,30},{1,31},{2,4},{3,5},{4,2},{5,3},{6,8},{7,9},{8,6},{9,7},{10,... | collective-permute-start | bytes 36872 | tf_op jit(solution)/shard_map/ppermute | solution.py:350
  57.9 9.7 %collective-permute-start.5 = (f32[128,256]{1,0:T(8,128)S(1)}, f32[128,256]{1,0:T(8,128)S(1)}, u32[]{:S(2)}, u32[]{:S(2)}) collective-permute-start(f32[128,256]{1,0:T(8,128)S(1)} %get-tuple-element.30), channel_id=1, source_target_pairs={{0,3},{1,2},{2,1},{3,0},{4,7},{5,6},{6,5},{7,4},{8,11},{9,10},{10,... | collective-permute-start | bytes 393224 | tf_op jit(solution)/shard_map/ppermute | solution.py:350
  62.4 7.1 %collective-permute-start.6 = (f32[128,256]{1,0:T(8,128)S(1)}, f32[128,256]{1,0:T(8,128)S(1)}, u32[]{:S(2)}, u32[]{:S(2)}) collective-permute-start(f32[128,256]{1,0:T(8,128)S(1)} %get-tuple-element.30), channel_id=1, source_target_pairs={{0,30},{1,31},{2,4},{3,5},{4,2},{5,3},{6,8},{7,9},{8,6},{9,7},{10,... | collective-permute-start | bytes 393224 | tf_op jit(solution)/shard_map/ppermute | solution.py:350
  69.5 4.0 %copy-start.2 = (f32[128,16]{0,1:T(8,128)S(1)}, f32[128,16]{0,1:T(8,128)}, u32[]{:S(2)}) copy-start(f32[128,16]{0,1:T(8,128)} %param.9) | copy-start | bytes 24580
  70.0 1.6 %collective-permute-start.15 = (f32[512,128]{1,0:T(8,128)S(1)}, f32[512,128]{1,0:T(8,128)S(1)}, u32[]{:S(2)}, u32[]{:S(2)}) collective-permute-start(f32[512,128]{1,0:T(8,128)S(1)} %get-tuple-element.44), channel_id=1, source_target_pairs={{0,2},{1,3},{2,0},{3,1},{4,6},{5,7},{6,4},{7,5},{8,10},{9,11},{10,... | collective-permute-start | bytes 786440 | tf_op jit(solution)/shard_map/ppermute | solution.py:350
  71.8 3.7 %collective-permute-start.16 = (f32[16,128]{1,0:T(8,128)S(1)}, f32[16,128]{1,0:T(8,128)S(1)}, u32[]{:S(2)}, u32[]{:S(2)}) collective-permute-start(f32[16,128]{1,0:T(8,128)S(1)} %get-tuple-element.47), channel_id=1, source_target_pairs={{0,1},{1,0},{2,3},{3,2},{4,5},{5,4},{6,7},{7,6},{8,9},{9,8},{10,11... | collective-permute-start | bytes 24584 | tf_op jit(solution)/shard_map/ppermute | solution.py:350
  73.5 6.3 %collective-permute-start.17 = (f32[16,128]{1,0:T(8,128)S(1)}, f32[16,128]{1,0:T(8,128)S(1)}, u32[]{:S(2)}, u32[]{:S(2)}) collective-permute-start(f32[16,128]{1,0:T(8,128)S(1)} %get-tuple-element.48), channel_id=1, source_target_pairs={{28,0},{29,1},{6,2},{7,3},{0,4},{1,5},{10,6},{11,7},{4,8},{5,9},{1... | collective-permute-start | bytes 24584 | tf_op jit(solution)/shard_map/ppermute | solution.py:350

commit v4 on v2

v4 whole, which is shorter than its diff:
```python
import functools

import jax
import jax.numpy as jnp
from jax import lax
from jax.experimental import pallas as pl
from jax.experimental.pallas import tpu as pltpu
from jax.sharding import PartitionSpec as P


AXES = ("blk", "grp")
LANES = 128
SUBLANES = 8
NT = (((1,), (1,)), ((), ()))
FAR = 1e30
NEVER = -3e38


def exchange(tiles, i, j):
    low, high = jnp.minimum(tiles[i], tiles[j]), jnp.maximum(tiles[i], tiles[j])
    tiles[i], tiles[j] = low, high


def sort_tiles(tiles):
    tiles = list(tiles)
    n = len(tiles)
    p = 1
    while p < n:
        k = p
        while k >= 1:
            for j in range(k % p, n - k, 2 * k):
                for i in range(min(k, n - j - k)):
                    if (i + j) // (2 * p) == (i + j + k) // (2 * p):
                        exchange(tiles, i + j, i + j + k)
            k //= 2
        p *= 2
    return tiles


def bitonic(tiles):
    tiles = list(tiles)
    step = len(tiles) // 2
    while step >= 1:
        for i in range(len(tiles)):
            if not i & step:
                exchange(tiles, i, i + step)
        step //= 2
    return tiles


def merge_lowest(a, b, keep):
    if len(a) + len(b) <= keep:
        return bitonic(a + b[::-1])
    return bitonic([jnp.minimum(x, y) for x, y in zip(a, b[::-1])])


def lowest(tiles, keep):
    group = 1
    while group * 2 <= min(keep, len(tiles)):
        group *= 2
    while len(tiles) % group:
        tiles = tiles + [jnp.full((SUBLANES, LANES), FAR, jnp.float32)]
    lists = [sort_tiles(tiles[i : i + group]) for i in range(0, len(tiles), group)]
    while len(lists) > 1:
        paired = [
            merge_lowest(lists[i], lists[i + 1], keep)
            for i in range(0, len(lists) - 1, 2)
        ]
        if len(lists) % 2:
            rest = lists[-1]
            while len(rest) < len(paired[0]):
                rest = rest + [jnp.full((SUBLANES, LANES), FAR, jnp.float32)]
            paired.append(rest)
        lists = paired
    found = lists[0]
    shift = SUBLANES // 2
    while shift:
        found = merge_lowest(found, [pltpu.roll(t, shift, 0) for t in found], keep)
        shift //= 2
    return found


def tiles_of(array):
    return [array[i : i + SUBLANES] for i in range(0, array.shape[0], SUBLANES)]


def describe_kernel(count_ref, index_ref, lists_ref, meta_ref):
    listed, pts = lists_ref.shape
    slots = index_ref.shape[1]
    meta_ref[0:listed] = lists_ref[...]
    spread = jnp.broadcast_to(index_ref[...].astype(jnp.float32), (pts, slots)).T
    slot = lax.broadcasted_iota(jnp.int32, (slots, pts), 0)
    row = lax.broadcasted_iota(jnp.int32, (slots, pts), 1)
    hit = (spread.astype(jnp.int32) == row) & (slot < count_ref[0])
    live = jnp.max(jnp.where(hit, 1.0, 0.0), axis=0, keepdims=True)
    meta_ref[listed : listed + SUBLANES] = jnp.broadcast_to(
        live.astype(jnp.int32), (SUBLANES, pts)
    )


def mask_kernel(
    listed, cycle, members, o, t, o2, t2, u, v, own_ref, far_ref
):
    blk, grp = lax.axis_index("blk"), lax.axis_index("grp")
    turned = lax.rem(blk, 2)
    steps = (0, 1 - 2 * turned, 0, 1 - 2 * turned, 2 - 4 * turned, 2 * turned - 1)
    sides = (grp, grp, 1 - grp, 1 - grp, grp, grp)
    base = [
        lax.rem(blk + step + cycle, cycle) * members + side
        for step, side in zip(steps, sides)
    ]
    metas = (o, t, o2, t2, u, v)
    pts = o.shape[1]
    alive = [
        jnp.broadcast_to(m[listed : listed + 1].astype(jnp.float32), (pts, pts)).T > 0.5
        for m in metas
    ]
    row = lax.broadcasted_iota(jnp.int32, (pts, pts), 0)
    lane = lax.broadcasted_iota(jnp.int32, (pts, pts), 1)

    def floor(target, cand):
        ids = row + base[cand] * pts
        lists = metas[target]
        bad = jnp.logical_not(alive[cand])
        for k in range(listed):
            bad = bad | (ids == lists[k : k + 1])
        if target == cand:
            bad = bad | (row == lane)
        return jnp.where(bad, FAR, NEVER)

    for i in range(6):
        own_ref[i * pts : (i + 1) * pts] = floor(0, i)
    for i, (target, cand) in enumerate(((2, 4), (2, 5), (4, 0), (4, 2))):
        far_ref[i * pts : (i + 1) * pts] = floor(target, cand)


def split(x):
    high = x.astype(jnp.bfloat16)
    return high, (x - high.astype(jnp.float32)).astype(jnp.bfloat16)


def squared(x):
    total = x[:, :LANES] * x[:, :LANES]
    for j in range(LANES, x.shape[1], LANES):
        total = total + x[:, j : j + LANES] * x[:, j : j + LANES]
    return total


def product(rows, columns):
    def dot(a, b):
        return lax.dot_general(a, b, NT, preferred_element_type=jnp.float32)

    return (
        dot(rows[0], columns[1]) + dot(rows[1], columns[0]) + dot(rows[0], columns[0])
    )


def lengths(total):
    return (
        jnp.sum(total, axis=1, keepdims=True),
        jnp.sum(total.T, axis=0, keepdims=True),
    )


def add(before, values):
    return [value + ref for value, ref in zip(values, before)] if before else values


def home_kernel(*refs):
    *own, beside, dist_ref, squares_ref = refs
    pts = own[0].shape[0]
    total, squares, start = None, None, 0
    for ref in own:
        lanes = slice(start, start + ref.shape[1])
        start += ref.shape[1]
        here, there = split(ref[...]), split(beside[:, lanes])
        rows = tuple(jnp.concatenate(pair, axis=0) for pair in zip(here, there))
        part = product(rows, here)
        more = [squared(ref[...]), squared(beside[:, lanes])]
        total = part if total is None else total + part
        squares = add(squares, more)
    across = lengths(squares[0])[1]
    for i, sums in enumerate(squares):
        at = slice(i * pts, (i + 1) * pts)
        dist_ref[at] = lengths(sums)[0] + across - 2.0 * total[at]
    squares_ref[...] = squares[0]


def direct_products(o, o2, u, before, hi_ref, lo_ref):
    pts = o.shape[0]
    for i, ref in enumerate((o, o2)):
        at = slice(i * pts, (i + 1) * pts)
        hi_ref[at], lo_ref[at] = split(ref[...])
    ahead = split(u[...])
    rows = [
        jnp.concatenate([ref[pts : 2 * pts], part], axis=0)
        for ref, part in zip((hi_ref, lo_ref), ahead)
    ]
    total = product(rows, (hi_ref[...], lo_ref[...]))
    squares = jnp.concatenate([squared(o2[...]), squared(u[...])], axis=0)
    return add([ref[...] for ref in before], [total, squares])


def passed_products(t2, v, hi, lo, before):
    parts = zip(split(t2[...]), split(v[...]))
    rows = [jnp.concatenate(pair, axis=0) for pair in parts]
    total = product(rows, (hi[...], lo[...]))
    squares = jnp.concatenate([squared(t2[...]), squared(v[...])], axis=0)
    return add([ref[...] for ref in before], [total, squares])


def direct_kernel(o, o2, u, *refs):
    *before, hi_ref, lo_ref, total_ref, squares_ref = refs
    total_ref[...], squares_ref[...] = direct_products(
        o, o2, u, before, hi_ref, lo_ref
    )


def passed_kernel(t2, v, hi, lo, *refs):
    *before, total_ref, squares_ref = refs
    total_ref[...], squares_ref[...] = passed_products(t2, v, hi, lo, before)


def store_lowest(ref, blocks, scale, keep):
    tiles = []
    for block, floor in blocks:
        tiles += tiles_of(jnp.maximum(block * scale, floor))
    for i, tile in enumerate(lowest(tiles, keep)):
        ref[i : i + 1] = tile[0:1]


def last_direct_kernel(scale, keep, o, o2, u, own_squares, floors, *refs):
    *before, hi_ref, lo_ref, squares_ref, dist_ref, along_ref = refs
    pts = o.shape[0]
    total, squares = direct_products(o, o2, u, before, hi_ref, lo_ref)
    squares_ref[...] = squares
    of_o = lengths(own_squares[...])
    of_o2, of_u = lengths(squares[:pts]), lengths(squares[pts:])
    crossed = of_o2[0] + of_o[1] - 2.0 * total[:pts, :pts]
    near = of_u[0] + of_o[1] - 2.0 * total[pts:, :pts]
    far = of_u[0] + of_o2[1] - 2.0 * total[pts:, pts:]
    for i, block in enumerate((crossed, near, far)):
        dist_ref[i * pts : (i + 1) * pts] = block
    pairs = ((near.T, floors[2 * pts : 3 * pts]), (far.T, floors[3 * pts : 4 * pts]))
    store_lowest(along_ref, pairs, scale, keep)


def last_passed_kernel(
    scale, keep, t2, v, hi, lo, own_squares, squares, dist, floors, *refs
):
    *before, dist_ref, across_ref = refs
    pts = t2.shape[0]
    total, passed = passed_products(t2, v, hi, lo, before)
    of_o = lengths(own_squares[...])
    of_o2 = lengths(squares[0:pts])
    of_t2, of_v = lengths(passed[:pts]), lengths(passed[pts:])
    dist_ref[0:pts] = of_t2[0] + of_o[1] - 2.0 * total[:pts, :pts]
    dist_ref[pts : 2 * pts] = of_v[0] + of_o[1] - 2.0 * total[pts:, :pts]
    far = of_v[0] + of_o2[1] - 2.0 * total[pts:, pts:]
    pairs = ((dist[2 * pts : 3 * pts], floors[0:pts]), (far, floors[pts : 2 * pts]))
    store_lowest(across_ref, pairs, scale, keep)


def own_kernel(scale, keep, home, direct, passed, floors, old, found_ref):
    pts = floors.shape[1]
    order = (home, 0), (home, 1), (direct, 0), (passed, 0), (direct, 1), (passed, 1)
    pairs = [
        (ref[at * pts : (at + 1) * pts], floors[i * pts : (i + 1) * pts])
        for i, (ref, at) in enumerate(order)
    ]
    store_lowest(found_ref, pairs, scale, keep)
    found_ref[keep : 2 * keep] = old[...]


def finish_kernel(keep, found, across, along, best_ref, total_ref):
    tiles = tiles_of(found[...]) + tiles_of(across[...]) + tiles_of(along[...])
    ranked = lowest(tiles, keep)
    total = jnp.sum(ranked[keep - 1][0:1], axis=1, keepdims=True)
    total_ref[...] = jnp.broadcast_to(total[None], total_ref.shape)
    for i, tile in enumerate(ranked):
        best_ref[i : i + 1] = tile[0:1]


def scale_kernel(points_in_all, best, totals, out_ref):
    total = jnp.sum(totals[:, 0, :], axis=0, keepdims=True)
    out_ref[...] = best[...] / (total * (1.0 / points_in_all))


def cut_kernel(spans, points, *refs):
    *outs, done = refs[-1 - len(spans) :]
    copies = [
        pltpu.make_async_copy(points.at[:, pl.ds(start, width)], out, done.at[i])
        for i, ((start, width), out) in enumerate(zip(spans, outs))
    ]
    for copy in copies:
        copy.start()
    for copy in copies:
        copy.wait()


CUTS = (0, 2, 8, 13, 15, 16)


def body(points, cand_index, cand_count, neighbor_ids, old_dist):
    pts, width = points.shape
    keep = old_dist.shape[1]
    cycle = lax.axis_size("blk")
    members = lax.axis_size("grp")
    f32 = jnp.float32

    def links(move):
        return [
            (b * members + g, (move(b, g)[0] % cycle) * members + move(b, g)[1])
            for b in range(cycle)
            for g in range(members)
        ]

    sibling = links(lambda b, g: (b ^ 1, g))
    over_same = links(lambda b, g: (b, 1 - g))
    over_cross = links(lambda b, g: (b ^ 1, 1 - g))
    along_same = links(lambda b, g: (b + (2 if b % 2 else -2), g))
    along_cross = links(lambda b, g: (b + (1 if b % 2 else -1), g))
    along_back = [(b, a) for a, b in along_same]

    def labelled(value, pairs):
        return lax.ppermute(value, AXES, pairs)

    whole_array = pl.BlockSpec(memory_space=pltpu.VMEM)
    scalars = pl.BlockSpec(memory_space=pltpu.SMEM)

    def call(
        kernel,
        out_shape,
        args,
        flops=0,
        first=whole_array,
        second=whole_array,
        scratch=(),
        limit=4,
    ):
        specs = [first, second] + [whole_array] * len(args)
        return pl.pallas_call(
            kernel,
            out_shape=out_shape,
            in_specs=specs[: len(args)],
            scratch_shapes=scratch,
            out_specs=jax.tree.map(lambda _: whole_array, out_shape),
            cost_estimate=pl.CostEstimate(
                flops=flops, bytes_accessed=0, transcendentals=0
            ),
            compiler_params=pltpu.CompilerParams(vmem_limit_bytes=limit << 20),
        )(*args)

    def array(rows, lanes=pts, dtype=f32):
        return jax.ShapeDtypeStruct((rows, lanes), dtype)

    def cut(pieces, after=()):
        return call(
            functools.partial(cut_kernel, pieces),
            [pltpu.VMEM((pts, wide), f32) for _, wide in pieces],
            (pltpu.with_memory_space_constraint(points, pltpu.HBM),) + after,
            first=pl.BlockSpec(memory_space=pltpu.HBM),
            scratch=[pltpu.SemaphoreType.DMA((len(pieces),))],
        )

    meta = call(
        describe_kernel,
        array(keep + SUBLANES, dtype=jnp.int32),
        (cand_count, cand_index, neighbor_ids.T),
        first=scalars,
    )
    cuts = [width * c // CUTS[-1] for c in CUTS]
    spans = [(a, b - a) for a, b in zip(cuts, cuts[1:])]
    o = cut(spans[:1])
    o += cut(spans[1:2])
    o += cut(spans[2:], (meta,))
    metas = (
        meta,
        labelled(meta, sibling),
        labelled(meta, over_same),
        labelled(meta, over_cross),
        labelled(meta, along_same),
        labelled(meta, along_cross),
    )
    u = [labelled(piece, along_same) for piece in o]
    o2 = [labelled(piece, over_same) for piece in o]
    t = labelled(points, sibling)
    t2 = [labelled(piece, sibling) for piece in o2]
    v = [labelled(piece, sibling) for piece in u]

    own_floor, far_floor = call(
        functools.partial(mask_kernel, keep, cycle, members),
        (array(6 * pts), array(4 * pts)),
        metas,
        flops=1 << 29,
    )
    block_flops = 6 * pts * pts * width
    home, own_squares = call(
        home_kernel,
        (array(2 * pts), array(pts, LANES)),
        (*o, t),
        flops=2 * block_flops,
        limit=24,
    )

    scale = 1.0 / width
    final = len(spans) - 1
    direct, passed = (), ()
    for i, (_, wide) in enumerate(spans):
        parts = (array(2 * pts, wide, jnp.bfloat16),) * 2
        sums = (array(2 * pts, 2 * pts), array(2 * pts, LANES))
        flops = 4 * block_flops * wide // width
        if i < final:
            hi, lo, *direct = call(
                direct_kernel,
                parts + sums,
                (o[i], o2[i], u[i], *direct),
                flops=flops,
                limit=16,
            )
            passed = call(
                passed_kernel,
                sums,
                (t2[i], v[i], hi, lo, *passed),
                flops=flops,
                limit=16,
            )
    ready = (o2[final], u[final], own_squares, own_floor, far_floor)
    o2_last, u_last, own_squares, own_floor, far_floor = lax.optimization_barrier(ready)
    hi, lo, squares, direct_dist, along = call(
        functools.partial(last_direct_kernel, scale, keep),
        parts + (array(2 * pts, LANES), array(3 * pts), array(keep)),
        (o[final], o2_last, u_last, own_squares, far_floor, *direct),
        flops=flops,
        limit=16,
    )
    along = labelled(along, along_back)
    passed_dist, across = call(
        functools.partial(last_passed_kernel, scale, keep),
        (array(2 * pts), array(keep)),
        (t2[final], v[final], hi, lo)
        + (own_squares, squares, direct_dist, far_floor, *passed),
        flops=flops,
        limit=16,
    )
    across = labelled(across, over_same)
    found = call(
        functools.partial(own_kernel, scale, keep),
        array(2 * keep),
        (home, direct_dist, passed_dist, own_floor, old_dist.T),
        flops=1 << 29,
    )
    devices = cycle * members
    best, total = call(
        functools.partial(finish_kernel, keep),
        (array(keep), jax.ShapeDtypeStruct((devices, 1, LANES), f32)),
        (found, across, along),
        flops=1 << 26,
    )
    totals = lax.all_to_all(total, AXES, 0, 0)
    scaled = call(
        functools.partial(scale_kernel, pts * devices), array(keep), (best, totals)
    )
    return scaled.T


def solution(mesh):
    return jax.shard_map(
        body,
        mesh=mesh,
        in_specs=(
            P(AXES, None),
            P(AXES, None),
            P(AXES),
            P(AXES, None),
            P(AXES, None),
        ),
        out_specs=P(AXES, None),
        check_vma=False,
    )
```

time: 83.6 us -> 95.9 us (1.15)
  waiting for transfers between devices: 34.6 us -> 48.4 us
  Pallas kernels: 10.8 us -> 13.7 us
  starting transfers between devices: 25.6 us -> 23.7 us
  local copies, waits for them, and re-layouts: 1.35 us -> 0.02 us
  blocking collectives: 10.2 us -> 8.9 us
    ppermute x16 -> x28, waiting for transfers between devices: 34.6 us -> 48.4 us  [labelled(): return lax.ppermute(value, AXES, pairs)]
    pallas_call x11 -> x19, Pallas kernels: 10.8 us -> 13.7 us  [call(): pl.pallas_call(kernel, out_shape=out_shape, in_specs=specs[:len(args)], s...]
    ppermute x16 -> x28, starting transfers between devices: 25.6 us -> 23.7 us  [labelled(): return lax.ppermute(value, AXES, pairs)]
    unnamed x6 -> x8, local copies, waits for them, and re-layouts: 1.35 us -> 0.02 us
    all_to_all x1, blocking collectives: 10.2 us -> 8.9 us  [body(): totals = lax.all_to_all(total, AXES, 0, 0)]
  transfers between devices with their start and end apart: 16 -> 28, of which waited for: 8 -> 14; matrix products, arithmetic and copies ran while one was open for 0% -> 0% of each run, Pallas kernels for 9% -> 12%
where the time goes in v4:
time: 95.9 us; the launch traced here: 95.7 us
  waiting for transfers between devices  48.4 us (50%)
  starting transfers between devices  23.7 us (25%)
  Pallas kernels  13.7 us (14%)
  blocking collectives  8.9 us (9%)
    ppermute x28, waiting for transfers between devices, labelled(): return lax.ppermute(value, AXES, pairs)  48.4 us
    ppermute x28, starting transfers between devices, labelled(): return lax.ppermute(value, AXES, pairs)  23.7 us
    pallas_call x19, Pallas kernels, call(): pl.pallas_call(kernel, out_shape=out_shape, in_specs=specs[:len(args)], s...  13.7 us
    all_to_all x1, blocking collectives, body(): totals = lax.all_to_all(total, AXES, 0, 0)  8.9 us
  transfers between devices with their start and end apart: 28, of which 14 were waited for; matrix products, arithmetic and copies ran while one was open for 0% of the time, Pallas kernels for 12%

profile of v4, /device:TPU:0, one launch (start us, length us, event | category | flops | bytes accessed | tf_op | source)
XLA Modules:
  0.0 95.7 jit_solution(3873530702813249410)
XLA Ops:
  0.0 1.1 %shard_map.55.refs_0_.o = f32[128,512]{1,0:T(8,128)S(1)} custom-call(f32[128,4096]{1,0:T(8,128)} %points.5), custom_call_target="tpu_custom_call" | custom-call | tf_op jit(solution)/shard_map/pallas_call | solution.py:342
  1.1 3.0 %collective-permute-start.14 = (f32[128,512]{1,0:T(8,128)S(1)}, f32[128,512]{1,0:T(8,128)S(1)}, u32[]{:S(2)}, u32[]{:S(2)}) collective-permute-start(f32[128,512]{1,0:T(8,128)S(1)} %shard_map.55.refs_0_.o), channel_id=1, source_target_pairs={{0,1},{1,0},{2,3},{3,2},{4,5},{5,4},{6,7},{7,6},{8,9},{9,8},{10,11... | collective-permute-start | bytes 786440 | tf_op jit(solution)/shard_map/ppermute | solution.py:326
  4.2 4.6 %collective-permute-start.15 = (f32[128,512]{1,0:T(8,128)S(1)}, f32[128,512]{1,0:T(8,128)S(1)}, u32[]{:S(2)}, u32[]{:S(2)}) collective-permute-start(f32[128,512]{1,0:T(8,128)S(1)} %shard_map.55.refs_0_.o), channel_id=1, source_target_pairs={{0,28},{1,29},{2,6},{3,7},{4,0},{5,1},{6,10},{7,11},{8,4},{9,5},{1... | collective-permute-start | bytes 786440 | tf_op jit(solution)/shard_map/ppermute | solution.py:326
  10.6 2.3 %collective-permute-done.3.t = s32[24,128]{1,0:T(8,128)S(1)} collective-permute-done((s32[24,128]{1,0:T(8,128)S(1)}, s32[24,128]{1,0:T(8,128)S(1)}, u32[]{:S(2)}, u32[]{:S(2)}) %collective-permute-start.3) | collective-permute-done | bytes 12320 | tf_op jit(solution)/shard_map/ppermute | solution.py:326
  13.8 1.8 %collective-permute-start.6 = (s32[24,128]{1,0:T(8,128)S(1)}, s32[24,128]{1,0:T(8,128)S(1)}, u32[]{:S(2)}, u32[]{:S(2)}) collective-permute-start(s32[24,128]{1,0:T(8,128)S(1)} %shard_map.57.refs_0_.o), channel_id=1, source_target_pairs={{0,28},{1,29},{2,6},{3,7},{4,0},{5,1},{6,10},{7,11},{8,4},{9,5},{1... | collective-permute-start | bytes 36872 | tf_op jit(solution)/shard_map/ppermute | solution.py:326
  16.0 1.6 %collective-permute-start.7 = (s32[24,128]{1,0:T(8,128)S(1)}, s32[24,128]{1,0:T(8,128)S(1)}, u32[]{:S(2)}, u32[]{:S(2)}) collective-permute-start(s32[24,128]{1,0:T(8,128)S(1)} %shard_map.57.refs_0_.o), channel_id=1, source_target_pairs={{0,30},{1,31},{2,4},{3,5},{4,2},{5,3},{6,8},{7,9},{8,6},{9,7},{10,... | collective-permute-start | bytes 36872 | tf_op jit(solution)/shard_map/ppermute | solution.py:326
  17.6 1.2 %shard_map.58 = (f32[128,1280]{1,0:T(8,128)S(1)}, f32[128,512]{1,0:T(8,128)S(1)}, f32[128,256]{1,0:T(8,128)S(1)}) custom-call(f32[128,4096]{1,0:T(8,128)} %points.5, s32[24,128]{1,0:T(8,128)S(1)} %shard_map.57.refs_0_.o), custom_call_target="tpu_custom_call" | custom-call | tf_op jit(solution)/shard_map/pallas_call | solution.py:342
  18.8 1.6 %collective-permute-start.1 = (f32[128,256]{1,0:T(8,128)S(1)}, f32[128,256]{1,0:T(8,128)S(1)}, u32[]{:S(2)}, u32[]{:S(2)}) collective-permute-start(f32[128,256]{1,0:T(8,128)S(1)} %get-tuple-element.52.refs_4_.o), channel_id=1, source_target_pairs={{0,1},{1,0},{2,3},{3,2},{4,5},{5,4},{6,7},{7,6},{8,9},{9,8},{10,11... | collective-permute-start | bytes 393224 | tf_op jit(solution)/shard_map/ppermute | solution.py:326
  20.4 1.5 %collective-permute-done.7.v = s32[24,128]{1,0:T(8,128)S(1)} collective-permute-done((s32[24,128]{1,0:T(8,128)S(1)}, s32[24,128]{1,0:T(8,128)S(1)}, u32[]{:S(2)}, u32[]{:S(2)}) %collective-permute-start.7) | collective-permute-done | bytes 12320 | tf_op jit(solution)/shard_map/ppermute | solution.py:326
  21.8 1.7 %collective-permute-start.2 = (f32[128,256]{1,0:T(8,128)S(1)}, f32[128,256]{1,0:T(8,128)S(1)}, u32[]{:S(2)}, u32[]{:S(2)}) collective-permute-start(f32[128,256]{1,0:T(8,128)S(1)} %get-tuple-element.52.refs_4_.o), channel_id=1, source_target_pairs={{0,28},{1,29},{2,6},{3,7},{4,0},{5,1},{6,10},{7,11},{8,4},{9,5},{1... | collective-permute-start | bytes 393224 | tf_op jit(solution)/shard_map/ppermute | solution.py:326
  23.5 0.7 collective-permute-done.1.o2
  24.2 1.5 %collective-permute-start.8 = (f32[128,512]{1,0:T(8,128)S(1)}, f32[128,512]{1,0:T(8,128)S(1)}, u32[]{:S(2)}, u32[]{:S(2)}) collective-permute-start(f32[128,512]{1,0:T(8,128)S(1)} %get-tuple-element.51.refs_3_.o), channel_id=1, source_target_pairs={{0,1},{1,0},{2,3},{3,2},{4,5},{5,4},{6,7},{7,6},{8,9},{9,8},{10,11... | collective-permute-start | bytes 786440 | tf_op jit(solution)/shard_map/ppermute | solution.py:326
  25.7 2.4 %collective-permute-done.2.u = f32[128,256]{1,0:T(8,128)S(1)} collective-permute-done((f32[128,256]{1,0:T(8,128)S(1)}, f32[128,256]{1,0:T(8,128)S(1)}, u32[]{:S(2)}, u32[]{:S(2)}) %collective-permute-start.2) | collective-permute-done | bytes 131104 | tf_op jit(solution)/shard_map/ppermute | solution.py:326
  28.1 3.2 %collective-permute-start.9 = (f32[128,512]{1,0:T(8,128)S(1)}, f32[128,512]{1,0:T(8,128)S(1)}, u32[]{:S(2)}, u32[]{:S(2)}) collective-permute-start(f32[128,512]{1,0:T(8,128)S(1)} %get-tuple-element.51.refs_3_.o), channel_id=1, source_target_pairs={{0,28},{1,29},{2,6},{3,7},{4,0},{5,1},{6,10},{7,11},{8,4},{9,5},{1... | collective-permute-start | bytes 786440 | tf_op jit(solution)/shard_map/ppermute | solution.py:326
  31.3 1.1 %shard_map.56.refs_1_.o = f32[128,1536]{1,0:T(8,128)S(1)} custom-call(f32[128,4096]{1,0:T(8,128)} %points.5), custom_call_target="tpu_custom_call" | custom-call | tf_op jit(solution)/shard_map/pallas_call | solution.py:342
  32.9 12.8 %collective-permute-done.9.u = f32[128,512]{1,0:T(8,128)S(1)} collective-permute-done((f32[128,512]{1,0:T(8,128)S(1)}, f32[128,512]{1,0:T(8,128)S(1)}, u32[]{:S(2)}, u32[]{:S(2)}) %collective-permute-start.9) | collective-permute-done | bytes 262176 | tf_op jit(solution)/shard_map/ppermute | solution.py:326
  45.7 0.9 collective-permute-start.10
  46.6 0.7 collective-permute-done.25.v
  47.3 1.1 %collective-permute-done.12.o2 = f32[128,1536]{1,0:T(8,128)S(1)} collective-permute-done((f32[128,1536]{1,0:T(8,128)S(1)}, f32[128,1536]{1,0:T(8,128)S(1)}, u32[]{:S(2)}, u32[]{:S(2)}) %collective-permute-start.12) | collective-permute-done | bytes 786464 | tf_op jit(solution)/shard_map/ppermute | solution.py:326
  48.3 12.9 %collective-permute-done.13.u = f32[128,1536]{1,0:T(8,128)S(1)} collective-permute-done((f32[128,1536]{1,0:T(8,128)S(1)}, f32[128,1536]{1,0:T(8,128)S(1)}, u32[]{:S(2)}, u32[]{:S(2)}) %collective-permute-start.13) | collective-permute-done | bytes 786464 | tf_op jit(solution)/shard_map/ppermute | solution.py:326
  61.2 1.7 %collective-permute-done.10.o2 = f32[128,1280]{1,0:T(8,128)S(1)} collective-permute-done((f32[128,1280]{1,0:T(8,128)S(1)}, f32[128,1280]{1,0:T(8,128)S(1)}, u32[]{:S(2)}, u32[]{:S(2)}) %collective-permute-start.10) | collective-permute-done | bytes 655392 | tf_op jit(solution)/shard_map/ppermute | solution.py:326
  62.9 5.3 %collective-permute-done.11.u = f32[128,1280]{1,0:T(8,128)S(1)} collective-permute-done((f32[128,1280]{1,0:T(8,128)S(1)}, f32[128,1280]{1,0:T(8,128)S(1)}, u32[]{:S(2)}, u32[]{:S(2)}) %collective-permute-start.11) | collective-permute-done | bytes 655392 | tf_op jit(solution)/shard_map/ppermute | solution.py:326
  68.2 1.5 %shard_map.60 = (f32[768,128]{1,0:T(8,128)S(1)}, f32[512,128]{1,0:T(8,128)S(1)}) custom-call(s32[24,128]{1,0:T(8,128)S(1)} %shard_map.57.refs_0_.o, s32[24,128]{1,0:T(8,128)S(1)} %collective-permute-done.3.t, s32[24,128]{1,0:T(8,128)S(1)} %collective-permute-done.4.o2, s32[24,128]{1,0:T(8,128)S(1)} %collective-permute-done.5.t2, ...), custom_call_target="tpu_custom_call" | custom-call | flops 536870912 | tf_op jit(solution)/shard_map/pallas_call | solution.py:342
  71.2 1.0 shard_map.62
  72.2 0.8 shard_map.63
  73.4 0.8 shard_map.67
  74.8 0.7 shard_map.68
  76.0 1.8 %shard_map.59 = (f32[256,128]{1,0:T(8,128)S(1)}, f32[128,128]{1,0:T(8,128)S(1)}) custom-call(f32[128,512]{1,0:T(8,128)S(1)} %shard_map.55.refs_0_.o, f32[128,1536]{1,0:T(8,128)S(1)} %shard_map.56.refs_1_.o, f32[128,1280]{1,0:T(8,128)S(1)} %get-tuple-element.50.refs_2_.o, f32[128,512]{1,0:T(8,128)S(1)} %get-tuple-element.51.refs_3_.o, ...), custom_call_target="tpu_custom_call" | custom-call | flops 805306368 | tf_op jit(solution)/shard_map/pallas_call | solution.py:342
  78.7 0.9 collective-permute-start.26
  79.9 2.6 %collective-permute-done.26.across = f32[16,128]{1,0:T(8,128)S(1)} collective-permute-done((f32[16,128]{1,0:T(8,128)S(1)}, f32[16,128]{1,0:T(8,128)S(1)}, u32[]{:S(2)}, u32[]{:S(2)}) %collective-permute-start.26) | collective-permute-done | bytes 8224 | tf_op jit(solution)/shard_map/ppermute | solution.py:326
  82.5 3.6 %collective-permute-done.27.along = f32[16,128]{1,0:T(8,128)S(1)} collective-permute-done((f32[16,128]{1,0:T(8,128)S(1)}, f32[16,128]{1,0:T(8,128)S(1)}, u32[]{:S(2)}, u32[]{:S(2)}) %collective-permute-start.27) | collective-permute-done | bytes 8224 | tf_op jit(solution)/shard_map/ppermute | solution.py:326
  86.1 8.9 %all_to_all.5.totals = f32[32,1,128]{2,1,0:T(1,128)S(1)} all-to-all(f32[32,1,128]{2,1,0:T(1,128)S(1)} %get-tuple-element.94), channel_id=1, replica_groups=mesh['blk'=16,'grp'=2] {'blk','grp'}, dimensions={0} | all-to-all | bytes 32768 | tf_op jit(solution)/shard_map/all_to_all | solution.py:460
  (52 shorter events, 7.9 us)
Async XLA Ops:
  0.0 8.7 %copy-start.3 = (f32[128,4096]{1,0:T(8,128)S(1)}, f32[128,4096]{1,0:T(8,128)}, u32[]{:S(2)}) copy-start(f32[128,4096]{1,0:T(8,128)} %points.5) | copy-start | bytes 6291460
  0.0 9.4 %copy-start = (s32[128,16]{0,1:T(8,128)S(1)}, s32[128,16]{0,1:T(8,128)}, u32[]{:S(2)}) copy-start(s32[128,16]{0,1:T(8,128)} %param.8) | copy-start | bytes 24580
  0.0 9.4 %copy-start.1 = (s32[1,128]{1,0:T(1,128)S(1)}, s32[1,128]{1,0:T(1,128)}, u32[]{:S(2)}) copy-start(s32[1,128]{1,0:T(1,128)} %index_ref.1) | copy-start | bytes 1540
  1.1 31.3 %collective-permute-start.14 = (f32[128,512]{1,0:T(8,128)S(1)}, f32[128,512]{1,0:T(8,128)S(1)}, u32[]{:S(2)}, u32[]{:S(2)}) collective-permute-start(f32[128,512]{1,0:T(8,128)S(1)} %shard_map.55.refs_0_.o), channel_id=1, source_target_pairs={{0,1},{1,0},{2,3},{3,2},{4,5},{5,4},{6,7},{7,6},{8,9},{9,8},{10,11... | collective-permute-start | bytes 786440 | tf_op jit(solution)/shard_map/ppermute | solution.py:326
  4.2 28.7 %collective-permute-start.15 = (f32[128,512]{1,0:T(8,128)S(1)}, f32[128,512]{1,0:T(8,128)S(1)}, u32[]{:S(2)}, u32[]{:S(2)}) collective-permute-start(f32[128,512]{1,0:T(8,128)S(1)} %shard_map.55.refs_0_.o), channel_id=1, source_target_pairs={{0,28},{1,29},{2,6},{3,7},{4,0},{5,1},{6,10},{7,11},{8,4},{9,5},{1... | collective-permute-start | bytes 786440 | tf_op jit(solution)/shard_map/ppermute | solution.py:326
  8.7 67.3 %collective-permute-start = (f32[128,4096]{1,0:T(8,128)S(1)}, f32[128,4096]{1,0:T(8,128)S(1)}, u32[]{:S(2)}, u32[]{:S(2)}) collective-permute-start(f32[128,4096]{1,0:T(8,128)S(1)} %copy-done.3), channel_id=1, source_target_pairs={{0,2},{1,3},{2,0},{3,1},{4,6},{5,7},{6,4},{7,5},{8,10},{9,11},{10,... | collective-permute-start | bytes 6291464 | tf_op jit(solution)/shard_map/ppermute | solution.py:326
  9.5 3.4 %collective-permute-start.3 = (s32[24,128]{1,0:T(8,128)S(1)}, s32[24,128]{1,0:T(8,128)S(1)}, u32[]{:S(2)}, u32[]{:S(2)}) collective-permute-start(s32[24,128]{1,0:T(8,128)S(1)} %shard_map.57.refs_0_.o), channel_id=1, source_target_pairs={{0,2},{1,3},{2,0},{3,1},{4,6},{5,7},{6,4},{7,5},{8,10},{9,11},{10,... | collective-permute-start | bytes 36872 | tf_op jit(solution)/shard_map/ppermute | solution.py:326
  10.1 3.7 %collective-permute-start.4 = (s32[24,128]{1,0:T(8,128)S(1)}, s32[24,128]{1,0:T(8,128)S(1)}, u32[]{:S(2)}, u32[]{:S(2)}) collective-permute-start(s32[24,128]{1,0:T(8,128)S(1)} %shard_map.57.refs_0_.o), channel_id=1, source_target_pairs={{0,1},{1,0},{2,3},{3,2},{4,5},{5,4},{6,7},{7,6},{8,9},{9,8},{10,11... | collective-permute-start | bytes 36872 | tf_op jit(solution)/shard_map/ppermute | solution.py:326
  12.9 3.1 %collective-permute-start.5 = (s32[24,128]{1,0:T(8,128)S(1)}, s32[24,128]{1,0:T(8,128)S(1)}, u32[]{:S(2)}, u32[]{:S(2)}) collective-permute-start(s32[24,128]{1,0:T(8,128)S(1)} %shard_map.57.refs_0_.o), channel_id=1, source_target_pairs={{0,3},{1,2},{2,1},{3,0},{4,7},{5,6},{6,5},{7,4},{8,11},{9,10},{10,... | collective-permute-start | bytes 36872 | tf_op jit(solution)/shard_map/ppermute | solution.py:326
  13.8 5.0 %collective-permute-start.6 = (s32[24,128]{1,0:T(8,128)S(1)}, s32[24,128]{1,0:T(8,128)S(1)}, u32[]{:S(2)}, u32[]{:S(2)}) collective-permute-start(s32[24,128]{1,0:T(8,128)S(1)} %shard_map.57.refs_0_.o), channel_id=1, source_target_pairs={{0,28},{1,29},{2,6},{3,7},{4,0},{5,1},{6,10},{7,11},{8,4},{9,5},{1... | collective-permute-start | bytes 36872 | tf_op jit(solution)/shard_map/ppermute | solution.py:326
  16.0 5.8 %collective-permute-start.7 = (s32[24,128]{1,0:T(8,128)S(1)}, s32[24,128]{1,0:T(8,128)S(1)}, u32[]{:S(2)}, u32[]{:S(2)}) collective-permute-start(s32[24,128]{1,0:T(8,128)S(1)} %shard_map.57.refs_0_.o), channel_id=1, source_target_pairs={{0,30},{1,31},{2,4},{3,5},{4,2},{5,3},{6,8},{7,9},{8,6},{9,7},{10,... | collective-permute-start | bytes 36872 | tf_op jit(solution)/shard_map/ppermute | solution.py:326
  18.8 5.4 %collective-permute-start.1 = (f32[128,256]{1,0:T(8,128)S(1)}, f32[128,256]{1,0:T(8,128)S(1)}, u32[]{:S(2)}, u32[]{:S(2)}) collective-permute-start(f32[128,256]{1,0:T(8,128)S(1)} %get-tuple-element.52.refs_4_.o), channel_id=1, source_target_pairs={{0,1},{1,0},{2,3},{3,2},{4,5},{5,4},{6,7},{7,6},{8,9},{9,8},{10,11... | collective-permute-start | bytes 393224 | tf_op jit(solution)/shard_map/ppermute | solution.py:326
  21.8 6.3 %collective-permute-start.2 = (f32[128,256]{1,0:T(8,128)S(1)}, f32[128,256]{1,0:T(8,128)S(1)}, u32[]{:S(2)}, u32[]{:S(2)}) collective-permute-start(f32[128,256]{1,0:T(8,128)S(1)} %get-tuple-element.52.refs_4_.o), channel_id=1, source_target_pairs={{0,28},{1,29},{2,6},{3,7},{4,0},{5,1},{6,10},{7,11},{8,4},{9,5},{1... | collective-permute-start | bytes 393224 | tf_op jit(solution)/shard_map/ppermute | solution.py:326
  24.2 8.7 %collective-permute-start.8 = (f32[128,512]{1,0:T(8,128)S(1)}, f32[128,512]{1,0:T(8,128)S(1)}, u32[]{:S(2)}, u32[]{:S(2)}) collective-permute-start(f32[128,512]{1,0:T(8,128)S(1)} %get-tuple-element.51.refs_3_.o), channel_id=1, source_target_pairs={{0,1},{1,0},{2,3},{3,2},{4,5},{5,4},{6,7},{7,6},{8,9},{9,8},{10,11... | collective-permute-start | bytes 786440 | tf_op jit(solution)/shard_map/ppermute | solution.py:326
  28.1 17.6 %collective-permute-start.9 = (f32[128,512]{1,0:T(8,128)S(1)}, f32[128,512]{1,0:T(8,128)S(1)}, u32[]{:S(2)}, u32[]{:S(2)}) collective-permute-start(f32[128,512]{1,0:T(8,128)S(1)} %get-tuple-element.51.refs_3_.o), channel_id=1, source_target_pairs={{0,28},{1,29},{2,6},{3,7},{4,0},{5,1},{6,10},{7,11},{8,4},{9,5},{1... | collective-permute-start | bytes 786440 | tf_op jit(solution)/shard_map/ppermute | solution.py:326
  32.4 15.9 %collective-permute-start.12 = (f32[128,1536]{1,0:T(8,128)S(1)}, f32[128,1536]{1,0:T(8,128)S(1)}, u32[]{:S(2)}, u32[]{:S(2)}) collective-permute-start(f32[128,1536]{1,0:T(8,128)S(1)} %shard_map.56.refs_1_.o), channel_id=1, source_target_pairs={{0,1},{1,0},{2,3},{3,2},{4,5},{5,4},{6,7},{7,6},{8,9},{9,8},{10,11... | collective-permute-start | bytes 2359304 | tf_op jit(solution)/shard_map/ppermute | solution.py:326
  32.8 28.3 %collective-permute-start.13 = (f32[128,1536]{1,0:T(8,128)S(1)}, f32[128,1536]{1,0:T(8,128)S(1)}, u32[]{:S(2)}, u32[]{:S(2)}) collective-permute-start(f32[128,1536]{1,0:T(8,128)S(1)} %shard_map.56.refs_1_.o), channel_id=1, source_target_pairs={{0,28},{1,29},{2,6},{3,7},{4,0},{5,1},{6,10},{7,11},{8,4},{9,5},{1... | collective-permute-start | bytes 2359304 | tf_op jit(solution)/shard_map/ppermute | solution.py:326
  32.9 12.9 %collective-permute-start.24 = (f32[128,512]{1,0:T(8,128)S(1)}, f32[128,512]{1,0:T(8,128)S(1)}, u32[]{:S(2)}, u32[]{:S(2)}) collective-permute-start(f32[128,512]{1,0:T(8,128)S(1)} %collective-permute-done.14.o2), channel_id=1, source_target_pairs={{0,2},{1,3},{2,0},{3,1},{4,6},{5,7},{6,4},{7,5},{8,10},{9,11},{10,... | collective-permute-start | bytes 786440 | tf_op jit(solution)/shard_map/ppermute | solution.py:326
  45.7 1.5 %collective-permute-start.25 = (f32[128,512]{1,0:T(8,128)S(1)}, f32[128,512]{1,0:T(8,128)S(1)}, u32[]{:S(2)}, u32[]{:S(2)}) collective-permute-start(f32[128,512]{1,0:T(8,128)S(1)} %collective-permute-done.15.u), channel_id=1, source_target_pairs={{0,2},{1,3},{2,0},{3,1},{4,6},{5,7},{6,4},{7,5},{8,10},{9,11},{10,... | collective-permute-start | bytes 786440 | tf_op jit(solution)/shard_map/ppermute | solution.py:326
  45.7 17.1 %collective-permute-start.10 = (f32[128,1280]{1,0:T(8,128)S(1)}, f32[128,1280]{1,0:T(8,128)S(1)}, u32[]{:S(2)}, u32[]{:S(2)}) collective-permute-start(f32[128,1280]{1,0:T(8,128)S(1)} %get-tuple-element.50.refs_2_.o), channel_id=1, source_target_pairs={{0,1},{1,0},{2,3},{3,2},{4,5},{5,4},{6,7},{7,6},{8,9},{9,8},{10,11... | collective-permute-start | bytes 1966088 | tf_op jit(solution)/shard_map/ppermute | solution.py:326
  47.3 20.9 %collective-permute-start.11 = (f32[128,1280]{1,0:T(8,128)S(1)}, f32[128,1280]{1,0:T(8,128)S(1)}, u32[]{:S(2)}, u32[]{:S(2)}) collective-permute-start(f32[128,1280]{1,0:T(8,128)S(1)} %get-tuple-element.50.refs_2_.o), channel_id=1, source_target_pairs={{0,28},{1,29},{2,6},{3,7},{4,0},{5,1},{6,10},{7,11},{8,4},{9,5},{1... | collective-permute-start | bytes 1966088 | tf_op jit(solution)/shard_map/ppermute | solution.py:326
  48.3 21.4 %collective-permute-start.22 = (f32[128,1536]{1,0:T(8,128)S(1)}, f32[128,1536]{1,0:T(8,128)S(1)}, u32[]{:S(2)}, u32[]{:S(2)}) collective-permute-start(f32[128,1536]{1,0:T(8,128)S(1)} %collective-permute-done.12.o2), channel_id=1, source_target_pairs={{0,2},{1,3},{2,0},{3,1},{4,6},{5,7},{6,4},{7,5},{8,10},{9,11},{10,... | collective-permute-start | bytes 2359304 | tf_op jit(solution)/shard_map/ppermute | solution.py:326
  61.2 9.1 %collective-permute-start.23 = (f32[128,1536]{1,0:T(8,128)S(1)}, f32[128,1536]{1,0:T(8,128)S(1)}, u32[]{:S(2)}, u32[]{:S(2)}) collective-permute-start(f32[128,1536]{1,0:T(8,128)S(1)} %collective-permute-done.13.u), channel_id=1, source_target_pairs={{0,2},{1,3},{2,0},{3,1},{4,6},{5,7},{6,4},{7,5},{8,10},{9,11},{10,... | collective-permute-start | bytes 2359304 | tf_op jit(solution)/shard_map/ppermute | solution.py:326
  62.9 11.4 %collective-permute-start.20 = (f32[128,1280]{1,0:T(8,128)S(1)}, f32[128,1280]{1,0:T(8,128)S(1)}, u32[]{:S(2)}, u32[]{:S(2)}) collective-permute-start(f32[128,1280]{1,0:T(8,128)S(1)} %collective-permute-done.10.o2), channel_id=1, source_target_pairs={{0,2},{1,3},{2,0},{3,1},{4,6},{5,7},{6,4},{7,5},{8,10},{9,11},{10,... | collective-permute-start | bytes 1966088 | tf_op jit(solution)/shard_map/ppermute | solution.py:326
  68.2 6.6 %collective-permute-start.21 = (f32[128,1280]{1,0:T(8,128)S(1)}, f32[128,1280]{1,0:T(8,128)S(1)}, u32[]{:S(2)}, u32[]{:S(2)}) collective-permute-start(f32[128,1280]{1,0:T(8,128)S(1)} %collective-permute-done.11.u), channel_id=1, source_target_pairs={{0,2},{1,3},{2,0},{3,1},{4,6},{5,7},{6,4},{7,5},{8,10},{9,11},{10,... | collective-permute-start | bytes 1966088 | tf_op jit(solution)/shard_map/ppermute | solution.py:326
  69.7 5.9 %collective-permute-start.18 = (f32[128,512]{1,0:T(8,128)S(1)}, f32[128,512]{1,0:T(8,128)S(1)}, u32[]{:S(2)}, u32[]{:S(2)}) collective-permute-start(f32[128,512]{1,0:T(8,128)S(1)} %collective-permute-done.8.o2), channel_id=1, source_target_pairs={{0,2},{1,3},{2,0},{3,1},{4,6},{5,7},{6,4},{7,5},{8,10},{9,11},{10,... | collective-permute-start | bytes 786440 | tf_op jit(solution)/shard_map/ppermute | solution.py:326
  70.3 5.3 %collective-permute-start.19 = (f32[128,512]{1,0:T(8,128)S(1)}, f32[128,512]{1,0:T(8,128)S(1)}, u32[]{:S(2)}, u32[]{:S(2)}) collective-permute-start(f32[128,512]{1,0:T(8,128)S(1)} %collective-permute-done.9.u), channel_id=1, source_target_pairs={{0,2},{1,3},{2,0},{3,1},{4,6},{5,7},{6,4},{7,5},{8,10},{9,11},{10,... | collective-permute-start | bytes 786440 | tf_op jit(solution)/shard_map/ppermute | solution.py:326
  74.2 4.1 %collective-permute-start.16 = (f32[128,256]{1,0:T(8,128)S(1)}, f32[128,256]{1,0:T(8,128)S(1)}, u32[]{:S(2)}, u32[]{:S(2)}) collective-permute-start(f32[128,256]{1,0:T(8,128)S(1)} %collective-permute-done.1.o2), channel_id=1, source_target_pairs={{0,2},{1,3},{2,0},{3,1},{4,6},{5,7},{6,4},{7,5},{8,10},{9,11},{10,... | collective-permute-start | bytes 393224 | tf_op jit(solution)/shard_map/ppermute | solution.py:326
  74.7 3.6 %collective-permute-start.17 = (f32[128,256]{1,0:T(8,128)S(1)}, f32[128,256]{1,0:T(8,128)S(1)}, u32[]{:S(2)}, u32[]{:S(2)}) collective-permute-start(f32[128,256]{1,0:T(8,128)S(1)} %collective-permute-done.2.u), channel_id=1, source_target_pairs={{0,2},{1,3},{2,0},{3,1},{4,6},{5,7},{6,4},{7,5},{8,10},{9,11},{10,... | collective-permute-start | bytes 393224 | tf_op jit(solution)/shard_map/ppermute | solution.py:326
  77.8 1.8 %copy-start.2 = (f32[128,16]{0,1:T(8,128)S(1)}, f32[128,16]{0,1:T(8,128)}, u32[]{:S(2)}) copy-start(f32[128,16]{0,1:T(8,128)} %param.9) | copy-start | bytes 24580
  78.7 3.7 %collective-permute-start.26 = (f32[16,128]{1,0:T(8,128)S(1)}, f32[16,128]{1,0:T(8,128)S(1)}, u32[]{:S(2)}, u32[]{:S(2)}) collective-permute-start(f32[16,128]{1,0:T(8,128)S(1)} %get-tuple-element.91), channel_id=1, source_target_pairs={{0,1},{1,0},{2,3},{3,2},{4,5},{5,4},{6,7},{7,6},{8,9},{9,8},{10,11... | collective-permute-start | bytes 24584 | tf_op jit(solution)/shard_map/ppermute | solution.py:326
  79.7 6.3 %collective-permute-start.27 = (f32[16,128]{1,0:T(8,128)S(1)}, f32[16,128]{1,0:T(8,128)S(1)}, u32[]{:S(2)}, u32[]{:S(2)}) collective-permute-start(f32[16,128]{1,0:T(8,128)S(1)} %get-tuple-element.92), channel_id=1, source_target_pairs={{28,0},{29,1},{6,2},{7,3},{0,4},{1,5},{10,6},{11,7},{4,8},{5,9},{1... | collective-permute-start | bytes 24584 | tf_op jit(solution)/shard_map/ppermute | solution.py:326

commit v5 on v4

--- a/solution.py
+++ b/solution.py
@@ -298,7 +298,7 @@
         copy.wait()
 
 
-CUTS = (0, 2, 8, 13, 15, 16)
+CUTS = (0, 4, 8, 13, 16)
 
 
 def body(points, cand_index, cand_count, neighbor_ids, old_dist):
@@ -372,8 +372,7 @@
     cuts = [width * c // CUTS[-1] for c in CUTS]
     spans = [(a, b - a) for a, b in zip(cuts, cuts[1:])]
     o = cut(spans[:1])
-    o += cut(spans[1:2])
-    o += cut(spans[2:], (meta,))
+    o += cut(spans[1:], (meta,))
     metas = (
         meta,
         labelled(meta, sibling),

time: 95.9 us -> 93.6 us (0.976)
  starting transfers between devices: 23.7 us -> 21.5 us
  local copies, waits for them, and re-layouts: 0.02 us -> 1.35 us
  Pallas kernels: 13.7 us -> 12.4 us
    ppermute x28 -> x24, starting transfers between devices: 23.7 us -> 21.5 us  [labelled(): return lax.ppermute(value, AXES, pairs)]
    unnamed x8, local copies, waits for them, and re-layouts: 0.02 us -> 1.35 us
    pallas_call x19 -> x16, Pallas kernels: 13.7 us -> 12.4 us  [call(): pl.pallas_call(kernel, out_shape=out_shape, in_specs=specs[:len(args)], s...]
    ppermute x28 -> x24, waiting for transfers between devices: 48.4 us -> 48.3 us  [labelled(): return lax.ppermute(value, AXES, pairs)]
  transfers between devices with their start and end apart: 28 -> 24, of which waited for: 14 -> 13; matrix products, arithmetic and copies ran while one was open for 0% -> 0% of each run, Pallas kernels for 12% -> 10%
where the time goes in v5:
time: 93.6 us; the launch traced here: 93.4 us
  waiting for transfers between devices  48.3 us (52%)
  starting transfers between devices  21.5 us (23%)
  Pallas kernels  12.4 us (13%)
  blocking collectives  8.9 us (10%)
  local copies, waits for them, and re-layouts  1.35 us (1%)
    ppermute x24, waiting for transfers between devices, labelled(): return lax.ppermute(value, AXES, pairs)  48.3 us
    ppermute x24, starting transfers between devices, labelled(): return lax.ppermute(value, AXES, pairs)  21.5 us
    pallas_call x16, Pallas kernels, call(): pl.pallas_call(kernel, out_shape=out_shape, in_specs=specs[:len(args)], s...  12.4 us
    all_to_all x1, blocking collectives, body(): totals = lax.all_to_all(total, AXES, 0, 0)  8.9 us
  transfers between devices with their start and end apart: 24, of which 13 were waited for; matrix products, arithmetic and copies ran while one was open for 0% of the time, Pallas kernels for 10%

profile of v5, /device:TPU:0, one launch (start us, length us, event | category | flops | bytes accessed | tf_op | source)
XLA Modules:
  0.0 93.4 jit_solution(13583711015583720887)
XLA Ops:
  0.7 0.7 copy-done
  1.4 0.7 copy-done.1
  2.1 1.5 %shard_map.57 = (f32[128,1024]{1,0:T(8,128)S(1)}, f32[128,1280]{1,0:T(8,128)S(1)}, f32[128,768]{1,0:T(8,128)S(1)}) custom-call(f32[128,4096]{1,0:T(8,128)} %points.3, s32[24,128]{1,0:T(8,128)S(1)} %shard_map.56.refs_0_.o), custom_call_target="tpu_custom_call" | custom-call | tf_op jit(solution)/shard_map/pallas_call | solution.py:342
  3.6 3.0 %collective-permute-start.1 = (f32[128,768]{1,0:T(8,128)S(1)}, f32[128,768]{1,0:T(8,128)S(1)}, u32[]{:S(2)}, u32[]{:S(2)}) collective-permute-start(f32[128,768]{1,0:T(8,128)S(1)} %get-tuple-element.46.refs_3_.o), channel_id=1, source_target_pairs={{0,1},{1,0},{2,3},{3,2},{4,5},{5,4},{6,7},{7,6},{8,9},{9,8},{10,11... | collective-permute-start | bytes 1179656 | tf_op jit(solution)/shard_map/ppermute | solution.py:326
  6.7 4.6 %collective-permute-start.2 = (f32[128,768]{1,0:T(8,128)S(1)}, f32[128,768]{1,0:T(8,128)S(1)}, u32[]{:S(2)}, u32[]{:S(2)}) collective-permute-start(f32[128,768]{1,0:T(8,128)S(1)} %get-tuple-element.46.refs_3_.o), channel_id=1, source_target_pairs={{0,28},{1,29},{2,6},{3,7},{4,0},{5,1},{6,10},{7,11},{8,4},{9,5},{1... | collective-permute-start | bytes 1179656 | tf_op jit(solution)/shard_map/ppermute | solution.py:326
  12.3 3.1 %collective-permute-done.3.t = s32[24,128]{1,0:T(8,128)S(1)} collective-permute-done((s32[24,128]{1,0:T(8,128)S(1)}, s32[24,128]{1,0:T(8,128)S(1)}, u32[]{:S(2)}, u32[]{:S(2)}) %collective-permute-start.3) | collective-permute-done | bytes 12320 | tf_op jit(solution)/shard_map/ppermute | solution.py:326
  16.0 4.9 %collective-permute-start.6 = (s32[24,128]{1,0:T(8,128)S(1)}, s32[24,128]{1,0:T(8,128)S(1)}, u32[]{:S(2)}, u32[]{:S(2)}) collective-permute-start(s32[24,128]{1,0:T(8,128)S(1)} %shard_map.56.refs_0_.o), channel_id=1, source_target_pairs={{0,28},{1,29},{2,6},{3,7},{4,0},{5,1},{6,10},{7,11},{8,4},{9,5},{1... | collective-permute-start | bytes 36872 | tf_op jit(solution)/shard_map/ppermute | solution.py:326
  21.0 1.1 %shard_map.55.refs_0_.o = f32[128,1024]{1,0:T(8,128)S(1)} custom-call(f32[128,4096]{1,0:T(8,128)} %points.3), custom_call_target="tpu_custom_call" | custom-call | tf_op jit(solution)/shard_map/pallas_call | solution.py:342
  22.4 1.5 %collective-permute-start.12 = (f32[128,1024]{1,0:T(8,128)S(1)}, f32[128,1024]{1,0:T(8,128)S(1)}, u32[]{:S(2)}, u32[]{:S(2)}) collective-permute-start(f32[128,1024]{1,0:T(8,128)S(1)} %shard_map.55.refs_0_.o), channel_id=1, source_target_pairs={{0,1},{1,0},{2,3},{3,2},{4,5},{5,4},{6,7},{7,6},{8,9},{9,8},{10,11... | collective-permute-start | bytes 1572872 | tf_op jit(solution)/shard_map/ppermute | solution.py:326
  23.9 2.9 %collective-permute-done.7.v = s32[24,128]{1,0:T(8,128)S(1)} collective-permute-done((s32[24,128]{1,0:T(8,128)S(1)}, s32[24,128]{1,0:T(8,128)S(1)}, u32[]{:S(2)}, u32[]{:S(2)}) %collective-permute-start.7) | collective-permute-done | bytes 12320 | tf_op jit(solution)/shard_map/ppermute | solution.py:326
  26.8 2.1 %collective-permute-start.13 = (f32[128,1024]{1,0:T(8,128)S(1)}, f32[128,1024]{1,0:T(8,128)S(1)}, u32[]{:S(2)}, u32[]{:S(2)}) collective-permute-start(f32[128,1024]{1,0:T(8,128)S(1)} %shard_map.55.refs_0_.o), channel_id=1, source_target_pairs={{0,28},{1,29},{2,6},{3,7},{4,0},{5,1},{6,10},{7,11},{8,4},{9,5},{1... | collective-permute-start | bytes 1572872 | tf_op jit(solution)/shard_map/ppermute | solution.py:326
  29.5 7.7 %collective-permute-done.12.o2 = f32[128,1024]{1,0:T(8,128)S(1)} collective-permute-done((f32[128,1024]{1,0:T(8,128)S(1)}, f32[128,1024]{1,0:T(8,128)S(1)}, u32[]{:S(2)}, u32[]{:S(2)}) %collective-permute-start.12) | collective-permute-done | bytes 524320 | tf_op jit(solution)/shard_map/ppermute | solution.py:326
  37.2 1.5 %collective-permute-start.8 = (f32[128,1280]{1,0:T(8,128)S(1)}, f32[128,1280]{1,0:T(8,128)S(1)}, u32[]{:S(2)}, u32[]{:S(2)}) collective-permute-start(f32[128,1280]{1,0:T(8,128)S(1)} %get-tuple-element.45.refs_2_.o), channel_id=1, source_target_pairs={{0,1},{1,0},{2,3},{3,2},{4,5},{5,4},{6,7},{7,6},{8,9},{9,8},{10,11... | collective-permute-start | bytes 1966088 | tf_op jit(solution)/shard_map/ppermute | solution.py:326
  38.7 7.2 %collective-permute-done.13.u = f32[128,1024]{1,0:T(8,128)S(1)} collective-permute-done((f32[128,1024]{1,0:T(8,128)S(1)}, f32[128,1024]{1,0:T(8,128)S(1)}, u32[]{:S(2)}, u32[]{:S(2)}) %collective-permute-start.13) | collective-permute-done | bytes 524320 | tf_op jit(solution)/shard_map/ppermute | solution.py:326
  45.9 2.5 %collective-permute-done.10.o2 = f32[128,1024]{1,0:T(8,128)S(1)} collective-permute-done((f32[128,1024]{1,0:T(8,128)S(1)}, f32[128,1024]{1,0:T(8,128)S(1)}, u32[]{:S(2)}, u32[]{:S(2)}) %collective-permute-start.10) | collective-permute-done | bytes 524320 | tf_op jit(solution)/shard_map/ppermute | solution.py:326
  48.4 10.1 %collective-permute-done.11.u = f32[128,1024]{1,0:T(8,128)S(1)} collective-permute-done((f32[128,1024]{1,0:T(8,128)S(1)}, f32[128,1024]{1,0:T(8,128)S(1)}, u32[]{:S(2)}, u32[]{:S(2)}) %collective-permute-start.11) | collective-permute-done | bytes 524320 | tf_op jit(solution)/shard_map/ppermute | solution.py:326
  58.5 1.9 %collective-permute-done.8.o2 = f32[128,1280]{1,0:T(8,128)S(1)} collective-permute-done((f32[128,1280]{1,0:T(8,128)S(1)}, f32[128,1280]{1,0:T(8,128)S(1)}, u32[]{:S(2)}, u32[]{:S(2)}) %collective-permute-start.8) | collective-permute-done | bytes 655392 | tf_op jit(solution)/shard_map/ppermute | solution.py:326
  60.4 5.1 %collective-permute-done.9.u = f32[128,1280]{1,0:T(8,128)S(1)} collective-permute-done((f32[128,1280]{1,0:T(8,128)S(1)}, f32[128,1280]{1,0:T(8,128)S(1)}, u32[]{:S(2)}, u32[]{:S(2)}) %collective-permute-start.9) | collective-permute-done | bytes 655392 | tf_op jit(solution)/shard_map/ppermute | solution.py:326
  66.6 0.9 collective-permute-done.19.v
  67.6 1.5 %shard_map.59 = (f32[768,128]{1,0:T(8,128)S(1)}, f32[512,128]{1,0:T(8,128)S(1)}) custom-call(s32[24,128]{1,0:T(8,128)S(1)} %shard_map.56.refs_0_.o, s32[24,128]{1,0:T(8,128)S(1)} %collective-permute-done.3.t, s32[24,128]{1,0:T(8,128)S(1)} %collective-permute-done.4.o2, s32[24,128]{1,0:T(8,128)S(1)} %collective-permute-done.5.t2, ...), custom_call_target="tpu_custom_call" | custom-call | flops 536870912 | tf_op jit(solution)/shard_map/pallas_call | solution.py:342
  69.1 0.7 shard_map.60
  69.8 0.7 shard_map.61
  70.5 0.8 shard_map.62
  71.9 0.6 shard_map.65
  72.6 0.7 shard_map.66
  73.3 1.9 %shard_map.58 = (f32[256,128]{1,0:T(8,128)S(1)}, f32[128,128]{1,0:T(8,128)S(1)}) custom-call(f32[128,1024]{1,0:T(8,128)S(1)} %shard_map.55.refs_0_.o, f32[128,1024]{1,0:T(8,128)S(1)} %get-tuple-element.44.refs_1_.o, f32[128,1280]{1,0:T(8,128)S(1)} %get-tuple-element.45.refs_2_.o, f32[128,768]{1,0:T(8,128)S(1)} %get-tuple-element.46.refs_3_.o, ...), custom_call_target="tpu_custom_call" | custom-call | flops 805306368 | tf_op jit(solution)/shard_map/pallas_call | solution.py:342
  75.2 0.7 shard_map.63
  76.5 0.9 collective-permute-start.22
  77.6 2.6 %collective-permute-done.22.across = f32[16,128]{1,0:T(8,128)S(1)} collective-permute-done((f32[16,128]{1,0:T(8,128)S(1)}, f32[16,128]{1,0:T(8,128)S(1)}, u32[]{:S(2)}, u32[]{:S(2)}) %collective-permute-start.22) | collective-permute-done | bytes 8224 | tf_op jit(solution)/shard_map/ppermute | solution.py:326
  80.2 3.5 %collective-permute-done.23.along = f32[16,128]{1,0:T(8,128)S(1)} collective-permute-done((f32[16,128]{1,0:T(8,128)S(1)}, f32[16,128]{1,0:T(8,128)S(1)}, u32[]{:S(2)}, u32[]{:S(2)}) %collective-permute-start.23) | collective-permute-done | bytes 8224 | tf_op jit(solution)/shard_map/ppermute | solution.py:326
  83.9 8.9 %all_to_all.5.totals = f32[32,1,128]{2,1,0:T(1,128)S(1)} all-to-all(f32[32,1,128]{2,1,0:T(1,128)S(1)} %get-tuple-element.82), channel_id=1, replica_groups=mesh['blk'=16,'grp'=2] {'blk','grp'}, dimensions={0} | all-to-all | bytes 32768 | tf_op jit(solution)/shard_map/all_to_all | solution.py:459
  92.8 0.6 shard_map.70
  (41 shorter events, 5.5 us)
Async XLA Ops:
  0.7 0.7 copy-start
  1.4 0.7 copy-start.1
  2.0 9.2 %copy-start.3 = (f32[128,4096]{1,0:T(8,128)S(1)}, f32[128,4096]{1,0:T(8,128)}, u32[]{:S(2)}) copy-start(f32[128,4096]{1,0:T(8,128)} %points.3) | copy-start | bytes 6291460
  3.6 25.2 %collective-permute-start.1 = (f32[128,768]{1,0:T(8,128)S(1)}, f32[128,768]{1,0:T(8,128)S(1)}, u32[]{:S(2)}, u32[]{:S(2)}) collective-permute-start(f32[128,768]{1,0:T(8,128)S(1)} %get-tuple-element.46.refs_3_.o), channel_id=1, source_target_pairs={{0,1},{1,0},{2,3},{3,2},{4,5},{5,4},{6,7},{7,6},{8,9},{9,8},{10,11... | collective-permute-start | bytes 1179656 | tf_op jit(solution)/shard_map/ppermute | solution.py:326
  6.7 22.7 %collective-permute-start.2 = (f32[128,768]{1,0:T(8,128)S(1)}, f32[128,768]{1,0:T(8,128)S(1)}, u32[]{:S(2)}, u32[]{:S(2)}) collective-permute-start(f32[128,768]{1,0:T(8,128)S(1)} %get-tuple-element.46.refs_3_.o), channel_id=1, source_target_pairs={{0,28},{1,29},{2,6},{3,7},{4,0},{5,1},{6,10},{7,11},{8,4},{9,5},{1... | collective-permute-start | bytes 1179656 | tf_op jit(solution)/shard_map/ppermute | solution.py:326
  11.2 62.1 %collective-permute-start = (f32[128,4096]{1,0:T(8,128)S(1)}, f32[128,4096]{1,0:T(8,128)S(1)}, u32[]{:S(2)}, u32[]{:S(2)}) collective-permute-start(f32[128,4096]{1,0:T(8,128)S(1)} %copy-done.3), channel_id=1, source_target_pairs={{0,2},{1,3},{2,0},{3,1},{4,6},{5,7},{6,4},{7,5},{8,10},{9,11},{10,... | collective-permute-start | bytes 6291464 | tf_op jit(solution)/shard_map/ppermute | solution.py:326
  11.2 4.2 %collective-permute-start.3 = (s32[24,128]{1,0:T(8,128)S(1)}, s32[24,128]{1,0:T(8,128)S(1)}, u32[]{:S(2)}, u32[]{:S(2)}) collective-permute-start(s32[24,128]{1,0:T(8,128)S(1)} %shard_map.56.refs_0_.o), channel_id=1, source_target_pairs={{0,2},{1,3},{2,0},{3,1},{4,6},{5,7},{6,4},{7,5},{8,10},{9,11},{10,... | collective-permute-start | bytes 36872 | tf_op jit(solution)/shard_map/ppermute | solution.py:326
  11.7 4.3 %collective-permute-start.4 = (s32[24,128]{1,0:T(8,128)S(1)}, s32[24,128]{1,0:T(8,128)S(1)}, u32[]{:S(2)}, u32[]{:S(2)}) collective-permute-start(s32[24,128]{1,0:T(8,128)S(1)} %shard_map.56.refs_0_.o), channel_id=1, source_target_pairs={{0,1},{1,0},{2,3},{3,2},{4,5},{5,4},{6,7},{7,6},{8,9},{9,8},{10,11... | collective-permute-start | bytes 36872 | tf_op jit(solution)/shard_map/ppermute | solution.py:326
  15.4 5.6 %collective-permute-start.5 = (s32[24,128]{1,0:T(8,128)S(1)}, s32[24,128]{1,0:T(8,128)S(1)}, u32[]{:S(2)}, u32[]{:S(2)}) collective-permute-start(s32[24,128]{1,0:T(8,128)S(1)} %shard_map.56.refs_0_.o), channel_id=1, source_target_pairs={{0,3},{1,2},{2,1},{3,0},{4,7},{5,6},{6,5},{7,4},{8,11},{9,10},{10,... | collective-permute-start | bytes 36872 | tf_op jit(solution)/shard_map/ppermute | solution.py:326
  16.0 6.3 %collective-permute-start.6 = (s32[24,128]{1,0:T(8,128)S(1)}, s32[24,128]{1,0:T(8,128)S(1)}, u32[]{:S(2)}, u32[]{:S(2)}) collective-permute-start(s32[24,128]{1,0:T(8,128)S(1)} %shard_map.56.refs_0_.o), channel_id=1, source_target_pairs={{0,28},{1,29},{2,6},{3,7},{4,0},{5,1},{6,10},{7,11},{8,4},{9,5},{1... | collective-permute-start | bytes 36872 | tf_op jit(solution)/shard_map/ppermute | solution.py:326
  21.0 5.8 %collective-permute-start.7 = (s32[24,128]{1,0:T(8,128)S(1)}, s32[24,128]{1,0:T(8,128)S(1)}, u32[]{:S(2)}, u32[]{:S(2)}) collective-permute-start(s32[24,128]{1,0:T(8,128)S(1)} %shard_map.56.refs_0_.o), channel_id=1, source_target_pairs={{0,30},{1,31},{2,4},{3,5},{4,2},{5,3},{6,8},{7,9},{8,6},{9,7},{10,... | collective-permute-start | bytes 36872 | tf_op jit(solution)/shard_map/ppermute | solution.py:326
  22.4 14.8 %collective-permute-start.12 = (f32[128,1024]{1,0:T(8,128)S(1)}, f32[128,1024]{1,0:T(8,128)S(1)}, u32[]{:S(2)}, u32[]{:S(2)}) collective-permute-start(f32[128,1024]{1,0:T(8,128)S(1)} %shard_map.55.refs_0_.o), channel_id=1, source_target_pairs={{0,1},{1,0},{2,3},{3,2},{4,5},{5,4},{6,7},{7,6},{8,9},{9,8},{10,11... | collective-permute-start | bytes 1572872 | tf_op jit(solution)/shard_map/ppermute | solution.py:326
  26.8 19.1 %collective-permute-start.13 = (f32[128,1024]{1,0:T(8,128)S(1)}, f32[128,1024]{1,0:T(8,128)S(1)}, u32[]{:S(2)}, u32[]{:S(2)}) collective-permute-start(f32[128,1024]{1,0:T(8,128)S(1)} %shard_map.55.refs_0_.o), channel_id=1, source_target_pairs={{0,28},{1,29},{2,6},{3,7},{4,0},{5,1},{6,10},{7,11},{8,4},{9,5},{1... | collective-permute-start | bytes 1572872 | tf_op jit(solution)/shard_map/ppermute | solution.py:326
  28.9 19.5 %collective-permute-start.10 = (f32[128,1024]{1,0:T(8,128)S(1)}, f32[128,1024]{1,0:T(8,128)S(1)}, u32[]{:S(2)}, u32[]{:S(2)}) collective-permute-start(f32[128,1024]{1,0:T(8,128)S(1)} %get-tuple-element.44.refs_1_.o), channel_id=1, source_target_pairs={{0,1},{1,0},{2,3},{3,2},{4,5},{5,4},{6,7},{7,6},{8,9},{9,8},{10,11... | collective-permute-start | bytes 1572872 | tf_op jit(solution)/shard_map/ppermute | solution.py:326
  29.4 29.1 %collective-permute-start.11 = (f32[128,1024]{1,0:T(8,128)S(1)}, f32[128,1024]{1,0:T(8,128)S(1)}, u32[]{:S(2)}, u32[]{:S(2)}) collective-permute-start(f32[128,1024]{1,0:T(8,128)S(1)} %get-tuple-element.44.refs_1_.o), channel_id=1, source_target_pairs={{0,28},{1,29},{2,6},{3,7},{4,0},{5,1},{6,10},{7,11},{8,4},{9,5},{1... | collective-permute-start | bytes 1572872 | tf_op jit(solution)/shard_map/ppermute | solution.py:326
  37.2 23.2 %collective-permute-start.8 = (f32[128,1280]{1,0:T(8,128)S(1)}, f32[128,1280]{1,0:T(8,128)S(1)}, u32[]{:S(2)}, u32[]{:S(2)}) collective-permute-start(f32[128,1280]{1,0:T(8,128)S(1)} %get-tuple-element.45.refs_2_.o), channel_id=1, source_target_pairs={{0,1},{1,0},{2,3},{3,2},{4,5},{5,4},{6,7},{7,6},{8,9},{9,8},{10,11... | collective-permute-start | bytes 1966088 | tf_op jit(solution)/shard_map/ppermute | solution.py:326
  45.9 19.7 %collective-permute-start.9 = (f32[128,1280]{1,0:T(8,128)S(1)}, f32[128,1280]{1,0:T(8,128)S(1)}, u32[]{:S(2)}, u32[]{:S(2)}) collective-permute-start(f32[128,1280]{1,0:T(8,128)S(1)} %get-tuple-element.45.refs_2_.o), channel_id=1, source_target_pairs={{0,28},{1,29},{2,6},{3,7},{4,0},{5,1},{6,10},{7,11},{8,4},{9,5},{1... | collective-permute-start | bytes 1966088 | tf_op jit(solution)/shard_map/ppermute | solution.py:326
  48.4 17.1 %collective-permute-start.20 = (f32[128,1024]{1,0:T(8,128)S(1)}, f32[128,1024]{1,0:T(8,128)S(1)}, u32[]{:S(2)}, u32[]{:S(2)}) collective-permute-start(f32[128,1024]{1,0:T(8,128)S(1)} %collective-permute-done.12.o2), channel_id=1, source_target_pairs={{0,2},{1,3},{2,0},{3,1},{4,6},{5,7},{6,4},{7,5},{8,10},{9,11},{10,... | collective-permute-start | bytes 1572872 | tf_op jit(solution)/shard_map/ppermute | solution.py:326
  58.5 7.5 %collective-permute-start.21 = (f32[128,1024]{1,0:T(8,128)S(1)}, f32[128,1024]{1,0:T(8,128)S(1)}, u32[]{:S(2)}, u32[]{:S(2)}) collective-permute-start(f32[128,1024]{1,0:T(8,128)S(1)} %collective-permute-done.13.u), channel_id=1, source_target_pairs={{0,2},{1,3},{2,0},{3,1},{4,6},{5,7},{6,4},{7,5},{8,10},{9,11},{10,... | collective-permute-start | bytes 1572872 | tf_op jit(solution)/shard_map/ppermute | solution.py:326
  60.4 5.7 %collective-permute-start.18 = (f32[128,1024]{1,0:T(8,128)S(1)}, f32[128,1024]{1,0:T(8,128)S(1)}, u32[]{:S(2)}, u32[]{:S(2)}) collective-permute-start(f32[128,1024]{1,0:T(8,128)S(1)} %collective-permute-done.10.o2), channel_id=1, source_target_pairs={{0,2},{1,3},{2,0},{3,1},{4,6},{5,7},{6,4},{7,5},{8,10},{9,11},{10,... | collective-permute-start | bytes 1572872 | tf_op jit(solution)/shard_map/ppermute | solution.py:326
  65.5 1.9 %collective-permute-start.19 = (f32[128,1024]{1,0:T(8,128)S(1)}, f32[128,1024]{1,0:T(8,128)S(1)}, u32[]{:S(2)}, u32[]{:S(2)}) collective-permute-start(f32[128,1024]{1,0:T(8,128)S(1)} %collective-permute-done.11.u), channel_id=1, source_target_pairs={{0,2},{1,3},{2,0},{3,1},{4,6},{5,7},{6,4},{7,5},{8,10},{9,11},{10,... | collective-permute-start | bytes 1572872 | tf_op jit(solution)/shard_map/ppermute | solution.py:326
  65.6 7.0 %collective-permute-start.16 = (f32[128,1280]{1,0:T(8,128)S(1)}, f32[128,1280]{1,0:T(8,128)S(1)}, u32[]{:S(2)}, u32[]{:S(2)}) collective-permute-start(f32[128,1280]{1,0:T(8,128)S(1)} %collective-permute-done.8.o2), channel_id=1, source_target_pairs={{0,2},{1,3},{2,0},{3,1},{4,6},{5,7},{6,4},{7,5},{8,10},{9,11},{10,... | collective-permute-start | bytes 1966088 | tf_op jit(solution)/shard_map/ppermute | solution.py:326
  66.1 6.5 %collective-permute-start.17 = (f32[128,1280]{1,0:T(8,128)S(1)}, f32[128,1280]{1,0:T(8,128)S(1)}, u32[]{:S(2)}, u32[]{:S(2)}) collective-permute-start(f32[128,1280]{1,0:T(8,128)S(1)} %collective-permute-done.9.u), channel_id=1, source_target_pairs={{0,2},{1,3},{2,0},{3,1},{4,6},{5,7},{6,4},{7,5},{8,10},{9,11},{10,... | collective-permute-start | bytes 1966088 | tf_op jit(solution)/shard_map/ppermute | solution.py:326
  66.1 9.8 %collective-permute-start.14 = (f32[128,768]{1,0:T(8,128)S(1)}, f32[128,768]{1,0:T(8,128)S(1)}, u32[]{:S(2)}, u32[]{:S(2)}) collective-permute-start(f32[128,768]{1,0:T(8,128)S(1)} %collective-permute-done.1.o2), channel_id=1, source_target_pairs={{0,2},{1,3},{2,0},{3,1},{4,6},{5,7},{6,4},{7,5},{8,10},{9,11},{10,... | collective-permute-start | bytes 1179656 | tf_op jit(solution)/shard_map/ppermute | solution.py:326
  67.5 8.4 %collective-permute-start.15 = (f32[128,768]{1,0:T(8,128)S(1)}, f32[128,768]{1,0:T(8,128)S(1)}, u32[]{:S(2)}, u32[]{:S(2)}) collective-permute-start(f32[128,768]{1,0:T(8,128)S(1)} %collective-permute-done.2.u), channel_id=1, source_target_pairs={{0,2},{1,3},{2,0},{3,1},{4,6},{5,7},{6,4},{7,5},{8,10},{9,11},{10,... | collective-permute-start | bytes 1179656 | tf_op jit(solution)/shard_map/ppermute | solution.py:326
  75.2 2.2 %copy-start.2 = (f32[128,16]{0,1:T(8,128)S(1)}, f32[128,16]{0,1:T(8,128)}, u32[]{:S(2)}) copy-start(f32[128,16]{0,1:T(8,128)} %param.9) | copy-start | bytes 24580
  76.5 3.7 %collective-permute-start.22 = (f32[16,128]{1,0:T(8,128)S(1)}, f32[16,128]{1,0:T(8,128)S(1)}, u32[]{:S(2)}, u32[]{:S(2)}) collective-permute-start(f32[16,128]{1,0:T(8,128)S(1)} %get-tuple-element.79), channel_id=1, source_target_pairs={{0,1},{1,0},{2,3},{3,2},{4,5},{5,4},{6,7},{7,6},{8,9},{9,8},{10,11... | collective-permute-start | bytes 24584 | tf_op jit(solution)/shard_map/ppermute | solution.py:326
  77.4 6.3 %collective-permute-start.23 = (f32[16,128]{1,0:T(8,128)S(1)}, f32[16,128]{1,0:T(8,128)S(1)}, u32[]{:S(2)}, u32[]{:S(2)}) collective-permute-start(f32[16,128]{1,0:T(8,128)S(1)} %get-tuple-element.80), channel_id=1, source_target_pairs={{28,0},{29,1},{6,2},{7,3},{0,4},{1,5},{10,6},{11,7},{4,8},{5,9},{1... | collective-permute-start | bytes 24584 | tf_op jit(solution)/shard_map/ppermute | solution.py:326
